TPU v7x, 32 devices: a whole 2x2x4 slice. The times are simulated.
32 devices in a mesh: comp: 2 (over core), lat: 4 (over z), lon: 4 (over y, x).
Axes of the slice: x: 2, y: 2, z: 4, core: 2. Of those that a mesh axis runs over, the one named last changes fastest.
Arguments:
- fields: float32 [2, 7, 2048, 256], P('comp', None, ('lat', 'lon')), may hold values from -4 to 4, as said below
- block_owner: int32 [2048], P(('lat', 'lon')), may hold values from 0 to 2047, as said below
- ice_covered: int32 [2048], P(('lat', 'lon')), may hold values 0 or 1
- land_mask: int32 [2048, 256], P(('lat', 'lon')), may hold values 0 or 1
Outputs:
- coupled_out: float32 [2, 2, 2048, 256], P('comp', None, ('lat', 'lon'))
Inputs may be any that keep to these rules, and one draw needn't show every extreme that they name: `block_owner`: every block id appears once. Slot d of lat+lon index o holds a block of the ice tile of index d, that is an id from d * 128 to d * 128 + 127. `fields`: ocean channels: winds within 4, currents within 1.5, tilts within 1, air density 0.9 to 1.3; ice channels: velocities within 1.5, mass 0.5 to 4, concentration 0.05 to 1, stresses within 1.5.
All inputs are finite; a program needn't handle non-finite values.
Results may differ from a plain program's by a relative error of at most 0.00002.
Values sent between devices are 32-bit elements.
No kernel may reach another device: no remote copies, remote signals or barrier semaphores. Data moves between devices by JAX's collectives and lax.ppermute only.
A program may use at most 64 MiB of HBM per device.

v0:
```python
import jax
import jax.numpy as jnp
from jax import lax
from jax.sharding import PartitionSpec as P

GX = 1
BY = 2
BX = 128
NSUB = 4


CD_ICE = 0.1
CW = 1.5
CSTAR = 2.0
ECC2 = 4.0
DMIN2 = 0.25
RELAX = 0.5
DTE = 0.5
CORIO = 0.3
MASS_FLOOR = 0.5
DRAG_FLOOR = 0.1


def from_behind(x, axis, by):
    size = lax.axis_size(axis)
    pairs = [(i, i + by) for i in range(size) if 0 <= i + by < size]
    return lax.ppermute(x, axis, pairs)


def with_halo(x, sides, width, wrap):
    for axis, dim in sides:
        size, length = (lax.axis_size(axis), x.shape[dim])
        up = [(i, (i + 1) % size) for i in range(size if wrap else size - 1)]
        down = [(j, i) for i, j in up]
        last = lax.slice_in_dim(x, length - width, length, axis=dim)
        first = lax.slice_in_dim(x, 0, width, axis=dim)
        before = lax.ppermute(last, axis, up)
        after = lax.ppermute(first, axis, down)
        x = jnp.concatenate([before, x, after], axis=dim)
    return x


def air_stress(ocean):
    wind_x, wind_y, current_x, current_y, tilt_x, tilt_y, density = ocean
    speed_ice = jnp.sqrt(wind_x * wind_x + wind_y * wind_y + 1.0)
    scale_ice = density * CD_ICE * speed_ice
    rel_x = wind_x - current_x
    rel_y = wind_y - current_y
    speed_open = jnp.sqrt(rel_x * rel_x + rel_y * rel_y + 1.0)
    scale_open = density * (0.1 + 0.05 * speed_open) * speed_open
    outbound = jnp.stack(
        [scale_ice * wind_x, scale_ice * wind_y, current_x, current_y, tilt_x, tilt_y]
    )
    open_stress = jnp.stack([scale_open * rel_x, scale_open * rel_y])
    return (outbound, open_stress)


def prepare(ice_tile, forcing, active):
    ice_mass = ice_tile[2]
    concentration = ice_tile[3]
    strength = ice_mass * jnp.exp(CSTAR * (concentration - 1.0)) * active
    drag_base = CW * concentration * active
    push_x = active * (concentration * forcing[0] - ice_mass * forcing[4])
    push_y = active * (concentration * forcing[1] - ice_mass * forcing[5])
    return jnp.stack(
        [strength, ice_mass, drag_base, push_x, push_y, forcing[2], forcing[3], active]
    )


def subcycle(ice_state, statics):
    east_vel, north_vel, stress_one, stress_two, stress_three = ice_state
    strength = statics[0]
    east_base = east_vel[:-1, :-1]
    north_base = north_vel[:-1, :-1]
    strain_xx = east_vel[:-1, 1:] - east_base
    strain_yy = north_vel[1:, :-1] - north_base
    shear = east_vel[1:, :-1] - east_base + (north_vel[:-1, 1:] - north_base)
    divergence = strain_xx + strain_yy
    tension = strain_xx - strain_yy
    delta_norm = jnp.sqrt(
        divergence * divergence + (tension * tension + shear * shear) / ECC2 + DMIN2
    )
    viscosity = strength[:-1, :-1] / delta_norm
    stress_sum = (stress_one[:-1, :-1] + RELAX * viscosity * (divergence - delta_norm)) / (
        1.0 + RELAX
    )
    stress_diff = (stress_two[:-1, :-1] + RELAX * viscosity * tension / ECC2) / (1.0 + RELAX)
    stress_shear = (stress_three[:-1, :-1] + RELAX * viscosity * shear / (2.0 * ECC2)) / (
        1.0 + RELAX
    )
    stress_xx = 0.5 * (stress_sum + stress_diff)
    stress_yy = 0.5 * (stress_sum - stress_diff)
    force_x = (
        stress_xx[1:, 1:] - stress_xx[1:, :-1] + (stress_shear[1:, 1:] - stress_shear[:-1, 1:])
    )
    force_y = (
        stress_shear[1:, 1:] - stress_shear[1:, :-1] + (stress_yy[1:, 1:] - stress_yy[:-1, 1:])
    )
    trimmed = statics[:, 1:-1, 1:-1]
    strength, ice_mass, drag_base, push_x, push_y, current_x, current_y, active = trimmed
    east_old = east_vel[1:-1, 1:-1]
    north_old = north_vel[1:-1, 1:-1]
    diff_x = current_x - east_old
    diff_y = current_y - north_old
    drag_coef = drag_base * jnp.sqrt(diff_x * diff_x + diff_y * diff_y + DRAG_FLOOR)
    denominator = jnp.maximum(ice_mass, MASS_FLOOR) / DTE + drag_coef
    east_new = (
        active
        * (
            ice_mass / DTE * east_old
            + force_x
            + push_x
            + drag_coef * current_x
            + CORIO * ice_mass * north_old
        )
        / denominator
    )
    north_new = (
        active
        * (
            ice_mass / DTE * north_old
            + force_y
            + push_y
            + drag_coef * current_y
            - CORIO * ice_mass * east_old
        )
        / denominator
    )
    new_state = jnp.stack(
        [east_new, north_new, stress_sum[1:, 1:], stress_diff[1:, 1:], stress_shear[1:, 1:]]
    )
    return (new_state, trimmed)


def give_back(ice_state, statics):
    east_vel = ice_state[0]
    north_vel = ice_state[1]
    drag_base = statics[2]
    current_x = statics[5]
    current_y = statics[6]
    diff_x = east_vel - current_x
    diff_y = north_vel - current_y
    factor = drag_base * jnp.sqrt(diff_x * diff_x + diff_y * diff_y + DRAG_FLOOR)
    return jnp.stack([factor * diff_x, factor * diff_y, drag_base / CW])


def to_tile(blocks):
    channels, count, cells = blocks.shape
    arranged = blocks.reshape(channels, count // GX, GX, BY, BX).transpose(0, 1, 3, 2, 4)
    return arranged.reshape(channels, count // GX * BY, GX * BX)


def from_tile(values):
    channels, rows, columns = values.shape
    arranged = values.reshape(channels, rows // BY, BY, GX, BX).transpose(0, 1, 3, 2, 4)
    return arranged.reshape(channels, rows // BY * GX, BY * BX)


def per_device(fields, block_owner, ice_covered, land_mask):
    count = block_owner.shape[0]
    is_ocean = lax.axis_index("comp") == 0
    outbound, open_stress = air_stress(fields[0])
    owner_row = block_owner.reshape(1, count)
    crossed = from_behind(outbound, "comp", 1)
    received, anchor = (
        lax.all_to_all(crossed, ("lat", "lon"), split_axis=1, concat_axis=1, tiled=True),
        lax.all_to_all(owner_row, ("lat", "lon"), split_axis=1, concat_axis=1, tiled=True),
    )
    local_ids = anchor[0] % count
    position = jnp.zeros((count,), jnp.int32).at[local_ids].set(jnp.arange(count, dtype=jnp.int32))
    forcing = to_tile(received[:, position])
    ice_tile = to_tile(fields[0])
    covered = ice_covered.astype(jnp.float32)[:, None] * (1 - land_mask).astype(jnp.float32)
    active = to_tile(covered[None])[0]
    statics = prepare(ice_tile, forcing, active)
    ice_state = jnp.stack([ice_tile[0], ice_tile[1], ice_tile[4], ice_tile[5], ice_tile[6]])
    joined = jnp.concatenate([ice_state, statics], 0)
    joined = with_halo(joined, (("lon", 2),), NSUB, True)
    joined = with_halo(joined, (("lat", 1),), NSUB, False)
    ice_state = joined[:5]
    statics = joined[5:]
    for repeat in range(NSUB):
        ice_state, statics = subcycle(ice_state, statics)
    returned = from_tile(give_back(ice_state, statics))
    back_send = returned[:, local_ids]
    regrouped = lax.all_to_all(back_send, ("lat", "lon"), split_axis=1, concat_axis=1, tiled=True)
    received_back = from_behind(regrouped, "comp", -1)
    ocean_out = received_back[:2] + (1.0 - received_back[2]) * open_stress
    ice_out = from_tile(ice_state[:2])
    return jnp.where(is_ocean, ocean_out, ice_out)[None]


def solution(mesh):
    placed = (
        P("comp", None, ("lat", "lon"), None),
        P(("lat", "lon")),
        P(("lat", "lon")),
        P(("lat", "lon"), None),
    )
    return jax.shard_map(
        per_device,
        mesh=mesh,
        in_specs=placed,
        out_specs=P("comp", None, ("lat", "lon"), None),
        check_vma=False,
    )
```

profile of v0, /device:TPU:0, one launch (start us, length us, event | category | flops | bytes accessed | tf_op | source)
XLA Modules:
  0.0 125.6 jit_solution(1248778814458722191)
XLA Ops:
  0.0 1.8 %fusion.89 = f32[6,128,256]{2,1,0:T(8,128)} fusion(f32[1,7,128,256]{3,2,1,0:T(8,128)} %param.4), kind=kLoop, calls=%fused_computation.211 | loop fusion | flops 229375 | bytes 524288
  1.8 1.8 %fusion.88 = f32[6,128,256]{2,1,0:T(8,128)} fusion(f32[6,128,256]{2,1,0:T(8,128)} %fusion.89, f32[1,7,128,256]{3,2,1,0:T(8,128)} %param.4), kind=kLoop, calls=%fused_computation.208 | loop fusion | flops 229376 | bytes 524288
  3.6 1.6 %bitcast_dynamic-update-slice_fusion.3 = f32[6,128,256]{2,1,0:T(8,128)} fusion(f32[6,128,256]{2,1,0:T(8,128)} %fusion.88, f32[1,7,128,256]{3,2,1,0:T(8,128)} %param.4), kind=kLoop, calls=%fused_computation.201 | loop fusion | bytes 262144
  5.2 0.8 fusion.92
  7.3 3.3 %collective-permute-start = (f32[6,128,256]{2,1,0:T(8,128)}, f32[6,128,256]{2,1,0:T(8,128)}, u32[]{:S(2)}, u32[]{:S(2)}) collective-permute-start(f32[6,128,256]{2,1,0:T(8,128)} %bitcast_dynamic-update-slice_fusion), channel_id=1, source_target_pairs={{0,16},{1,17},{2,18},{3,19},{4,20},{5,21},{6,22},{7,23},{8,24},{9,... | collective-permute-start | bytes 2359304 | tf_op jit(solution)/shard_map/ppermute | solution.py:27
  11.2 7.7 %all-to-all-start.1 = ((s32[1,16,8]{2,0,1:T(1,128)}), s32[1,16,8]{2,0,1:T(1,128)S(1)}, u32[]{:S(2)}, u32[]{:S(2)}) async-start(s32[1,16,8]{2,0,1:T(1,128)} %bitcast.7), calls=%async_computation.1 | async-start | bytes 16384 | tf_op jit(solution)/shard_map/all_to_all | solution.py:167
  19.3 1.6 %fusion.83 = (f32[1,128,256]{2,1,0:T(8,128)}, f32[128,256]{1,0:T(8,128)S(1)}) fusion(f32[1,7,128,256]{3,2,1,0:T(8,128)S(1)} %copy-done, s32[128,256]{1,0:T(8,128)} %param.7, f32[128]{0:T(128)S(1)} %convert_element_type.6), kind=kLoop, calls=%fused_computation.195 | loop fusion | flops 196608 | bytes 524800 | tf_op jit(solution)/shard_map/div | solution.py:144
  21.0 0.7 copy.225
  21.7 0.8 copy.226
  22.5 0.7 copy.227
  23.6 2.6 %copy.211 = f32[6,128,256]{2,0,1:T(8,128)} copy(f32[6,128,256]{2,1,0:T(8,128)} %collective-permute-done) | data formatting | bytes 1572864 | tf_op jit(solution)/shard_map/ppermute | solution.py:27
  26.2 6.9 %all-to-all-start = ((f32[6,128,256]{2,0,1:T(8,128)}), f32[6,128,256]{2,0,1:T(8,128)S(1)}, u32[]{:S(2)}, u32[]{:S(2)}) async-start(f32[6,128,256]{2,0,1:T(8,128)} %copy.211), calls=%async_computation | async-start | bytes 2097152 | tf_op jit(solution)/shard_map/all_to_all | solution.py:166
  33.2 0.9 constant_dynamic-update-slice_fusion.6
  34.1 0.9 constant_dynamic-update-slice_fusion.5
  35.0 0.9 constant_dynamic-update-slice_fusion.4
  37.2 1.0 scatter_custom_fusion
  38.2 17.4 %all-to-all-done = f32[6,128,256]{2,0,1:T(8,128)S(1)} async-done(((f32[6,128,256]{2,0,1:T(8,128)}), f32[6,128,256]{2,0,1:T(8,128)S(1)}, u32[]{:S(2)}, u32[]{:S(2)}) %all-to-all-start) | async-done | bytes 786464 | tf_op jit(solution)/shard_map/all_to_all | solution.py:166
  55.7 1.8 %gather_fusion = f32[128,6,256]{2,1,0:T(8,128)} fusion(f32[6,128,256]{2,0,1:T(8,128)S(1)} %all-to-all-done, s32[1024]{0:T(1024)S(1)} %pad_clamp_fusion.1), kind=kCustom, calls=%fused_computation | custom fusion | bytes 1573376 | tf_op jit(solution)/shard_map/gather | solution.py:171
  57.4 4.3 %fusion.122 = (f32[1,128,256]{2,0,1:T(1,128)S(1)}, f32[1,128,256]{2,0,1:T(1,128)S(1)}, f32[1,128,256]{2,0,1:T(1,128)S(1)}, f32[1,128,256]{2,0,1:T(1,128)S(1)}, f...) fusion(f32[6,128,256]{2,0,1:T(8,128)} %bitcast.344), kind=kLoop, calls=%fused_computation.251 | loop fusion | bytes 1572864 | tf_op jit(solution)/shard_map/slice | solution.py:64
  61.8 0.9 copy.216
  63.4 0.8 copy.221
  64.2 0.8 copy.219
  65.1 1.0 multiply_dynamic-update-slice_fusion.1
  66.2 1.0 multiply_dynamic-update-slice_fusion
  67.3 2.0 %collective-permute-start.2 = (f32[13,256,4]{1,2,0:T(4,128)S(1)}, f32[13,256,4]{1,2,0:T(4,128)S(1)}, u32[]{:S(2)}, u32[]{:S(2)}) collective-permute-start(f32[13,256,4]{1,2,0:T(4,128)S(1)} %get-tuple-element.45), channel_id=1, source_target_pairs={{1,0},{2,1},{3,2},{0,3},{5,4},{6,5},{7,6},{4,7},{9,8},{10,9},{11,1... | collective-permute-start | bytes 159752 | tf_op jit(solution)/shard_map/ppermute | solution.py:38
  69.4 0.7 copy.204
  70.2 0.8 copy.203
  70.9 0.7 copy.205
  71.7 2.7 %collective-permute-done.1 = f32[13,256,4]{1,2,0:T(4,128)S(1)} collective-permute-done((f32[13,256,4]{1,2,0:T(4,128)S(1)}, f32[13,256,4]{1,2,0:T(4,128)S(1)}, u32[]{:S(2)}, u32[]{:S(2)}) %collective-permute-start.1) | collective-permute-done | bytes 53280 | tf_op jit(solution)/shard_map/ppermute | solution.py:37
  75.4 1.1 copy.233
  76.6 1.4 %collective-permute-start.4 = (f32[13,4,136]{2,1,0:T(4,128)}, f32[13,4,136]{2,1,0:T(4,128)S(1)}, u32[]{:S(2)}, u32[]{:S(2)}) collective-permute-start(f32[13,4,136]{2,1,0:T(4,128)} %copy.233), channel_id=1, source_target_pairs={{4,0},{8,4},{12,8},{5,1},{9,5},{13,9},{6,2},{10,6},{14,10},{7,3},{... | collective-permute-start | bytes 84872 | tf_op jit(solution)/shard_map/ppermute | solution.py:38
  78.5 5.5 %collective-permute-start.3 = (f32[13,4,136]{2,1,0:T(4,128)S(1)}, f32[13,4,136]{2,1,0:T(4,128)}, u32[]{:S(2)}, u32[]{:S(2)}) collective-permute-start(f32[13,4,136]{2,1,0:T(4,128)S(1)} %copy.232), channel_id=1, source_target_pairs={{0,4},{4,8},{8,12},{1,5},{5,9},{9,13},{2,6},{6,10},{10,14},{3,7},{... | collective-permute-start | bytes 84872 | tf_op jit(solution)/shard_map/ppermute | solution.py:37
  84.0 1.7 %copy.242 = f32[256,128]{0,1:T(8,128)} copy(f32[256,128]{1,0:T(8,128)} %bitcast.357) | data formatting | bytes 262144 | tf_op jit(solution)/shard_map/unstack | solution.py:100
  85.6 1.7 %copy.241 = f32[256,128]{0,1:T(8,128)} copy(f32[256,128]{1,0:T(8,128)} %bitcast.355) | data formatting | bytes 262144 | tf_op jit(solution)/shard_map/unstack | solution.py:100
  87.3 1.6 %copy.239 = f32[256,128]{0,1:T(8,128)} copy(f32[256,128]{1,0:T(8,128)} %bitcast.353) | data formatting | bytes 262144 | tf_op jit(solution)/shard_map/squeeze | solution.py:63
  88.9 0.8 copy.237
  89.7 0.8 copy.251
  90.5 0.7 copy.249
  91.6 1.2 copy.234
  92.7 2.0 %pad_maximum_fusion = f32[13,264,136]{1,2,0:T(8,128)S(1)} fusion(f32[13,4,136]{1,2,0:T(8,128)S(1)} %copy.235, f32[13,256,4]{1,2,0:T(4,128)} %copy-done.22, f32[13,256,128]{1,2,0:T(8,128)S(1)} %constant_dynamic-update-slice_fusion, f32[13,256,4]{1,2,0:T(4,128)} %copy-done.23, f32[13,4,136]{1,2,0:T(8,128)S(1)} %copy.234), kind=kLoop, calls=%fused_computation.3 | loop fusion | flops 1867008 | bytes 3734016 | tf_op jit(solution)/shard_map/concatenate | solution.py:39
  95.6 0.8 fusion.59
  97.6 0.8 fusion.39
  99.6 0.8 fusion.19
  103.5 0.9 gather_fusion.1
  104.4 16.7 %all_to_all.19 = f32[3,128,256]{2,0,1:T(4,128)S(1)} all-to-all(f32[3,128,256]{2,0,1:T(4,128)S(1)} %bitcast.345), channel_id=1, replica_groups=mesh['comp'=2,'lat'=4,'lon'=4] {'lat','lon'}, dimensions={1} | all-to-all | bytes 786432 | tf_op jit(solution)/shard_map/all_to_all | solution.py:186
  121.2 1.3 %collective-permute-start.5 = (f32[3,128,256]{2,1,0:T(8,128)S(1)}, f32[3,128,256]{2,1,0:T(8,128)S(1)}, u32[]{:S(2)}, u32[]{:S(2)}) collective-permute-start(f32[3,128,256]{2,1,0:T(8,128)S(1)} %copy.259), channel_id=1, source_target_pairs={{16,0},{17,1},{18,2},{19,3},{20,4},{21,5},{22,6},{23,7},{24,8},{25... | collective-permute-start | bytes 1179656 | tf_op jit(solution)/shard_map/ppermute | solution.py:27
  122.7 2.0 %collective-permute-done.5 = f32[3,128,256]{2,1,0:T(8,128)S(1)} collective-permute-done((f32[3,128,256]{2,1,0:T(8,128)S(1)}, f32[3,128,256]{2,1,0:T(8,128)S(1)}, u32[]{:S(2)}, u32[]{:S(2)}) %collective-permute-start.5) | collective-permute-done | bytes 393248 | tf_op jit(solution)/shard_map/ppermute | solution.py:27
  124.8 0.8 fusion.1
  (135 shorter events, 13.6 us)
Async XLA Ops:
  0.0 5.1 %copy-start = (f32[1,7,128,256]{3,2,1,0:T(8,128)S(1)}, f32[1,7,128,256]{3,2,1,0:T(8,128)}, u32[]{:S(2)}) copy-start(f32[1,7,128,256]{3,2,1,0:T(8,128)} %param.4) | copy-start | bytes 2752516
  0.0 10.6 %copy-start.24 = (s32[128]{0:T(128)S(1)}, s32[128]{0:T(128)}, u32[]{:S(2)}) copy-start(s32[128]{0:T(128)} %param.5) | copy-start | bytes 1540
  0.0 18.9 %copy-start.25 = (s32[128]{0:T(128)S(1)}, s32[128]{0:T(128)}, u32[]{:S(2)}) copy-start(s32[128]{0:T(128)} %param.6) | copy-start | bytes 1540
  7.3 16.3 %collective-permute-start = (f32[6,128,256]{2,1,0:T(8,128)}, f32[6,128,256]{2,1,0:T(8,128)}, u32[]{:S(2)}, u32[]{:S(2)}) collective-permute-start(f32[6,128,256]{2,1,0:T(8,128)} %bitcast_dynamic-update-slice_fusion), channel_id=1, source_target_pairs={{0,16},{1,17},{2,18},{3,19},{4,20},{5,21},{6,22},{7,23},{8,24},{9,... | collective-permute-start | bytes 2359304 | tf_op jit(solution)/shard_map/ppermute | solution.py:27
  11.2 15.0 %all-to-all-start.1 = ((s32[1,16,8]{2,0,1:T(1,128)}), s32[1,16,8]{2,0,1:T(1,128)S(1)}, u32[]{:S(2)}, u32[]{:S(2)}) async-start(s32[1,16,8]{2,0,1:T(1,128)} %bitcast.7), calls=%async_computation.1 | async-start | bytes 16384 | tf_op jit(solution)/shard_map/all_to_all | solution.py:167
  26.2 29.4 %all-to-all-start = ((f32[6,128,256]{2,0,1:T(8,128)}), f32[6,128,256]{2,0,1:T(8,128)S(1)}, u32[]{:S(2)}, u32[]{:S(2)}) async-start(f32[6,128,256]{2,0,1:T(8,128)} %copy.211), calls=%async_computation | async-start | bytes 2097152 | tf_op jit(solution)/shard_map/all_to_all | solution.py:166
  61.8 5.4 %copy-start.1 = (f32[1,128,256]{2,0,1:T(1,128)}, f32[1,128,256]{2,0,1:T(1,128)S(1)}, u32[]{:S(2)}) copy-start(f32[1,128,256]{2,0,1:T(1,128)S(1)} %get-tuple-element.46) | copy-start | bytes 393220
  61.8 5.4 %copy-start.3 = (f32[1,128,256]{2,0,1:T(1,128)}, f32[1,128,256]{2,0,1:T(1,128)S(1)}, u32[]{:S(2)}) copy-start(f32[1,128,256]{2,0,1:T(1,128)S(1)} %get-tuple-element.48) | copy-start | bytes 393220
  61.8 5.4 %copy-start.5 = (f32[1,128,256]{2,0,1:T(1,128)}, f32[1,128,256]{2,0,1:T(1,128)S(1)}, u32[]{:S(2)}) copy-start(f32[1,128,256]{2,0,1:T(1,128)S(1)} %get-tuple-element.50) | copy-start | bytes 393220
  61.8 5.4 %copy-start.9 = (f32[1,128,256]{2,0,1:T(1,128)}, f32[1,128,256]{2,0,1:T(1,128)S(1)}, u32[]{:S(2)}) copy-start(f32[1,128,256]{2,0,1:T(1,128)S(1)} %get-tuple-element.51) | copy-start | bytes 393220
  61.8 12.5 %copy-start.7 = (f32[1,128,256]{2,0,1:T(1,128)}, f32[1,128,256]{2,0,1:T(1,128)S(1)}, u32[]{:S(2)}) copy-start(f32[1,128,256]{2,0,1:T(1,128)S(1)} %get-tuple-element.49) | copy-start | bytes 393220
  61.8 12.5 %copy-start.8 = (f32[1,128,256]{2,0,1:T(1,128)}, f32[1,128,256]{2,0,1:T(1,128)S(1)}, u32[]{:S(2)}) copy-start(f32[1,128,256]{2,0,1:T(1,128)S(1)} %get-tuple-element.47) | copy-start | bytes 393220
  67.3 4.4 %collective-permute-start.2 = (f32[13,256,4]{1,2,0:T(4,128)S(1)}, f32[13,256,4]{1,2,0:T(4,128)S(1)}, u32[]{:S(2)}, u32[]{:S(2)}) collective-permute-start(f32[13,256,4]{1,2,0:T(4,128)S(1)} %get-tuple-element.45), channel_id=1, source_target_pairs={{1,0},{2,1},{3,2},{0,3},{5,4},{6,5},{7,6},{4,7},{9,8},{10,9},{11,1... | collective-permute-start | bytes 159752 | tf_op jit(solution)/shard_map/ppermute | solution.py:38
  69.3 5.0 %collective-permute-start.1 = (f32[13,256,4]{1,2,0:T(4,128)S(1)}, f32[13,256,4]{1,2,0:T(4,128)S(1)}, u32[]{:S(2)}, u32[]{:S(2)}) collective-permute-start(f32[13,256,4]{1,2,0:T(4,128)S(1)} %get-tuple-element.44), channel_id=1, source_target_pairs={{0,1},{1,2},{2,3},{3,0},{4,5},{5,6},{6,7},{7,4},{8,9},{9,10},{10,1... | collective-permute-start | bytes 159752 | tf_op jit(solution)/shard_map/ppermute | solution.py:37
  71.7 2.7 %copy-start.22 = (f32[13,256,4]{1,2,0:T(4,128)}, f32[13,256,4]{1,2,0:T(4,128)S(1)}, u32[]{:S(2)}) copy-start(f32[13,256,4]{1,2,0:T(4,128)S(1)} %collective-permute-done.2) | copy-start | bytes 159748
  74.4 0.6 copy-start.23
  76.6 12.4 %copy-start.6 = (f32[1,128,256]{2,0,1:T(1,128)S(1)}, f32[1,128,256]{2,0,1:T(1,128)}, u32[]{:S(2)}) copy-start(f32[1,128,256]{2,0,1:T(1,128)} %copy-done.5) | copy-start | bytes 393220
  76.6 13.1 %copy-start.4 = (f32[1,128,256]{2,0,1:T(1,128)S(1)}, f32[1,128,256]{2,0,1:T(1,128)}, u32[]{:S(2)}) copy-start(f32[1,128,256]{2,0,1:T(1,128)} %copy-done.3) | copy-start | bytes 393220
  76.6 13.9 %copy-start.2 = (f32[1,128,256]{2,0,1:T(1,128)S(1)}, f32[1,128,256]{2,0,1:T(1,128)}, u32[]{:S(2)}) copy-start(f32[1,128,256]{2,0,1:T(1,128)} %copy-done.1) | copy-start | bytes 393220
  76.6 14.6 %collective-permute-start.4 = (f32[13,4,136]{2,1,0:T(4,128)}, f32[13,4,136]{2,1,0:T(4,128)S(1)}, u32[]{:S(2)}, u32[]{:S(2)}) collective-permute-start(f32[13,4,136]{2,1,0:T(4,128)} %copy.233), channel_id=1, source_target_pairs={{4,0},{8,4},{12,8},{5,1},{9,5},{13,9},{6,2},{10,6},{14,10},{7,3},{... | collective-permute-start | bytes 84872 | tf_op jit(solution)/shard_map/ppermute | solution.py:38
  78.5 13.1 %collective-permute-start.3 = (f32[13,4,136]{2,1,0:T(4,128)S(1)}, f32[13,4,136]{2,1,0:T(4,128)}, u32[]{:S(2)}, u32[]{:S(2)}) collective-permute-start(f32[13,4,136]{2,1,0:T(4,128)S(1)} %copy.232), channel_id=1, source_target_pairs={{0,4},{4,8},{8,12},{1,5},{5,9},{9,13},{2,6},{6,10},{10,14},{3,7},{... | collective-permute-start | bytes 84872 | tf_op jit(solution)/shard_map/ppermute | solution.py:37
  100.9 0.9 copy-start.10
  101.0 1.0 copy-start.11
  101.0 1.0 copy-start.12
  101.0 1.1 copy-start.13
  101.0 1.1 copy-start.17
  101.0 1.2 copy-start.18
  101.0 1.2 copy-start.19
  101.0 1.2 copy-start.20
  101.0 1.3 %copy-start.21 = (f32[256,128]{0,1:T(8,128)S(1)}, f32[256,128]{0,1:T(8,128)}, u32[]{:S(2)}) copy-start(f32[256,128]{0,1:T(8,128)} %copy.249) | copy-start | bytes 393220
  102.3 0.9 copy-start.14
  104.4 20.4 %copy-start.15 = (f32[1,128,256]{2,1,0:T(8,128)S(1)}, f32[1,128,256]{2,1,0:T(8,128)}, u32[]{:S(2)}) copy-start(f32[1,128,256]{2,1,0:T(8,128)} %get-tuple-element.52) | copy-start | bytes 393220
  104.4 20.4 %copy-start.16 = (f32[1,128,256]{2,1,0:T(8,128)S(1)}, f32[1,128,256]{2,1,0:T(8,128)}, u32[]{:S(2)}) copy-start(f32[1,128,256]{2,1,0:T(8,128)} %get-tuple-element.54) | copy-start | bytes 393220
  121.2 3.6 %collective-permute-start.5 = (f32[3,128,256]{2,1,0:T(8,128)S(1)}, f32[3,128,256]{2,1,0:T(8,128)S(1)}, u32[]{:S(2)}, u32[]{:S(2)}) collective-permute-start(f32[3,128,256]{2,1,0:T(8,128)S(1)} %copy.259), channel_id=1, source_target_pairs={{16,0},{17,1},{18,2},{19,3},{20,4},{21,5},{22,6},{23,7},{24,8},{25... | collective-permute-start | bytes 1179656 | tf_op jit(solution)/shard_map/ppermute | solution.py:27
where the time goes:
time: 126 us
  local copies, waits for them, and re-layouts  39.3 us (31%)
  starting transfers between devices  28.1 us (22%)
  waiting for transfers between devices  22.1 us (18%)
  other arithmetic  18.5 us (15%)
  blocking collectives  16.7 us (13%)
    all_to_all x1, waiting for transfers between devices, per_device(): lax.all_to_all(crossed, ('lat', 'lon'), split_axis=1, concat_axis=1, tile...  17.4 us
    all_to_all x1, blocking collectives, per_device(): lax.all_to_all(back_send, ('lat', 'lon'), split_axis=1, concat_axis=1, ti...  16.7 us
    all_to_all x1, starting transfers between devices, per_device(): lax.all_to_all(owner_row, ('lat', 'lon'), split_axis=1, concat_axis=1, ti...  7.68 us
    all_to_all x1, starting transfers between devices, per_device(): lax.all_to_all(crossed, ('lat', 'lon'), split_axis=1, concat_axis=1, tile...  6.91 us
    unnamed x62, local copies, waits for them, and re-layouts  6.39 us
    unnamed x6, other arithmetic  5.66 us
    ppermute x2, starting transfers between devices, with_halo(): before = lax.ppermute(last, axis, up)  5.53 us
    ppermute x2, starting transfers between devices, from_behind(): return lax.ppermute(x, axis, pairs)  4.58 us
  transfers between devices with their start and end apart: 8, of which 3 were waited for; matrix products, arithmetic and copies ran while one was open for 18% of the time, Pallas kernels for 0%

commit v1 on v0

v1 whole, which is shorter than its diff:
```python
import functools

import jax
import jax.numpy as jnp
from jax import lax
from jax.experimental import pallas as pl
from jax.experimental.pallas import tpu as pltpu
from jax.sharding import PartitionSpec as P

BX = 128
NSUB = 4
FRONT = 8
STEP = 16

CD_ICE = 0.1
CW = 1.5
CSTAR = 2.0
CORIO = 0.3
DRAG_FLOOR = 0.1

VMEM = pl.BlockSpec(memory_space=pltpu.VMEM)
SMEM = pl.BlockSpec(memory_space=pltpu.SMEM)


def f32(*shape):
    return jax.ShapeDtypeStruct(shape, jnp.float32)


def lanes(rows):
    return lax.broadcasted_iota(jnp.int32, (rows, BX), 1)


def roll(x, by):
    return pltpu.roll(x, by % BX, 1)


def at_end(q, west, east):
    return jnp.where(q, west, east)


def pack_kernel(nlat, nlon, per, count, raw, idb, pay, edge, rim):
    n = nlat * nlon
    lane = lanes(per)
    group = lane // 8
    lat_base = 13 * per

    def tile(t, _):
        def half(ch, y):
            return raw[ch, t, :, y * BX : (y + 1) * BX]

        planes = [None] * 12
        for y in range(2):
            wx, wy, rho = half(0, y), half(1, y), half(6, y)
            scale = rho * CD_ICE * jnp.sqrt(wx * wx + wy * wy + 1.0)
            planes[y] = scale * wx
            planes[2 + y] = scale * wy
            for ch in range(2, 6):
                planes[2 * ch + y] = half(ch, y)
        ends = jnp.zeros((per, BX), jnp.float32)
        for p in range(12):
            pay[t, pl.ds(p, per, stride=12), :] = planes[p]
            ends = jnp.where(group == p, roll(planes[p], 8 * p + 4), ends)
        edge[t] = ends
        ids = idb[t]

        def pick(block, value):
            return jnp.sum(jnp.where(ids == block, value, 0.0), axis=0, keepdims=True)

        rows = [pick(0, x) for x in planes] + [pick(1, x) for x in planes[0::2]]
        rows += [pick(count - 1, x) for x in planes]
        rows += [pick(count - 2, x) for x in planes[1::2]]
        rows += [pick(b, ends) for b in (0, 1, count - 1, count - 2)]
        for k, row in enumerate(rows):
            rim[t, k : k + 1, :] = row
        return 0

    lax.fori_loop(0, n, tile, 0)

    def dest(d, _):
        i, j = d // nlon, d % nlon
        jw, je = (j + nlon - 1) % nlon, (j + 1) % nlon
        q8 = (lane % 8) < 4
        pay[d, 12 * per : 13 * per, :] = at_end(q8, edge[i * nlon + jw], edge[i * nlon + je])
        for ii, ok, lo, c in (
            (jnp.minimum(i + 1, nlat - 1), i + 1 < nlat, 0, 36),
            (jnp.maximum(i - 1, 0), i > 0, 18, 38),
        ):
            scale = jnp.where(ok, 1.0, 0.0)
            pay[d, lat_base + lo : lat_base + lo + 18, :] = rim[ii * nlon + j, lo : lo + 18, :] * scale
            q2 = (lanes(2) % 8) < 4
            corner = at_end(q2, rim[ii * nlon + jw, c : c + 2, :], rim[ii * nlon + je, c : c + 2, :])
            pay[d, lat_base + c : lat_base + c + 2, :] = corner * scale
        return 0

    lax.fori_loop(0, n, dest, 0)


def pack(raw, idb, nlat, nlon):
    _, n, per, _ = raw.shape
    rows = 13 * per + 40
    return pl.pallas_call(
        functools.partial(pack_kernel, nlat, nlon, per, n * per),
        out_shape=f32(n, rows, BX),
        in_specs=[VMEM, VMEM],
        out_specs=VMEM,
        scratch_shapes=[pltpu.VMEM((n, per, BX), jnp.float32), pltpu.VMEM((n, 40, BX), jnp.float32)],
        name="pack",
    )(raw, idb)


def ends_kernel(ice, covered, land, active, ends):
    count = covered.shape[0]
    lane = lanes(count)
    group = lane // 8
    total = jnp.zeros((count, BX), jnp.float32)
    for y in range(2):
        cells = slice(y * BX, (y + 1) * BX)
        act = covered[...].astype(jnp.float32) * (1 - land[:, cells]).astype(jnp.float32)
        active[:, cells] = act
        for ch in range(8):
            x = act if ch == 7 else ice[ch, :, cells]
            p = 2 * ch + y
            total = jnp.where(group == p, roll(x, 8 * p + 4), total)
    ends[...] = total


def ice_ends(ice, covered, land):
    count = covered.shape[0]
    return pl.pallas_call(
        ends_kernel,
        out_shape=[f32(count, 2 * BX), f32(count, BX)],
        in_specs=[VMEM] * 3,
        out_specs=[VMEM] * 2,
        name="ice_ends",
    )(ice, covered, land)


def rows_kernel(ice, active, west, east, sides, north, south):
    count = active.shape[0]
    q = (lanes(count) % 8) < 4
    sides[...] = jnp.where(q, west[...], east[...])
    for out, lo in ((north, count - 2), (south, 0)):
        for y in range(2):
            cells = slice(y * BX, (y + 1) * BX)
            for ch in range(8):
                p = 2 * ch + y
                x = active[lo : lo + 2, cells] if ch == 7 else ice[ch, lo : lo + 2, cells]
                out[2 * p : 2 * p + 2, :] = x
        out[32:34, :] = sides[lo : lo + 2, :]


def ice_rows(ice, active, west, east):
    count = active.shape[0]
    return pl.pallas_call(
        rows_kernel,
        out_shape=[f32(count, BX), f32(34, BX), f32(34, BX)],
        in_specs=[VMEM] * 4,
        out_specs=[VMEM] * 3,
        name="ice_rows",
    )(ice, active, west, east)


def east_of(first, second, last):
    a, b = roll(first, -1), roll(second, -1)
    return jnp.where(last, b, a), jnp.where(last, a, b)


def west_of(first, second, start):
    a, b = roll(first, 1), roll(second, 1)
    return jnp.where(start, b, a), jnp.where(start, a, b)


def ice_kernel(n, per, count, ids, recv, ice, active, sides, below, above, back, moved,
               spot, hw, he, grid, state, fixed, cross, out8):
    tiles = (count + 4 + 7) // 8
    height = tiles * 8
    blank = jnp.zeros((8, BX), jnp.float32)
    for k in range(count + 4, height):
        spot[k * STEP : k * STEP + 8, :] = blank
        spot[k * STEP + 8 : k * STEP + 16, :] = blank
    for k in (0, height - 8):
        hw[k : k + 8, :] = blank
        he[k : k + 8, :] = blank
    spot[0:8, :] = blank
    spot[8:16, :] = blank
    end = (count + 3) * STEP
    spot[end : end + 8, :] = blank
    spot[end + 8 : end + 16, :] = blank

    def place(o, acc):
        for j in range(per):
            b = pl.multiple_of((ids[o, j] + 2) * STEP, STEP)
            spot[pl.ds(b, 12), :] = recv[o, 12 * j : 12 * j + 12, :]
            row = recv[o, 12 * per + j : 12 * per + j + 1, :]
            hw[pl.ds(ids[o, per + j] + 2, 1), :] = row
            he[pl.ds(ids[o, 2 * per + j] + 2, 1), :] = row
        return acc + recv[o, 13 * per : 13 * per + 40, :]

    rim = lax.fori_loop(0, n, place, jnp.zeros((40, BX), jnp.float32))
    up, down = (count + 2) * STEP, STEP
    spot[up : up + 12, :] = rim[0:12]
    spot[down : down + 12, :] = rim[18:30]
    for ch in range(6):
        k = up + STEP + 2 * ch
        spot[k : k + 1, :] = rim[12 + ch : 13 + ch]
        k = 2 * ch + 1
        spot[k : k + 1, :] = rim[30 + ch : 31 + ch]
    for ref in (hw, he):
        ref[count + 2 : count + 4, :] = rim[36:38]
        ref[1:2, :] = rim[38:39]
        ref[0:1, :] = rim[39:40]

    q = (lanes(8) % 8) < 4
    for ch in range(8):
        for y in range(2):
            p = 2 * ch + y
            cells = slice(y * BX, (y + 1) * BX)
            shift = -(8 * p + 4)
            grid[ch, y, 0, 2 : 2 + count, :] = active[:, cells] if ch == 7 else ice[ch, :, cells]
            grid[ch, y, 1, 2 : 2 + count, :] = roll(sides[...], shift)
            for lo, msg in ((0, below), (count + 2, above)):
                grid[ch, y, 0, lo : lo + 2, :] = msg[2 * p : 2 * p + 2, :]
                grid[ch, y, 1, lo : lo + 2, :] = roll(msg[32:34, :], shift)
            grid[ch, y, 0, count + 4 :, :] = jnp.zeros((height - count - 4, BX), jnp.float32)
            grid[ch, y, 1, count + 4 :, :] = jnp.zeros((height - count - 4, BX), jnp.float32)

    for r in range(tiles):
        at = slice(8 * r, 8 * r + 8)
        to = slice(FRONT + 8 * r, FRONT + 8 * r + 8)
        ends = jnp.where(q, hw[at, :], he[at, :])
        for y in range(2):
            for w in range(2):
                if w == 0:
                    f = [spot[pl.ds(8 * r * STEP + 2 * ch + y, 8, stride=STEP), :] for ch in range(6)]
                else:
                    f = [roll(ends, -(8 * (2 * ch + y) + 4)) for ch in range(6)]
                u, v, mass, conc, s1, s2, s12, act = [grid[ch, y, w, at, :] for ch in range(8)]
                state[0, y, w, to, :] = u
                state[1, y, w, to, :] = v
                state[2, y, w, to, :] = s1
                state[3, y, w, to, :] = s2
                state[4, y, w, to, :] = s12
                fixed[0, y, w, at, :] = mass * jnp.exp(CSTAR * (conc - 1.0)) * act * (1.0 / 3.0)
                fixed[1, y, w, at, :] = mass
                fixed[2, y, w, at, :] = CW * conc * act
                fixed[3, y, w, at, :] = act * (conc * f[0] - mass * f[4])
                fixed[4, y, w, at, :] = act * (conc * f[1] - mass * f[5])
                fixed[5, y, w, at, :] = f[2]
                fixed[6, y, w, at, :] = f[3]
                fixed[7, y, w, at, :] = act

    tail = FRONT + height
    for k in range(2):
        for y in range(2):
            for w in range(2):
                state[k, y, w, tail : tail + 8, :] = blank
    for w in range(2):
        state[4, 1, w, 0:8, :] = blank
        cross[w, 0:8, :] = blank

    lane = lanes(8)
    last, start = lane == BX - 1, lane == 0
    both = [(y, w) for y in range(2) for w in range(2)]

    def subcycle(_, carry):
        for r in range(tiles):
            at = slice(8 * r, 8 * r + 8)
            lo = FRONT + 8 * r
            to, up1, down1 = slice(lo, lo + 8), slice(lo + 1, lo + 9), slice(lo - 1, lo + 7)
            u = {k: state[0, k[0], k[1], to, :] for k in both}
            v = {k: state[1, k[0], k[1], to, :] for k in both}
            un = {(0, w): u[1, w] for w in range(2)} | {(1, w): state[0, 0, w, up1, :] for w in range(2)}
            vn = {(0, w): v[1, w] for w in range(2)} | {(1, w): state[1, 0, w, up1, :] for w in range(2)}
            a, c, s12 = {}, {}, {}
            for y in range(2):
                ue = east_of(u[y, 0], u[y, 1], last)
                ve = east_of(v[y, 0], v[y, 1], last)
                for w in range(2):
                    k = y, w
                    sxx = ue[w] - u[k]
                    syy = vn[k] - v[k]
                    shear = (un[k] - u[k]) + (ve[w] - v[k])
                    div, ten = sxx + syy, sxx - syy
                    x = div * div + ((ten * ten + shear * shear) * 0.25 + 0.25)
                    inv = lax.rsqrt(x)
                    kr = fixed[0, y, w, at, :] * inv
                    t1 = state[2, y, w, to, :] * (2.0 / 3.0) + kr * (div - x * inv)
                    t2 = state[3, y, w, to, :] * (2.0 / 3.0) + kr * (ten * 0.25)
                    t3 = state[4, y, w, to, :] * (2.0 / 3.0) + kr * (shear * 0.125)
                    state[2, y, w, to, :] = t1
                    state[3, y, w, to, :] = t2
                    state[4, y, w, to, :] = t3
                    s12[k] = t3
                    a[k] = 0.5 * (t1 + t2)
                    c[k] = 0.5 * (t1 - t2)
            for w in range(2):
                cross[w, to, :] = c[1, w]
            for y in range(2):
                aw = west_of(a[y, 0], a[y, 1], start)
                sw = west_of(s12[y, 0], s12[y, 1], start)
                for w in range(2):
                    k = y, w
                    if y == 1:
                        s12s, cs = s12[0, w], c[0, w]
                    else:
                        s12s, cs = state[4, 1, w, down1, :], cross[w, down1, :]
                    fx = (a[k] - aw[w]) + (s12[k] - s12s)
                    fy = (s12[k] - sw[w]) + (c[k] - cs)
                    mass, base = fixed[1, y, w, at, :], fixed[2, y, w, at, :]
                    cx, cy = fixed[5, y, w, at, :], fixed[6, y, w, at, :]
                    dx, dy = cx - u[k], cy - v[k]
                    drag = base * jnp.sqrt(dx * dx + dy * dy + DRAG_FLOOR)
                    m2 = mass * 2.0
                    part = fixed[7, y, w, at, :] / (jnp.maximum(m2, 1.0) + drag)
                    mc = CORIO * mass
                    state[0, y, w, to, :] = part * (m2 * u[k] + fx + fixed[3, y, w, at, :] + drag * cx + mc * v[k])
                    state[1, y, w, to, :] = part * (m2 * v[k] + fy + fixed[4, y, w, at, :] + drag * cy - mc * u[k])
        return carry

    lax.fori_loop(0, NSUB, subcycle, 0)

    for r in range(tiles):
        at = slice(8 * r, 8 * r + 8)
        to = slice(FRONT + 8 * r, FRONT + 8 * r + 8)
        for y in range(2):
            base = fixed[2, y, 0, at, :]
            dx = state[0, y, 0, to, :] - fixed[5, y, 0, at, :]
            dy = state[1, y, 0, to, :] - fixed[6, y, 0, at, :]
            factor = base * jnp.sqrt(dx * dx + dy * dy + DRAG_FLOOR)
            for k, x in enumerate((factor * dx, factor * dy, base * (1.0 / CW))):
                out8[pl.ds(64 * r + 2 * k + y, 8, stride=8), :] = x
    for y in range(2):
        for k in range(2):
            moved[k, :, y * BX : (y + 1) * BX] = state[k, y, 0, FRONT + 2 : FRONT + 2 + count, :]

    def answer(o, _):
        for j in range(per):
            b = pl.multiple_of((ids[o, j] + 2) * 8, 8)
            back[o, 6 * j : 6 * j + 6, :] = out8[pl.ds(b, 6), :]
        return 0

    lax.fori_loop(0, n, answer, 0)


def ice_step(ids, recv, ice, active, sides, below, above):
    n, per = ids.shape[0], ids.shape[1] // 3
    count = n * per
    height = (count + 4 + 7) // 8 * 8
    tall = height + 2 * FRONT
    scratch = [
        (height * STEP, BX), (height, BX), (height, BX), (8, 2, 2, height, BX),
        (5, 2, 2, tall, BX), (8, 2, 2, height, BX), (2, tall, BX), (height * 8, BX),
    ]
    return pl.pallas_call(
        functools.partial(ice_kernel, n, per, count),
        out_shape=[f32(n, 6 * per, BX), f32(2, count, 2 * BX)],
        in_specs=[SMEM] + [VMEM] * 6,
        out_specs=[VMEM] * 2,
        scratch_shapes=[pltpu.VMEM(s, jnp.float32) for s in scratch],
        name="ice_step",
    )(ids, recv, ice, active, sides, below, above)


def final_kernel(n, per, flag, got, raw, moved, out):
    @pl.when(flag[0] == 0)
    def _():
        def tile(t, _):
            for y in range(2):
                cells = slice(y * BX, (y + 1) * BX)
                wx, wy, cx, cy, rho = [raw[ch, t, :, cells] for ch in (0, 1, 2, 3, 6)]
                rx, ry = wx - cx, wy - cy
                speed = jnp.sqrt(rx * rx + ry * ry + 1.0)
                scale = rho * (0.1 + 0.05 * speed) * speed
                gx, gy, gc = [got[t, pl.ds(2 * k + y, per, stride=6), :] for k in range(3)]
                rest = (1.0 - gc) * scale
                out[0, t, :, cells] = gx + rest * rx
                out[1, t, :, cells] = gy + rest * ry
            return 0

        lax.fori_loop(0, n, tile, 0)

    @pl.when(flag[0] != 0)
    def _():
        out[...] = moved[...]


def final(flag, got, raw, moved):
    _, n, per, cells = raw.shape
    return pl.pallas_call(
        functools.partial(final_kernel, n, per),
        out_shape=f32(2, n, per, cells),
        in_specs=[SMEM] + [VMEM] * 3,
        out_specs=VMEM,
        name="final",
    )(flag, got, raw, moved)


def per_device(fields, block_owner, ice_covered, land_mask):
    nlat, nlon = lax.axis_size("lat"), lax.axis_size("lon")
    n = nlat * nlon
    count = block_owner.shape[0]
    per = count // n
    side = lax.axis_index("comp")
    fields = fields[0]
    local = (block_owner % count).reshape(nlat, nlon, per)
    idb = jnp.broadcast_to(local.reshape(n, per, 1), (n, per, BX))
    ids = jnp.concatenate([local, jnp.roll(local, 1, 1), jnp.roll(local, -1, 1)], 2).reshape(n, 3 * per)
    split = fields.reshape(7, n, per, 2 * BX)
    raw = lax.ppermute(split, "comp", [(0, 1)])
    pay = pack(raw, idb, nlat, nlon)
    active, ends = ice_ends(fields, ice_covered.reshape(count, 1), land_mask)

    def exchange(pay, ids, active, ends):
        recv = lax.all_to_all(pay, ("lat", "lon"), split_axis=0, concat_axis=0, tiled=True)
        owner = lax.all_to_all(ids, ("lat", "lon"), split_axis=0, concat_axis=0, tiled=True)
        ring = [(i, (i + 1) % nlon) for i in range(nlon)]
        west = lax.ppermute(ends, "lon", ring)
        east = lax.ppermute(ends, "lon", [(j, i) for i, j in ring])
        sides, north, south = ice_rows(fields, active, west, east)
        line = [(i, i + 1) for i in range(nlat - 1)]
        below = lax.ppermute(north, "lat", line)
        above = lax.ppermute(south, "lat", [(j, i) for i, j in line])
        return recv, owner, sides, below, above

    def stay(pay, ids, active, ends):
        row = jnp.zeros((34, BX), jnp.float32)
        return pay, ids, ends, row, row

    recv, owner, sides, below, above = lax.cond(side == 1, exchange, stay, pay, ids, active, ends)
    back, moved = ice_step(owner, recv, fields, active, sides, below, above)

    def send(back):
        return lax.all_to_all(back, ("lat", "lon"), split_axis=0, concat_axis=0, tiled=True)

    back = lax.cond(side == 1, send, lambda x: x, back)
    got = lax.ppermute(back, "comp", [(1, 0)])
    out = final(side.reshape(1), got, split, moved.reshape(2, n, per, 2 * BX))
    return out.reshape(1, 2, count, 2 * BX)


def solution(mesh):
    placed = (
        P("comp", None, ("lat", "lon"), None),
        P(("lat", "lon")),
        P(("lat", "lon")),
        P(("lat", "lon"), None),
    )
    return jax.shard_map(
        per_device,
        mesh=mesh,
        in_specs=placed,
        out_specs=P("comp", None, ("lat", "lon"), None),
        check_vma=False,
    )
```

time: 126 us -> 72.5 us (0.58)
  local copies, waits for them, and re-layouts: 39.3 us -> 4.53 us
  waiting for transfers between devices: 22.1 us -> 46.6 us
  starting transfers between devices: 28.1 us -> 3.72 us
  other arithmetic: 18.5 us -> 0.76 us
  blocking collectives: 16.7 us -> 0 us
  Pallas kernels: 0 us -> 16.3 us
    ppermute x6 -> x2, waiting for transfers between devices: 4.7 us -> 46.6 us  [the longest x1 46.6 us: per_device(): got = lax.ppermute(back, 'comp', [(1, 0)])]
    all_to_all x2 -> x0, waiting for transfers between devices: 17.4 us -> none  [the longest x1 17.4 us: per_device(): lax.all_to_all(crossed, ('lat', 'lon'), split_axis=1, concat_axis=1, tile...]
    all_to_all x1 -> x0, blocking collectives: 16.7 us -> none  [per_device(): lax.all_to_all(back_send, ('lat', 'lon'), split_axis=1, concat_axis=1, ti...]
    pallas_call x0 -> x4, Pallas kernels: none -> 16.3 us  [the longest x1 8.34 us: ice_step(): pl.pallas_call(functools.partial(ice_kernel, n, per, count), out_shape=[f...]
    all_to_all x2 -> x0, starting transfers between devices: 14.6 us -> none  [the longest x1 7.68 us: per_device(): lax.all_to_all(owner_row, ('lat', 'lon'), split_axis=1, concat_axis=1, ti...]
    ppermute x6 -> x2, starting transfers between devices: 13.5 us -> 3.72 us  [the longest x1 2.44 us: per_device(): raw = lax.ppermute(split, 'comp', [(0, 1)])]
    slice x18 -> x2, local copies, waits for them, and re-layouts: 9.03 us -> 0.01 us  [per_device(): jnp.roll(local, 1, 1)]
    squeeze x18 -> x0, local copies, waits for them, and re-layouts: 8.42 us -> none  [the longest x4 3.99 us: prepare(): push_x = active * (concentration * forcing[0] - ice_mass * forcing[4])]
  transfers between devices with their start and end apart: 8 -> 2, of which waited for: 3 -> 1; matrix products, arithmetic and copies ran while one was open for 18% -> 3% of each run, Pallas kernels for 0% -> 2%
where the time goes in v1:
time: 72.5 us; the launch traced here: 72 us
  waiting for transfers between devices  46.6 us (64%)
  Pallas kernels  16.3 us (22%)
  local copies, waits for them, and re-layouts  4.53 us (6%)
  starting transfers between devices  3.72 us (5%)
  other arithmetic  0.76 us (1%)
    ppermute x1, waiting for transfers between devices, per_device(): got = lax.ppermute(back, 'comp', [(1, 0)])  46.6 us
    pallas_call x1, Pallas kernels, ice_step(): pl.pallas_call(functools.partial(ice_kernel, n, per, count), out_shape=[f...  8.34 us
    pallas_call x1, Pallas kernels, pack(): pl.pallas_call(functools.partial(pack_kernel, nlat, nlon, per, n * per),...  4.24 us
    ppermute x1, starting transfers between devices, per_device(): raw = lax.ppermute(split, 'comp', [(0, 1)])  2.44 us
    pallas_call x1, Pallas kernels, final(): pl.pallas_call(functools.partial(final_kernel, n, per), out_shape=f32(2,...  2.14 us
    pallas_call x1, Pallas kernels, ice_ends(): pl.pallas_call(ends_kernel, out_shape=[f32(count, 2 * BX), f32(count, BX)...  1.59 us
  transfers between devices with their start and end apart: 2, of which 1 were waited for; matrix products, arithmetic and copies ran while one was open for 3% of the time, Pallas kernels for 2%

profile of v1, /device:TPU:0, one launch (start us, length us, event | category | flops | bytes accessed | tf_op | source)
XLA Modules:
  0.0 72.0 jit_solution(12954511911959195149)
XLA Ops:
  0.0 2.4 %collective-permute-start.4 = (f32[7,16,8,256]{3,2,1,0:T(8,128)}, f32[7,16,8,256]{3,2,1,0:T(8,128)S(1)}, u32[]{:S(2)}, u32[]{:S(2)}) collective-permute-start(f32[7,16,8,256]{3,2,1,0:T(8,128)} %bitcast.10), channel_id=1, source_target_pairs={{0,16},{1,17},{2,18},{3,19},{4,20},{5,21},{6,22},{7,23},{8,24},{9,... | collective-permute-start | bytes 2752520 | tf_op jit(solution)/shard_map/ppermute | solution.py:409
  2.5 0.7 and_select_fusion
  3.1 0.1 reshape.24
  3.2 0.1 broadcast_in_dim.7
  3.3 1.4 %copy.7.covered = s32[128,1]{1,0:T(8,128)} copy(s32[128,1]{0,1:T(1,128)} %bitcast.20) | data formatting | bytes 1024 | tf_op jit(solution)/shard_map/reshape | solution.py:411
  4.7 1.6 %ice_ends.1 = (f32[128,256]{1,0:T(8,128)S(1)}, f32[128,128]{1,0:T(8,128)S(1)}) custom-call(f32[7,128,256]{2,1,0:T(8,128)} %bitcast.11, s32[128,1]{1,0:T(8,128)} %copy.7.covered, s32[128,256]{1,0:T(8,128)} %land.1), custom_call_target="tpu_custom_call" | custom-call | tf_op jit(solution)/shard_map/ice_ends/pallas_call | solution.py:129
  6.3 0.0 copy-start
  6.4 0.1 pad_add_fusion.2
  6.4 0.0 collective-permute-done.4.raw
  6.4 0.0 copy-start.1
  6.4 0.7 broadcast_in_dim.8.idb
  7.2 0.2 copy-done.1
  7.4 4.2 %pack.1 = f32[16,144,128]{2,1,0:T(8,128)} custom-call(f32[7,16,8,256]{3,2,1,0:T(8,128)} %copy-done.1, s32[16,8,128]{2,1,0:T(8,128)} %broadcast_in_dim.8.idb), custom_call_target="tpu_custom_call" | custom-call | tf_op jit(solution)/shard_map/pack/pallas_call | solution.py:101
  11.6 0.0 copy-done
  11.6 1.2 %conditional.2 = (f32[16,144,128]{2,1,0:T(8,128)}, s32[16,24]{1,0:T(8,128)S(1)}, f32[128,128]{1,0:T(8,128)S(1)}, f32[34,128]{1,0:T(8,128)}, f32[34,128]{1,0:T(8,128)}) conditional(s32[]{:T(128)} %convert_element_type.4, (f32[16,144,128]{2,1,0:T(8,128)}, s32[16,24]{1,0:T(8,128)S(1)}, f32[128,128]{1,0:T(8,128)S(1)}) %tuple.19, ...), branch_computations={%region_0.1_spmd, %region_1.2_spmd} | conditional | bytes 7092512 | solution.py:429
  11.6 0.6 broadcast.7.clone
  12.2 0.6 broadcast.7
  12.9 8.3 %ice_step.1 = (f32[16,48,128]{2,1,0:T(8,128)S(1)}, f32[2,128,256]{2,1,0:T(8,128)}) custom-call(s32[16,24]{1,0:T(8,128)S(1)} %get-tuple-element.48.ids, f32[16,144,128]{2,1,0:T(8,128)} %get-tuple-element.49.recv, f32[7,128,256]{2,1,0:T(8,128)S(1)} %bitcast.13, f32[128,256]{1,0:T(8,128)S(1)} %get-tuple-element.47.active, ...), custom_call_target="tpu_custom_call" | custom-call | tf_op jit(solution)/shard_map/ice_step/pallas_call | solution.py:354
  21.2 1.3 %collective-permute-start.5 = (f32[16,48,128]{2,1,0:T(8,128)S(1)}, f32[16,48,128]{2,1,0:T(8,128)S(1)}, u32[]{:S(2)}, u32[]{:S(2)}) collective-permute-start(f32[16,48,128]{2,1,0:T(8,128)S(1)} %get-tuple-element.71), channel_id=1, source_target_pairs={{16,0},{17,1},{18,2},{19,3},{20,4},{21,5},{22,6},{23,7},{24,8},{25... | collective-permute-start | bytes 1179656 | tf_op jit(solution)/shard_map/ppermute | solution.py:436
  22.5 46.6 %collective-permute-done.5.got = f32[16,48,128]{2,1,0:T(8,128)S(1)} collective-permute-done((f32[16,48,128]{2,1,0:T(8,128)S(1)}, f32[16,48,128]{2,1,0:T(8,128)S(1)}, u32[]{:S(2)}, u32[]{:S(2)}) %collective-permute-start.5) | collective-permute-done | bytes 393248 | tf_op jit(solution)/shard_map/ppermute | solution.py:436
  69.1 0.0 copy-start.2
  69.1 0.8 %copy-done.2 = f32[16,48,128]{2,1,0:T(8,128)} copy-done((f32[16,48,128]{2,1,0:T(8,128)}, f32[16,48,128]{2,1,0:T(8,128)S(1)}, u32[]{:S(2)}) %copy-start.2) | copy-done | bytes 393240
  69.9 2.1 %final.1 = f32[2,16,8,256]{3,2,1,0:T(8,128)} custom-call(s32[1]{0:T(128)} %bitcast.2.flag, f32[16,48,128]{2,1,0:T(8,128)} %copy-done.2, f32[7,16,8,256]{3,2,1,0:T(8,128)S(1)} %bitcast.14, f32[2,16,8,256]{3,2,1,0:T(8,128)} %bitcast.15), custom_call_target="tpu_custom_call" | custom-call | tf_op jit(solution)/shard_map/final/pallas_call | solution.py:389
  (4 shorter events, 0.0 us)
Async XLA Ops:
  0.0 6.4 %collective-permute-start.4 = (f32[7,16,8,256]{3,2,1,0:T(8,128)}, f32[7,16,8,256]{3,2,1,0:T(8,128)S(1)}, u32[]{:S(2)}, u32[]{:S(2)}) collective-permute-start(f32[7,16,8,256]{3,2,1,0:T(8,128)} %bitcast.10), channel_id=1, source_target_pairs={{0,16},{1,17},{2,18},{3,19},{4,20},{5,21},{6,22},{7,23},{8,24},{9,... | collective-permute-start | bytes 2752520 | tf_op jit(solution)/shard_map/ppermute | solution.py:409
  6.3 5.3 %copy-start = (f32[1,7,128,256]{3,2,1,0:T(8,128)S(1)}, f32[1,7,128,256]{3,2,1,0:T(8,128)}, u32[]{:S(2)}) copy-start(f32[1,7,128,256]{3,2,1,0:T(8,128)} %param.8) | copy-start | bytes 2752516
  6.4 1.0 %copy-start.1 = (f32[7,16,8,256]{3,2,1,0:T(8,128)}, f32[7,16,8,256]{3,2,1,0:T(8,128)S(1)}, u32[]{:S(2)}) copy-start(f32[7,16,8,256]{3,2,1,0:T(8,128)S(1)} %collective-permute-done.4.raw) | copy-start | bytes 2752516
  21.2 47.9 %collective-permute-start.5 = (f32[16,48,128]{2,1,0:T(8,128)S(1)}, f32[16,48,128]{2,1,0:T(8,128)S(1)}, u32[]{:S(2)}, u32[]{:S(2)}) collective-permute-start(f32[16,48,128]{2,1,0:T(8,128)S(1)} %get-tuple-element.71), channel_id=1, source_target_pairs={{16,0},{17,1},{18,2},{19,3},{20,4},{21,5},{22,6},{23,7},{24,8},{25... | collective-permute-start | bytes 1179656 | tf_op jit(solution)/shard_map/ppermute | solution.py:436
  69.1 0.8 %copy-start.2 = (f32[16,48,128]{2,1,0:T(8,128)}, f32[16,48,128]{2,1,0:T(8,128)S(1)}, u32[]{:S(2)}) copy-start(f32[16,48,128]{2,1,0:T(8,128)S(1)} %collective-permute-done.5.got) | copy-start | bytes 1179652

commit v2 on v1

--- a/solution.py
+++ b/solution.py
@@ -22,6 +22,10 @@
 SMEM = pl.BlockSpec(memory_space=pltpu.SMEM)
 
 
+def params(mib):
+    return pltpu.CompilerParams(vmem_limit_bytes=mib * 1024 * 1024)
+
+
 def f32(*shape):
     return jax.ShapeDtypeStruct(shape, jnp.float32)
 
@@ -38,7 +42,7 @@
     return jnp.where(q, west, east)
 
 
-def pack_kernel(nlat, nlon, per, count, raw, idb, pay, edge, rim):
+def pack_body(nlat, nlon, per, count, raw, idb, pay, opened, edge, rim):
     n = nlat * nlon
     lane = lanes(per)
     group = lane // 8
@@ -56,6 +60,11 @@
             planes[2 + y] = scale * wy
             for ch in range(2, 6):
                 planes[2 * ch + y] = half(ch, y)
+            rx, ry = wx - planes[4 + y], wy - planes[6 + y]
+            speed = jnp.sqrt(rx * rx + ry * ry + 1.0)
+            rate = rho * (0.1 + 0.05 * speed) * speed
+            opened[t, 2 * y] = rate * rx
+            opened[t, 2 * y + 1] = rate * ry
         ends = jnp.zeros((per, BX), jnp.float32)
         for p in range(12):
             pay[t, pl.ds(p, per, stride=12), :] = planes[p]
@@ -95,20 +104,7 @@
     lax.fori_loop(0, n, dest, 0)
 
 
-def pack(raw, idb, nlat, nlon):
-    _, n, per, _ = raw.shape
-    rows = 13 * per + 40
-    return pl.pallas_call(
-        functools.partial(pack_kernel, nlat, nlon, per, n * per),
-        out_shape=f32(n, rows, BX),
-        in_specs=[VMEM, VMEM],
-        out_specs=VMEM,
-        scratch_shapes=[pltpu.VMEM((n, per, BX), jnp.float32), pltpu.VMEM((n, 40, BX), jnp.float32)],
-        name="pack",
-    )(raw, idb)
-
-
-def ends_kernel(ice, covered, land, active, ends):
+def ends_body(ice, covered, land, active, ends):
     count = covered.shape[0]
     lane = lanes(count)
     group = lane // 8
@@ -118,21 +114,34 @@
         act = covered[...].astype(jnp.float32) * (1 - land[:, cells]).astype(jnp.float32)
         active[:, cells] = act
         for ch in range(8):
-            x = act if ch == 7 else ice[ch, :, cells]
+            x = act if ch == 7 else ice[ch, :, :, cells].reshape(count, BX)
             p = 2 * ch + y
             total = jnp.where(group == p, roll(x, 8 * p + 4), total)
     ends[...] = total
 
 
-def ice_ends(ice, covered, land):
-    count = covered.shape[0]
+def first_kernel(nlat, nlon, per, flag, raw, idb, covered, land, pay, opened, active, ends, edge, rim):
+    @pl.when(flag[0] == 0)
+    def _():
+        pack_body(nlat, nlon, per, nlat * nlon * per, raw, idb, pay, opened, edge, rim)
+
+    @pl.when(flag[0] != 0)
+    def _():
+        ends_body(raw, covered, land, active, ends)
+
+
+def first(flag, raw, idb, covered, land, nlat, nlon):
+    _, n, per, _ = raw.shape
+    count = n * per
     return pl.pallas_call(
-        ends_kernel,
-        out_shape=[f32(count, 2 * BX), f32(count, BX)],
-        in_specs=[VMEM] * 3,
-        out_specs=[VMEM] * 2,
-        name="ice_ends",
-    )(ice, covered, land)
+        functools.partial(first_kernel, nlat, nlon, per),
+        out_shape=[f32(n, 13 * per + 40, BX), f32(n, 4, per, BX), f32(count, 2 * BX), f32(count, BX)],
+        in_specs=[SMEM] + [VMEM] * 4,
+        out_specs=[VMEM] * 4,
+        scratch_shapes=[pltpu.VMEM((n, per, BX), jnp.float32), pltpu.VMEM((n, 40, BX), jnp.float32)],
+        compiler_params=params(12),
+        name="first",
+    )(flag, raw, idb, covered, land)
 
 
 def rows_kernel(ice, active, west, east, sides, north, south):
@@ -156,6 +165,7 @@
         out_shape=[f32(count, BX), f32(34, BX), f32(34, BX)],
         in_specs=[VMEM] * 4,
         out_specs=[VMEM] * 3,
+        compiler_params=params(8),
         name="ice_rows",
     )(ice, active, west, east)
 
@@ -170,8 +180,50 @@
     return jnp.where(start, b, a), jnp.where(start, a, b)
 
 
-def ice_kernel(n, per, count, ids, recv, ice, active, sides, below, above, back, moved,
-               spot, hw, he, grid, state, fixed, cross, out8):
+def prep_kernel(count, height, ice, active, sides, below, above, begin, still, grid):
+    for ch in range(8):
+        for y in range(2):
+            p = 2 * ch + y
+            cells = slice(y * BX, (y + 1) * BX)
+            shift = -(8 * p + 4)
+            grid[ch, y, 0, 2 : 2 + count, :] = active[:, cells] if ch == 7 else ice[ch, :, cells]
+            grid[ch, y, 1, 2 : 2 + count, :] = roll(sides[...], shift)
+            for lo, msg in ((0, below), (count + 2, above)):
+                grid[ch, y, 0, lo : lo + 2, :] = msg[2 * p : 2 * p + 2, :]
+                grid[ch, y, 1, lo : lo + 2, :] = roll(msg[32:34, :], shift)
+            grid[ch, y, 0, count + 4 :, :] = jnp.zeros((height - count - 4, BX), jnp.float32)
+            grid[ch, y, 1, count + 4 :, :] = jnp.zeros((height - count - 4, BX), jnp.float32)
+
+    for r in range(height // 8):
+        at = slice(8 * r, 8 * r + 8)
+        for y in range(2):
+            for w in range(2):
+                u, v, mass, conc, s1, s2, s12, act = [grid[ch, y, w, at, :] for ch in range(8)]
+                for k, x in enumerate((u, v, s1, s2, s12)):
+                    begin[k, y, w, at, :] = x
+                still[0, y, w, at, :] = mass * jnp.exp(CSTAR * (conc - 1.0)) * act * (1.0 / 3.0)
+                still[1, y, w, at, :] = mass
+                still[2, y, w, at, :] = CW * conc * act
+                still[3, y, w, at, :] = act
+                still[4, y, w, at, :] = conc
+
+
+def prep(ice, active, sides, below, above):
+    count = active.shape[0]
+    height = (count + 4 + 7) // 8 * 8
+    return pl.pallas_call(
+        functools.partial(prep_kernel, count, height),
+        out_shape=[f32(5, 2, 2, height, BX)] * 2,
+        in_specs=[VMEM] * 5,
+        out_specs=[VMEM] * 2,
+        scratch_shapes=[pltpu.VMEM((8, 2, 2, height, BX), jnp.float32)],
+        compiler_params=params(12),
+        name="prep",
+    )(ice, active, sides, below, above)
+
+
+def ice_kernel(n, per, count, ids, recv, begin, still, back, moved,
+               spot, hw, he, state, forced, cross, out8):
     tiles = (count + 4 + 7) // 8
     height = tiles * 8
     blank = jnp.zeros((8, BX), jnp.float32)
@@ -211,19 +263,6 @@
         ref[0:1, :] = rim[39:40]
 
     q = (lanes(8) % 8) < 4
-    for ch in range(8):
-        for y in range(2):
-            p = 2 * ch + y
-            cells = slice(y * BX, (y + 1) * BX)
-            shift = -(8 * p + 4)
-            grid[ch, y, 0, 2 : 2 + count, :] = active[:, cells] if ch == 7 else ice[ch, :, cells]
-            grid[ch, y, 1, 2 : 2 + count, :] = roll(sides[...], shift)
-            for lo, msg in ((0, below), (count + 2, above)):
-                grid[ch, y, 0, lo : lo + 2, :] = msg[2 * p : 2 * p + 2, :]
-                grid[ch, y, 1, lo : lo + 2, :] = roll(msg[32:34, :], shift)
-            grid[ch, y, 0, count + 4 :, :] = jnp.zeros((height - count - 4, BX), jnp.float32)
-            grid[ch, y, 1, count + 4 :, :] = jnp.zeros((height - count - 4, BX), jnp.float32)
-
     for r in range(tiles):
         at = slice(8 * r, 8 * r + 8)
         to = slice(FRONT + 8 * r, FRONT + 8 * r + 8)
@@ -234,20 +273,13 @@
                     f = [spot[pl.ds(8 * r * STEP + 2 * ch + y, 8, stride=STEP), :] for ch in range(6)]
                 else:
                     f = [roll(ends, -(8 * (2 * ch + y) + 4)) for ch in range(6)]
-                u, v, mass, conc, s1, s2, s12, act = [grid[ch, y, w, at, :] for ch in range(8)]
-                state[0, y, w, to, :] = u
-                state[1, y, w, to, :] = v
-                state[2, y, w, to, :] = s1
-                state[3, y, w, to, :] = s2
-                state[4, y, w, to, :] = s12
-                fixed[0, y, w, at, :] = mass * jnp.exp(CSTAR * (conc - 1.0)) * act * (1.0 / 3.0)
-                fixed[1, y, w, at, :] = mass
-                fixed[2, y, w, at, :] = CW * conc * act
-                fixed[3, y, w, at, :] = act * (conc * f[0] - mass * f[4])
-                fixed[4, y, w, at, :] = act * (conc * f[1] - mass * f[5])
-                fixed[5, y, w, at, :] = f[2]
-                fixed[6, y, w, at, :] = f[3]
-                fixed[7, y, w, at, :] = act
+                for k in range(5):
+                    state[k, y, w, to, :] = begin[k, y, w, at, :]
+                mass, act, conc = [still[k, y, w, at, :] for k in (1, 3, 4)]
+                forced[0, y, w, at, :] = act * (conc * f[0] - mass * f[4])
+                forced[1, y, w, at, :] = act * (conc * f[1] - mass * f[5])
+                forced[2, y, w, at, :] = f[2]
+                forced[3, y, w, at, :] = f[3]
 
     tail = FRONT + height
     for k in range(2):
@@ -283,7 +315,7 @@
                     div, ten = sxx + syy, sxx - syy
                     x = div * div + ((ten * ten + shear * shear) * 0.25 + 0.25)
                     inv = lax.rsqrt(x)
-                    kr = fixed[0, y, w, at, :] * inv
+                    kr = still[0, y, w, at, :] * inv
                     t1 = state[2, y, w, to, :] * (2.0 / 3.0) + kr * (div - x * inv)
                     t2 = state[3, y, w, to, :] * (2.0 / 3.0) + kr * (ten * 0.25)
                     t3 = state[4, y, w, to, :] * (2.0 / 3.0) + kr * (shear * 0.125)
@@ -306,15 +338,16 @@
                         s12s, cs = state[4, 1, w, down1, :], cross[w, down1, :]
                     fx = (a[k] - aw[w]) + (s12[k] - s12s)
                     fy = (s12[k] - sw[w]) + (c[k] - cs)
-                    mass, base = fixed[1, y, w, at, :], fixed[2, y, w, at, :]
-                    cx, cy = fixed[5, y, w, at, :], fixed[6, y, w, at, :]
+                    mass, base = still[1, y, w, at, :], still[2, y, w, at, :]
+                    cx, cy = forced[2, y, w, at, :], forced[3, y, w, at, :]
                     dx, dy = cx - u[k], cy - v[k]
-                    drag = base * jnp.sqrt(dx * dx + dy * dy + DRAG_FLOOR)
+                    y2 = dx * dx + dy * dy + DRAG_FLOOR
+                    drag = base * (y2 * lax.rsqrt(y2))
                     m2 = mass * 2.0
-                    part = fixed[7, y, w, at, :] / (jnp.maximum(m2, 1.0) + drag)
+                    part = still[3, y, w, at, :] / (jnp.maximum(m2, 1.0) + drag)
                     mc = CORIO * mass
-                    state[0, y, w, to, :] = part * (m2 * u[k] + fx + fixed[3, y, w, at, :] + drag * cx + mc * v[k])
-                    state[1, y, w, to, :] = part * (m2 * v[k] + fy + fixed[4, y, w, at, :] + drag * cy - mc * u[k])
+                    state[0, y, w, to, :] = part * (m2 * u[k] + fx + forced[0, y, w, at, :] + drag * cx + mc * v[k])
+                    state[1, y, w, to, :] = part * (m2 * v[k] + fy + forced[1, y, w, at, :] + drag * cy - mc * u[k])
         return carry
 
     lax.fori_loop(0, NSUB, subcycle, 0)
@@ -323,9 +356,9 @@
         at = slice(8 * r, 8 * r + 8)
         to = slice(FRONT + 8 * r, FRONT + 8 * r + 8)
         for y in range(2):
-            base = fixed[2, y, 0, at, :]
-            dx = state[0, y, 0, to, :] - fixed[5, y, 0, at, :]
-            dy = state[1, y, 0, to, :] - fixed[6, y, 0, at, :]
+            base = still[2, y, 0, at, :]
+            dx = state[0, y, 0, to, :] - forced[2, y, 0, at, :]
+            dy = state[1, y, 0, to, :] - forced[3, y, 0, at, :]
             factor = base * jnp.sqrt(dx * dx + dy * dy + DRAG_FLOOR)
             for k, x in enumerate((factor * dx, factor * dy, base * (1.0 / CW))):
                 out8[pl.ds(64 * r + 2 * k + y, 8, stride=8), :] = x
@@ -342,39 +375,35 @@
     lax.fori_loop(0, n, answer, 0)
 
 
-def ice_step(ids, recv, ice, active, sides, below, above):
+def ice_step(ids, recv, begin, still):
     n, per = ids.shape[0], ids.shape[1] // 3
     count = n * per
     height = (count + 4 + 7) // 8 * 8
     tall = height + 2 * FRONT
     scratch = [
-        (height * STEP, BX), (height, BX), (height, BX), (8, 2, 2, height, BX),
-        (5, 2, 2, tall, BX), (8, 2, 2, height, BX), (2, tall, BX), (height * 8, BX),
+        (height * STEP, BX), (height, BX), (height, BX),
+        (5, 2, 2, tall, BX), (4, 2, 2, height, BX), (2, tall, BX), (height * 8, BX),
     ]
     return pl.pallas_call(
         functools.partial(ice_kernel, n, per, count),
         out_shape=[f32(n, 6 * per, BX), f32(2, count, 2 * BX)],
-        in_specs=[SMEM] + [VMEM] * 6,
+        in_specs=[SMEM] + [VMEM] * 3,
         out_specs=[VMEM] * 2,
         scratch_shapes=[pltpu.VMEM(s, jnp.float32) for s in scratch],
+        compiler_params=params(12),
         name="ice_step",
-    )(ids, recv, ice, active, sides, below, above)
-
-
-def final_kernel(n, per, flag, got, raw, moved, out):
+    )(ids, recv, begin, still)
+
+
+def final_kernel(n, per, flag, got, opened, moved, out):
     @pl.when(flag[0] == 0)
     def _():
         def tile(t, _):
             for y in range(2):
                 cells = slice(y * BX, (y + 1) * BX)
-                wx, wy, cx, cy, rho = [raw[ch, t, :, cells] for ch in (0, 1, 2, 3, 6)]
-                rx, ry = wx - cx, wy - cy
-                speed = jnp.sqrt(rx * rx + ry * ry + 1.0)
-                scale = rho * (0.1 + 0.05 * speed) * speed
                 gx, gy, gc = [got[t, pl.ds(2 * k + y, per, stride=6), :] for k in range(3)]
-                rest = (1.0 - gc) * scale
-                out[0, t, :, cells] = gx + rest * rx
-                out[1, t, :, cells] = gy + rest * ry
+                out[0, t, :, cells] = gx + (1.0 - gc) * opened[t, 2 * y]
+                out[1, t, :, cells] = gy + (1.0 - gc) * opened[t, 2 * y + 1]
             return 0
 
         lax.fori_loop(0, n, tile, 0)
@@ -384,15 +413,16 @@
         out[...] = moved[...]
 
 
-def final(flag, got, raw, moved):
-    _, n, per, cells = raw.shape
+def final(flag, got, opened, moved):
+    n, _, per, _ = opened.shape
     return pl.pallas_call(
         functools.partial(final_kernel, n, per),
-        out_shape=f32(2, n, per, cells),
+        out_shape=f32(2, n, per, 2 * BX),
         in_specs=[SMEM] + [VMEM] * 3,
         out_specs=VMEM,
+        compiler_params=params(8),
         name="final",
-    )(flag, got, raw, moved)
+    )(flag, got, opened, moved)
 
 
 def per_device(fields, block_owner, ice_covered, land_mask):
@@ -401,40 +431,42 @@
     count = block_owner.shape[0]
     per = count // n
     side = lax.axis_index("comp")
+    flag = side.reshape(1)
     fields = fields[0]
     local = (block_owner % count).reshape(nlat, nlon, per)
     idb = jnp.broadcast_to(local.reshape(n, per, 1), (n, per, BX))
     ids = jnp.concatenate([local, jnp.roll(local, 1, 1), jnp.roll(local, -1, 1)], 2).reshape(n, 3 * per)
     split = fields.reshape(7, n, per, 2 * BX)
-    raw = lax.ppermute(split, "comp", [(0, 1)])
-    pay = pack(raw, idb, nlat, nlon)
-    active, ends = ice_ends(fields, ice_covered.reshape(count, 1), land_mask)
-
-    def exchange(pay, ids, active, ends):
-        recv = lax.all_to_all(pay, ("lat", "lon"), split_axis=0, concat_axis=0, tiled=True)
-        owner = lax.all_to_all(ids, ("lat", "lon"), split_axis=0, concat_axis=0, tiled=True)
-        ring = [(i, (i + 1) % nlon) for i in range(nlon)]
-        west = lax.ppermute(ends, "lon", ring)
-        east = lax.ppermute(ends, "lon", [(j, i) for i, j in ring])
+    pay, opened, active, ends = first(flag, split, idb, ice_covered.reshape(count, 1), land_mask, nlat, nlon)
+    pay = lax.ppermute(pay, "comp", [(0, 1)])
+    every = ("comp", "lat", "lon")
+    tiles = [(i, j) for i in range(nlat) for j in range(nlon)]
+    east_pairs = [(n + i * nlon + j, n + i * nlon + (j + 1) % nlon) for i, j in tiles]
+    west = lax.ppermute(ends, every, east_pairs)
+    east = lax.ppermute(ends, every, [(j, i) for i, j in east_pairs])
+
+    def everyone(x):
+        return lax.all_to_all(x, ("lat", "lon"), split_axis=0, concat_axis=0, tiled=True)
+
+    def ice_side(pay, ids, active, west, east):
+        recv = everyone(pay)
         sides, north, south = ice_rows(fields, active, west, east)
         line = [(i, i + 1) for i in range(nlat - 1)]
         below = lax.ppermute(north, "lat", line)
         above = lax.ppermute(south, "lat", [(j, i) for i, j in line])
-        return recv, owner, sides, below, above
-
-    def stay(pay, ids, active, ends):
+        return recv, ids, sides, below, above
+
+    def ocean_side(pay, ids, active, west, east):
         row = jnp.zeros((34, BX), jnp.float32)
-        return pay, ids, ends, row, row
-
-    recv, owner, sides, below, above = lax.cond(side == 1, exchange, stay, pay, ids, active, ends)
-    back, moved = ice_step(owner, recv, fields, active, sides, below, above)
-
-    def send(back):
-        return lax.all_to_all(back, ("lat", "lon"), split_axis=0, concat_axis=0, tiled=True)
-
-    back = lax.cond(side == 1, send, lambda x: x, back)
+        return jnp.zeros(pay.shape, jnp.float32), everyone(ids), jnp.zeros(west.shape, jnp.float32), row, row
+
+    recv, owner, sides, below, above = lax.cond(side == 1, ice_side, ocean_side, pay, ids, active, west, east)
+    swap = lax.ppermute(owner, "comp", [(0, 1), (1, 0)])
+    begin, still = prep(fields, active, sides, below, above)
+    back, moved = ice_step(swap, recv, begin, still)
+    back = lax.cond(side == 1, everyone, lambda x: x, back)
     got = lax.ppermute(back, "comp", [(1, 0)])
-    out = final(side.reshape(1), got, split, moved.reshape(2, n, per, 2 * BX))
+    out = final(flag, got, opened, moved.reshape(2, n, per, 2 * BX))
     return out.reshape(1, 2, count, 2 * BX)
 
 

time: 72.5 us -> 63.1 us (0.87)
  waiting for transfers between devices: 46.6 us -> 14.6 us
  blocking collectives: 0 us -> 15.6 us
  starting transfers between devices: 3.72 us -> 14.9 us
  Pallas kernels: 16.3 us -> 12.5 us
    ppermute x1, waiting for transfers between devices: 46.6 us -> 14.6 us  [per_device(): got = lax.ppermute(back, 'comp', [(1, 0)])]
    all_to_all x0 -> x1, blocking collectives: none -> 15.6 us  [everyone(): lax.all_to_all(x, ('lat', 'lon'), split_axis=0, concat_axis=0, tiled=True)]
    ppermute x1 -> x4, starting transfers between devices: 2.44 us -> 13.6 us  [the longest x1 9.9 us: per_device(): swap = lax.ppermute(owner, 'comp', [(0, 1), (1, 0)])]
    pallas_call x1, Pallas kernels: 2.14 us -> 0.81 us  [final(): pl.pallas_call(functools.partial(final_kernel, n, per), out_shape=f32(2,...]
    pallas_call x1, Pallas kernels: 8.34 us -> 7.06 us  [ice_step(): pl.pallas_call(functools.partial(ice_kernel, n, per, count), out_shape=[f...]
    pallas_call x2, Pallas kernels: 5.82 us -> 4.61 us  [the longest x1 3.27 us: first(): pl.pallas_call(functools.partial(first_kernel, nlat, nlon, per), out_shap...]
    another operation x2 -> x4, local copies, waits for them, and re-layouts: 1.23 us -> 2.28 us
  transfers between devices with their start and end apart: 2 -> 5, of which waited for: 1 -> 1; matrix products, arithmetic and copies ran while one was open for 3% -> 0% of each run, Pallas kernels for 2% -> 2%
where the time goes in v2:
time: 63.1 us; the launch traced here: 62.6 us
  blocking collectives  15.6 us (25%)
  starting transfers between devices  14.9 us (24%)
  waiting for transfers between devices  14.6 us (23%)
  Pallas kernels  12.5 us (20%)
  local copies, waits for them, and re-layouts  4.22 us (7%)
  other arithmetic  0.75 us (1%)
    all_to_all x1, blocking collectives, everyone(): lax.all_to_all(x, ('lat', 'lon'), split_axis=0, concat_axis=0, tiled=True)  15.6 us
    ppermute x1, waiting for transfers between devices, per_device(): got = lax.ppermute(back, 'comp', [(1, 0)])  14.6 us
    ppermute x1, starting transfers between devices, per_device(): swap = lax.ppermute(owner, 'comp', [(0, 1), (1, 0)])  9.9 us
    pallas_call x1, Pallas kernels, ice_step(): pl.pallas_call(functools.partial(ice_kernel, n, per, count), out_shape=[f...  7.06 us
    pallas_call x1, Pallas kernels, first(): pl.pallas_call(functools.partial(first_kernel, nlat, nlon, per), out_shap...  3.27 us
    ppermute x1, starting transfers between devices, per_device(): pay = lax.ppermute(pay, 'comp', [(0, 1)])  2.35 us
    another operation x4, local copies, waits for them, and re-layouts  2.28 us
    pallas_call x1, Pallas kernels, prep(): pl.pallas_call(functools.partial(prep_kernel, count, height), out_shape=[...  1.34 us
  transfers between devices with their start and end apart: 5, of which 1 were waited for; matrix products, arithmetic and copies ran while one was open for 0% of the time, Pallas kernels for 2%

profile of v2, /device:TPU:0, one launch (start us, length us, event | category | flops | bytes accessed | tf_op | source)
XLA Modules:
  0.0 62.6 jit_solution(530850063632365520)
XLA Ops:
  0.0 0.7 %and_select_fusion = s32[128]{0:T(128)S(1)} fusion(s32[128]{0:T(128)} %param.9), kind=kLoop, calls=%fused_computation.5 | loop fusion | flops 1408 | bytes 1024 | tf_op jit(solution)/shard_map/jit(remainder)/select_n | solution.py:436
  0.7 0.1 concatenate.19
  0.7 0.8 %copy.7.covered = s32[128,1]{1,0:T(8,128)S(1)} copy(s32[128,1]{0,1:T(1,128)} %bitcast.18) | data formatting | bytes 1024 | tf_op jit(solution)/shard_map/reshape | solution.py:440
  1.5 0.1 broadcast_in_dim.2.idb
  1.6 0.0 copy-start
  1.6 0.9 %copy-done = s32[128,256]{1,0:T(8,128)S(1)} copy-done((s32[128,256]{1,0:T(8,128)S(1)}, s32[128,256]{1,0:T(8,128)}, u32[]{:S(2)}) %copy-start) | copy-done | bytes 131096
  2.5 0.0 copy-start.1
  2.5 3.3 %first.1 = (f32[16,144,128]{2,1,0:T(8,128)S(1)}, f32[16,4,8,128]{3,2,1,0:T(8,128)S(1)}, f32[128,256]{1,0:T(8,128)S(1)}, f32[128,128]{1,0:T(8,128)S(1)}) custom-call(s32[1]{0:T(128)} %bitcast.2.flag, f32[7,16,8,256]{3,2,1,0:T(8,128)} %bitcast.11, s32[16,8,128]{2,1,0:T(8,128)S(1)} %broadcast_in_dim.2.idb, s32[128,1]{1,0:T(8,128)S(1)} %copy.7.covered, ...), custom_call_target="tpu_custom_call" | custom-call | tf_op jit(solution)/shard_map/first/pallas_call | solution.py:136
  5.8 2.3 %collective-permute-start.2 = (f32[16,144,128]{2,1,0:T(8,128)S(1)}, f32[16,144,128]{2,1,0:T(8,128)}, u32[]{:S(2)}, u32[]{:S(2)}) collective-permute-start(f32[16,144,128]{2,1,0:T(8,128)S(1)} %get-tuple-element.45), channel_id=1, source_target_pairs={{0,16},{1,17},{2,18},{3,19},{4,20},{5,21},{6,22},{7,23},{8,24},{9,... | collective-permute-start | bytes 3538952 | tf_op jit(solution)/shard_map/ppermute | solution.py:441
  8.1 0.7 %collective-permute-start.4 = (f32[128,128]{1,0:T(8,128)S(1)}, f32[128,128]{1,0:T(8,128)S(1)}, u32[]{:S(2)}, u32[]{:S(2)}) collective-permute-start(f32[128,128]{1,0:T(8,128)S(1)} %get-tuple-element.47), channel_id=1, source_target_pairs={{17,16},{18,17},{19,18},{16,19},{21,20},{22,21},{23,22},{20,23},{2... | collective-permute-start | bytes 196616 | tf_op jit(solution)/shard_map/ppermute | solution.py:446
  8.8 0.7 %collective-permute-start.3 = (f32[128,128]{1,0:T(8,128)S(1)}, f32[128,128]{1,0:T(8,128)S(1)}, u32[]{:S(2)}, u32[]{:S(2)}) collective-permute-start(f32[128,128]{1,0:T(8,128)S(1)} %get-tuple-element.47), channel_id=1, source_target_pairs={{16,17},{17,18},{18,19},{19,16},{20,21},{21,22},{22,23},{23,20},{2... | collective-permute-start | bytes 196616 | tf_op jit(solution)/shard_map/ppermute | solution.py:445
  9.5 0.1 reshape.26
  9.6 0.1 pad_add_fusion.2
  9.7 0.0 collective-permute-done.4
  9.7 0.0 collective-permute-done.3
  9.7 0.0 collective-permute-done.2
  9.7 0.0 copy-done.1
  9.7 17.9 %conditional.2 = (f32[16,144,128]{2,1,0:T(8,128)}, s32[16,24]{1,0:T(8,128)S(1)}, f32[128,128]{1,0:T(8,128)S(1)}, f32[34,128]{1,0:T(8,128)}, f32[34,128]{1,0:T(8,128)}) conditional(s32[]{:T(128)} %convert_element_type.4, s32[16,24]{1,0:T(8,128)S(1)} %pad_add_fusion.2, (f32[16,144,128]{2,1,0:T(8,128)}, f32[7,128,256]{2,1,0:T(8,128)S(1)}, ...), branch_computations={%region_0.1_spmd, %region_1.2_spmd} | conditional | bytes 3681432 | solution.py:463
  9.7 15.6 %all_to_all.17 = s32[16,1,24]{2,1,0:T(1,128)S(1)} all-to-all(s32[16,1,24]{2,1,0:T(1,128)S(1)} %bitcast.14), channel_id=1, replica_groups=mesh['comp'=2,'lat'=4,'lon'=4] {'lat','lon'}, dimensions={0} | all-to-all | bytes 3072 | tf_op jit(solution)/shard_map/cond/branch_0_fun/all_to_all | solution.py:449
  25.3 0.6 broadcast.13.clone
  25.9 0.6 broadcast.13
  26.5 1.1 %broadcast.11 = f32[16,144,128]{2,1,0:T(8,128)} broadcast(f32[]{:T(128)} %constant.20.clone), dimensions={} | broadcast | bytes 1179652 | tf_op jit(solution)/shard_map/broadcast.7
  27.6 9.9 %collective-permute-start.5 = (s32[16,24]{1,0:T(8,128)S(1)}, s32[16,24]{1,0:T(8,128)S(1)}, u32[]{:S(2)}, u32[]{:S(2)}) collective-permute-start(s32[16,24]{1,0:T(8,128)S(1)} %get-tuple-element.48), channel_id=1, source_target_pairs={{0,16},{16,0},{1,17},{17,1},{2,18},{18,2},{3,19},{19,3},{4,20},{20... | collective-permute-start | bytes 4616 | tf_op jit(solution)/shard_map/ppermute | solution.py:464
  37.5 1.3 %prep.1 = (f32[5,2,2,136,128]{4,3,2,1,0:T(8,128)S(1)}, f32[5,2,2,136,128]{4,3,2,1,0:T(8,128)S(1)}) custom-call(f32[7,128,256]{2,1,0:T(8,128)S(1)} %bitcast.13, f32[128,256]{1,0:T(8,128)S(1)} %get-tuple-element.46.active, f32[128,128]{1,0:T(8,128)S(1)} %get-tuple-element.50.sides, f32[34,128]{1,0:T(8,128)} %get-tuple-element.51.below, ...), custom_call_target="tpu_custom_call" | custom-call | tf_op jit(solution)/shard_map/prep/pallas_call | solution.py:214
  38.8 0.0 collective-permute-done.5.ids
  38.8 7.1 %ice_step.1 = (f32[16,48,128]{2,1,0:T(8,128)S(1)}, f32[2,128,256]{2,1,0:T(8,128)S(1)}) custom-call(s32[16,24]{1,0:T(8,128)S(1)} %collective-permute-done.5.ids, f32[16,144,128]{2,1,0:T(8,128)} %get-tuple-element.49.recv, f32[5,2,2,136,128]{4,3,2,1,0:T(8,128)S(1)} %get-tuple-element.53.begin, f32[5,2,2,136,128]{4,3,2,1,0:T(8,128)S(1)} %get-tuple-element.54.still), custom_call_target="tpu_custom_call" | custom-call | tf_op jit(solution)/shard_map/ice_step/pallas_call | solution.py:387
  45.9 1.3 %collective-permute-start.6 = (f32[16,48,128]{2,1,0:T(8,128)S(1)}, f32[16,48,128]{2,1,0:T(8,128)S(1)}, u32[]{:S(2)}, u32[]{:S(2)}) collective-permute-start(f32[16,48,128]{2,1,0:T(8,128)S(1)} %get-tuple-element.74), channel_id=1, source_target_pairs={{16,0},{17,1},{18,2},{19,3},{20,4},{21,5},{22,6},{23,7},{24,8},{25... | collective-permute-start | bytes 1179656 | tf_op jit(solution)/shard_map/ppermute | solution.py:468
  47.2 14.6 %collective-permute-done.6.got = f32[16,48,128]{2,1,0:T(8,128)S(1)} collective-permute-done((f32[16,48,128]{2,1,0:T(8,128)S(1)}, f32[16,48,128]{2,1,0:T(8,128)S(1)}, u32[]{:S(2)}, u32[]{:S(2)}) %collective-permute-start.6) | collective-permute-done | bytes 393248 | tf_op jit(solution)/shard_map/ppermute | solution.py:468
  61.8 0.8 %final.1 = f32[2,16,8,256]{3,2,1,0:T(8,128)} custom-call(s32[1]{0:T(128)} %bitcast.2.flag, f32[16,48,128]{2,1,0:T(8,128)S(1)} %collective-permute-done.6.got, f32[16,4,8,128]{3,2,1,0:T(8,128)S(1)} %get-tuple-element.56.opened, f32[2,16,8,256]{3,2,1,0:T(8,128)S(1)} %bitcast.10), custom_call_target="tpu_custom_call" | custom-call | tf_op jit(solution)/shard_map/final/pallas_call | solution.py:418
  (5 shorter events, 0.0 us)
Async XLA Ops:
  1.6 0.9 %copy-start = (s32[128,256]{1,0:T(8,128)S(1)}, s32[128,256]{1,0:T(8,128)}, u32[]{:S(2)}) copy-start(s32[128,256]{1,0:T(8,128)} %land.1) | copy-start | bytes 393220
  2.5 7.2 %copy-start.1 = (f32[1,7,128,256]{3,2,1,0:T(8,128)S(1)}, f32[1,7,128,256]{3,2,1,0:T(8,128)}, u32[]{:S(2)}) copy-start(f32[1,7,128,256]{3,2,1,0:T(8,128)} %param.8) | copy-start | bytes 2752516
  5.8 3.9 %collective-permute-start.2 = (f32[16,144,128]{2,1,0:T(8,128)S(1)}, f32[16,144,128]{2,1,0:T(8,128)}, u32[]{:S(2)}, u32[]{:S(2)}) collective-permute-start(f32[16,144,128]{2,1,0:T(8,128)S(1)} %get-tuple-element.45), channel_id=1, source_target_pairs={{0,16},{1,17},{2,18},{3,19},{4,20},{5,21},{6,22},{7,23},{8,24},{9,... | collective-permute-start | bytes 3538952 | tf_op jit(solution)/shard_map/ppermute | solution.py:441
  8.1 1.6 %collective-permute-start.4 = (f32[128,128]{1,0:T(8,128)S(1)}, f32[128,128]{1,0:T(8,128)S(1)}, u32[]{:S(2)}, u32[]{:S(2)}) collective-permute-start(f32[128,128]{1,0:T(8,128)S(1)} %get-tuple-element.47), channel_id=1, source_target_pairs={{17,16},{18,17},{19,18},{16,19},{21,20},{22,21},{23,22},{20,23},{2... | collective-permute-start | bytes 196616 | tf_op jit(solution)/shard_map/ppermute | solution.py:446
  8.8 0.9 %collective-permute-start.3 = (f32[128,128]{1,0:T(8,128)S(1)}, f32[128,128]{1,0:T(8,128)S(1)}, u32[]{:S(2)}, u32[]{:S(2)}) collective-permute-start(f32[128,128]{1,0:T(8,128)S(1)} %get-tuple-element.47), channel_id=1, source_target_pairs={{16,17},{17,18},{18,19},{19,16},{20,21},{21,22},{22,23},{23,20},{2... | collective-permute-start | bytes 196616 | tf_op jit(solution)/shard_map/ppermute | solution.py:445
  27.6 11.2 %collective-permute-start.5 = (s32[16,24]{1,0:T(8,128)S(1)}, s32[16,24]{1,0:T(8,128)S(1)}, u32[]{:S(2)}, u32[]{:S(2)}) collective-permute-start(s32[16,24]{1,0:T(8,128)S(1)} %get-tuple-element.48), channel_id=1, source_target_pairs={{0,16},{16,0},{1,17},{17,1},{2,18},{18,2},{3,19},{19,3},{4,20},{20... | collective-permute-start | bytes 4616 | tf_op jit(solution)/shard_map/ppermute | solution.py:464
  45.9 15.9 %collective-permute-start.6 = (f32[16,48,128]{2,1,0:T(8,128)S(1)}, f32[16,48,128]{2,1,0:T(8,128)S(1)}, u32[]{:S(2)}, u32[]{:S(2)}) collective-permute-start(f32[16,48,128]{2,1,0:T(8,128)S(1)} %get-tuple-element.74), channel_id=1, source_target_pairs={{16,0},{17,1},{18,2},{19,3},{20,4},{21,5},{22,6},{23,7},{24,8},{25... | collective-permute-start | bytes 1179656 | tf_op jit(solution)/shard_map/ppermute | solution.py:468

commit v3 on v2

--- a/solution.py
+++ b/solution.py
@@ -10,7 +10,8 @@
 BX = 128
 NSUB = 4
 FRONT = 8
-STEP = 16
+STEP = 13
+REPLY = 7
 
 CD_ICE = 0.1
 CW = 1.5
@@ -42,8 +43,17 @@
     return jnp.where(q, west, east)
 
 
-def pack_body(nlat, nlon, per, count, raw, idb, pay, opened, edge, rim):
+def column(row):
+    parts = []
+    for lo in range(0, row.shape[1], BX):
+        diag = lax.broadcasted_iota(jnp.int32, (BX, BX), 0) == lanes(BX)
+        parts.append(jnp.sum(jnp.where(diag, row[:, lo : lo + BX].astype(jnp.float32), 0.0), axis=1, keepdims=True))
+    return jnp.concatenate(parts, 0) if len(parts) > 1 else parts[0]
+
+
+def pack_body(nlat, nlon, per, count, raw, owner, pay, opened, edge, rim, idb):
     n = nlat * nlon
+    idb[...] = jnp.broadcast_to(column(owner[...]), (count, BX)).astype(jnp.int32)
     lane = lanes(per)
     group = lane // 8
     lat_base = 13 * per
@@ -70,7 +80,8 @@
             pay[t, pl.ds(p, per, stride=12), :] = planes[p]
             ends = jnp.where(group == p, roll(planes[p], 8 * p + 4), ends)
         edge[t] = ends
-        ids = idb[t]
+        spot = t * per
+        ids = idb[pl.ds(pl.multiple_of(spot, per), per), :] - t * count
 
         def pick(block, value):
             return jnp.sum(jnp.where(ids == block, value, 0.0), axis=0, keepdims=True)
@@ -105,13 +116,14 @@
 
 
 def ends_body(ice, covered, land, active, ends):
-    count = covered.shape[0]
+    count = covered.shape[1]
     lane = lanes(count)
     group = lane // 8
     total = jnp.zeros((count, BX), jnp.float32)
+    cover = column(covered[...])
     for y in range(2):
         cells = slice(y * BX, (y + 1) * BX)
-        act = covered[...].astype(jnp.float32) * (1 - land[:, cells]).astype(jnp.float32)
+        act = cover * (1 - land[:, cells]).astype(jnp.float32)
         active[:, cells] = act
         for ch in range(8):
             x = act if ch == 7 else ice[ch, :, :, cells].reshape(count, BX)
@@ -120,17 +132,17 @@
     ends[...] = total
 
 
-def first_kernel(nlat, nlon, per, flag, raw, idb, covered, land, pay, opened, active, ends, edge, rim):
+def first_kernel(nlat, nlon, per, flag, raw, owner, covered, land, pay, opened, active, ends, edge, rim, idb):
     @pl.when(flag[0] == 0)
     def _():
-        pack_body(nlat, nlon, per, nlat * nlon * per, raw, idb, pay, opened, edge, rim)
+        pack_body(nlat, nlon, per, nlat * nlon * per, raw, owner, pay, opened, edge, rim, idb)
 
     @pl.when(flag[0] != 0)
     def _():
         ends_body(raw, covered, land, active, ends)
 
 
-def first(flag, raw, idb, covered, land, nlat, nlon):
+def first(flag, raw, owner, covered, land, nlat, nlon):
     _, n, per, _ = raw.shape
     count = n * per
     return pl.pallas_call(
@@ -138,10 +150,11 @@
         out_shape=[f32(n, 13 * per + 40, BX), f32(n, 4, per, BX), f32(count, 2 * BX), f32(count, BX)],
         in_specs=[SMEM] + [VMEM] * 4,
         out_specs=[VMEM] * 4,
-        scratch_shapes=[pltpu.VMEM((n, per, BX), jnp.float32), pltpu.VMEM((n, 40, BX), jnp.float32)],
+        scratch_shapes=[pltpu.VMEM((n, per, BX), jnp.float32), pltpu.VMEM((n, 40, BX), jnp.float32),
+                        pltpu.VMEM((count, BX), jnp.int32)],
         compiler_params=params(12),
         name="first",
-    )(flag, raw, idb, covered, land)
+    )(flag, raw, owner, covered, land)
 
 
 def rows_kernel(ice, active, west, east, sides, north, south):
@@ -199,10 +212,10 @@
         for y in range(2):
             for w in range(2):
                 u, v, mass, conc, s1, s2, s12, act = [grid[ch, y, w, at, :] for ch in range(8)]
-                for k, x in enumerate((u, v, s1, s2, s12)):
+                for k, x in enumerate((u, v, 0.5 * s1, 0.5 * s2, s12)):
                     begin[k, y, w, at, :] = x
-                still[0, y, w, at, :] = mass * jnp.exp(CSTAR * (conc - 1.0)) * act * (1.0 / 3.0)
-                still[1, y, w, at, :] = mass
+                still[0, y, w, at, :] = mass * jnp.exp(CSTAR * (conc - 1.0)) * act * (1.0 / 6.0)
+                still[1, y, w, at, :] = 2.0 * mass
                 still[2, y, w, at, :] = CW * conc * act
                 still[3, y, w, at, :] = act
                 still[4, y, w, at, :] = conc
@@ -227,21 +240,17 @@
     tiles = (count + 4 + 7) // 8
     height = tiles * 8
     blank = jnp.zeros((8, BX), jnp.float32)
-    for k in range(count + 4, height):
-        spot[k * STEP : k * STEP + 8, :] = blank
-        spot[k * STEP + 8 : k * STEP + 16, :] = blank
+    for k in (0, 8):
+        spot[k : k + 8, :] = blank
+    for k in range((count + 3) * STEP, height * STEP, 8):
+        spot[k : k + 8, :] = blank
     for k in (0, height - 8):
         hw[k : k + 8, :] = blank
         he[k : k + 8, :] = blank
-    spot[0:8, :] = blank
-    spot[8:16, :] = blank
-    end = (count + 3) * STEP
-    spot[end : end + 8, :] = blank
-    spot[end + 8 : end + 16, :] = blank
 
     def place(o, acc):
         for j in range(per):
-            b = pl.multiple_of((ids[o, j] + 2) * STEP, STEP)
+            b = (ids[o, j] + 2) * STEP
             spot[pl.ds(b, 12), :] = recv[o, 12 * j : 12 * j + 12, :]
             row = recv[o, 12 * per + j : 12 * per + j + 1, :]
             hw[pl.ds(ids[o, per + j] + 2, 1), :] = row
@@ -276,6 +285,7 @@
                 for k in range(5):
                     state[k, y, w, to, :] = begin[k, y, w, at, :]
                 mass, act, conc = [still[k, y, w, at, :] for k in (1, 3, 4)]
+                mass = 0.5 * mass
                 forced[0, y, w, at, :] = act * (conc * f[0] - mass * f[4])
                 forced[1, y, w, at, :] = act * (conc * f[1] - mass * f[5])
                 forced[2, y, w, at, :] = f[2]
@@ -313,18 +323,20 @@
                     syy = vn[k] - v[k]
                     shear = (un[k] - u[k]) + (ve[w] - v[k])
                     div, ten = sxx + syy, sxx - syy
-                    x = div * div + ((ten * ten + shear * shear) * 0.25 + 0.25)
-                    inv = lax.rsqrt(x)
-                    kr = still[0, y, w, at, :] * inv
-                    t1 = state[2, y, w, to, :] * (2.0 / 3.0) + kr * (div - x * inv)
-                    t2 = state[3, y, w, to, :] * (2.0 / 3.0) + kr * (ten * 0.25)
-                    t3 = state[4, y, w, to, :] * (2.0 / 3.0) + kr * (shear * 0.125)
+                    twice = div + div
+                    inv = lax.rsqrt(twice * twice + (ten * ten + shear * shear) + 1.0)
+                    hard = still[0, y, w, at, :]
+                    kr = hard * inv
+                    half = 0.5 * kr
+                    t1 = (state[2, y, w, to, :] * (2.0 / 3.0) - hard) + kr * twice
+                    t2 = state[3, y, w, to, :] * (2.0 / 3.0) + half * ten
+                    t3 = state[4, y, w, to, :] * (2.0 / 3.0) + half * shear
                     state[2, y, w, to, :] = t1
                     state[3, y, w, to, :] = t2
                     state[4, y, w, to, :] = t3
                     s12[k] = t3
-                    a[k] = 0.5 * (t1 + t2)
-                    c[k] = 0.5 * (t1 - t2)
+                    a[k] = t1 + t2
+                    c[k] = t1 - t2
             for w in range(2):
                 cross[w, to, :] = c[1, w]
             for y in range(2):
@@ -338,14 +350,13 @@
                         s12s, cs = state[4, 1, w, down1, :], cross[w, down1, :]
                     fx = (a[k] - aw[w]) + (s12[k] - s12s)
                     fy = (s12[k] - sw[w]) + (c[k] - cs)
-                    mass, base = still[1, y, w, at, :], still[2, y, w, at, :]
+                    m2, base = still[1, y, w, at, :], still[2, y, w, at, :]
                     cx, cy = forced[2, y, w, at, :], forced[3, y, w, at, :]
                     dx, dy = cx - u[k], cy - v[k]
                     y2 = dx * dx + dy * dy + DRAG_FLOOR
                     drag = base * (y2 * lax.rsqrt(y2))
-                    m2 = mass * 2.0
-                    part = still[3, y, w, at, :] / (jnp.maximum(m2, 1.0) + drag)
-                    mc = CORIO * mass
+                    part = still[3, y, w, at, :] * (1.0 / (jnp.maximum(m2, 1.0) + drag))
+                    mc = (0.5 * CORIO) * m2
                     state[0, y, w, to, :] = part * (m2 * u[k] + fx + forced[0, y, w, at, :] + drag * cx + mc * v[k])
                     state[1, y, w, to, :] = part * (m2 * v[k] + fy + forced[1, y, w, at, :] + drag * cy - mc * u[k])
         return carry
@@ -361,14 +372,14 @@
             dy = state[1, y, 0, to, :] - forced[3, y, 0, at, :]
             factor = base * jnp.sqrt(dx * dx + dy * dy + DRAG_FLOOR)
             for k, x in enumerate((factor * dx, factor * dy, base * (1.0 / CW))):
-                out8[pl.ds(64 * r + 2 * k + y, 8, stride=8), :] = x
+                out8[pl.ds(8 * r * REPLY + 2 * k + y, 8, stride=REPLY), :] = x
     for y in range(2):
         for k in range(2):
             moved[k, :, y * BX : (y + 1) * BX] = state[k, y, 0, FRONT + 2 : FRONT + 2 + count, :]
 
     def answer(o, _):
         for j in range(per):
-            b = pl.multiple_of((ids[o, j] + 2) * 8, 8)
+            b = (ids[o, j] + 2) * REPLY
             back[o, 6 * j : 6 * j + 6, :] = out8[pl.ds(b, 6), :]
         return 0
 
@@ -381,8 +392,8 @@
     height = (count + 4 + 7) // 8 * 8
     tall = height + 2 * FRONT
     scratch = [
-        (height * STEP, BX), (height, BX), (height, BX),
-        (5, 2, 2, tall, BX), (4, 2, 2, height, BX), (2, tall, BX), (height * 8, BX),
+        (height * STEP + 8, BX), (height, BX), (height, BX),
+        (5, 2, 2, tall, BX), (4, 2, 2, height, BX), (2, tall, BX), (height * REPLY + 8, BX),
     ]
     return pl.pallas_call(
         functools.partial(ice_kernel, n, per, count),
@@ -434,33 +445,31 @@
     flag = side.reshape(1)
     fields = fields[0]
     local = (block_owner % count).reshape(nlat, nlon, per)
-    idb = jnp.broadcast_to(local.reshape(n, per, 1), (n, per, BX))
     ids = jnp.concatenate([local, jnp.roll(local, 1, 1), jnp.roll(local, -1, 1)], 2).reshape(n, 3 * per)
     split = fields.reshape(7, n, per, 2 * BX)
-    pay, opened, active, ends = first(flag, split, idb, ice_covered.reshape(count, 1), land_mask, nlat, nlon)
+    pay, opened, active, ends = first(
+        flag, split, block_owner.reshape(1, count), ice_covered.reshape(1, count), land_mask, nlat, nlon
+    )
     pay = lax.ppermute(pay, "comp", [(0, 1)])
-    every = ("comp", "lat", "lon")
-    tiles = [(i, j) for i in range(nlat) for j in range(nlon)]
-    east_pairs = [(n + i * nlon + j, n + i * nlon + (j + 1) % nlon) for i, j in tiles]
-    west = lax.ppermute(ends, every, east_pairs)
-    east = lax.ppermute(ends, every, [(j, i) for i, j in east_pairs])
-
     def everyone(x):
         return lax.all_to_all(x, ("lat", "lon"), split_axis=0, concat_axis=0, tiled=True)
 
-    def ice_side(pay, ids, active, west, east):
+    def ice_side(pay, ids, active, ends):
         recv = everyone(pay)
+        ring = [(i, (i + 1) % nlon) for i in range(nlon)]
+        west = lax.ppermute(ends, "lon", ring)
+        east = lax.ppermute(ends, "lon", [(j, i) for i, j in ring])
         sides, north, south = ice_rows(fields, active, west, east)
         line = [(i, i + 1) for i in range(nlat - 1)]
         below = lax.ppermute(north, "lat", line)
         above = lax.ppermute(south, "lat", [(j, i) for i, j in line])
         return recv, ids, sides, below, above
 
-    def ocean_side(pay, ids, active, west, east):
-        row = jnp.zeros((34, BX), jnp.float32)
-        return jnp.zeros(pay.shape, jnp.float32), everyone(ids), jnp.zeros(west.shape, jnp.float32), row, row
-
-    recv, owner, sides, below, above = lax.cond(side == 1, ice_side, ocean_side, pay, ids, active, west, east)
+    def ocean_side(pay, ids, active, ends):
+        row = ends[:34]
+        return jnp.zeros(pay.shape, jnp.float32), everyone(ids), ends, row, row
+
+    recv, owner, sides, below, above = lax.cond(side == 1, ice_side, ocean_side, pay, ids, active, ends)
     swap = lax.ppermute(owner, "comp", [(0, 1), (1, 0)])
     begin, still = prep(fields, active, sides, below, above)
     back, moved = ice_step(swap, recv, begin, still)

time: 63.1 us -> 59.3 us (0.940)
  blocking collectives: 15.6 us -> 0 us
  waiting for transfers between devices: 14.6 us -> 21 us
  starting transfers between devices: 14.9 us -> 19.3 us
  local copies, waits for them, and re-layouts: 4.22 us -> 5.43 us
    all_to_all x1 -> x0, blocking collectives: 15.6 us -> none  [everyone(): lax.all_to_all(x, ('lat', 'lon'), split_axis=0, concat_axis=0, tiled=True)]
    all_to_all x0 -> x1, starting transfers between devices: none -> 8.34 us  [everyone(): lax.all_to_all(x, ('lat', 'lon'), split_axis=0, concat_axis=0, tiled=True)]
    all_to_all x0 -> x1, waiting for transfers between devices: none -> 5.81 us  [everyone(): lax.all_to_all(x, ('lat', 'lon'), split_axis=0, concat_axis=0, tiled=True)]
    ppermute x1, starting transfers between devices: 9.9 us -> 7.35 us  [per_device(): swap = lax.ppermute(owner, 'comp', [(0, 1), (1, 0)])]
    cond x0 -> x1, local copies, waits for them, and re-layouts: none -> 1.33 us
    ppermute x2 -> x0, starting transfers between devices: 1.32 us -> none  [the longest x1 0.66 us: per_device(): west = lax.ppermute(ends, every, east_pairs)]
    unnamed x4 -> x8, local copies, waits for them, and re-layouts: 0.91 us -> 2.22 us
    another operation x4 -> x1, local copies, waits for them, and re-layouts: 2.28 us -> 1.08 us
  transfers between devices with their start and end apart: 5 -> 4, of which waited for: 1 -> 3; matrix products, arithmetic and copies ran while one was open for 0% -> 5% of each run, Pallas kernels for 2% -> 2%
where the time goes in v3:
time: 59.3 us; the launch traced here: 58.8 us
  waiting for transfers between devices  21 us (35%)
  starting transfers between devices  19.3 us (33%)
  Pallas kernels  12.2 us (21%)
  local copies, waits for them, and re-layouts  5.43 us (9%)
  other arithmetic  0.7 us (1%)
    ppermute x1, waiting for transfers between devices, per_device(): got = lax.ppermute(back, 'comp', [(1, 0)])  14.6 us
    all_to_all x1, starting transfers between devices, everyone(): lax.all_to_all(x, ('lat', 'lon'), split_axis=0, concat_axis=0, tiled=True)  8.34 us
    ppermute x1, starting transfers between devices, per_device(): swap = lax.ppermute(owner, 'comp', [(0, 1), (1, 0)])  7.35 us
    pallas_call x1, Pallas kernels, ice_step(): pl.pallas_call(functools.partial(ice_kernel, n, per, count), out_shape=[f...  6.75 us
    all_to_all x1, waiting for transfers between devices, everyone(): lax.all_to_all(x, ('lat', 'lon'), split_axis=0, concat_axis=0, tiled=True)  5.81 us
    pallas_call x1, Pallas kernels, first(): pl.pallas_call(functools.partial(first_kernel, nlat, nlon, per), out_shap...  3.36 us
    ppermute x1, starting transfers between devices, per_device(): pay = lax.ppermute(pay, 'comp', [(0, 1)])  2.34 us
    unnamed x8, local copies, waits for them, and re-layouts  2.22 us
  transfers between devices with their start and end apart: 4, of which 3 were waited for; matrix products, arithmetic and copies ran while one was open for 5% of the time, Pallas kernels for 2%

profile of v3, /device:TPU:0, one launch (start us, length us, event | category | flops | bytes accessed | tf_op | source)
XLA Modules:
  0.0 58.8 jit_solution(14010426843253527831)
XLA Ops:
  0.0 0.0 copy-start
  0.0 0.9 %copy-done = s32[128,256]{1,0:T(8,128)S(1)} copy-done((s32[128,256]{1,0:T(8,128)S(1)}, s32[128,256]{1,0:T(8,128)}, u32[]{:S(2)}) %copy-start) | copy-done | bytes 131096
  0.9 0.0 copy-start.1
  0.9 0.7 %copy-done.1 = s32[128]{0:T(128)S(1)} copy-done((s32[128]{0:T(128)S(1)}, s32[128]{0:T(128)}, u32[]{:S(2)}) %copy-start.1) | copy-done | bytes 536
  1.6 0.0 copy-start.2
  1.6 0.7 %copy-done.2 = s32[128]{0:T(128)S(1)} copy-done((s32[128]{0:T(128)S(1)}, s32[128]{0:T(128)}, u32[]{:S(2)}) %copy-start.2) | copy-done | bytes 536
  2.2 0.0 copy-start.3
  2.2 3.4 %first.1 = (f32[16,144,128]{2,1,0:T(8,128)S(1)}, f32[16,4,8,128]{3,2,1,0:T(8,128)S(1)}, f32[128,256]{1,0:T(8,128)S(1)}, f32[128,128]{1,0:T(8,128)S(1)}) custom-call(s32[1]{0:T(128)} %bitcast.2.flag, f32[7,16,8,256]{3,2,1,0:T(8,128)} %bitcast.14, s32[1,128]{1,0:T(1,128)S(1)} %bitcast.13, s32[1,128]{1,0:T(1,128)S(1)} %bitcast.12, s32[128,256]{1,0:T(8,128)S(1)} %copy-done), custom_call_target="tpu_custom_call" | custom-call | tf_op jit(solution)/shard_map/first/pallas_call | solution.py:148
  5.6 2.3 %collective-permute-start.4 = (f32[16,144,128]{2,1,0:T(8,128)S(1)}, f32[16,144,128]{2,1,0:T(8,128)}, u32[]{:S(2)}, u32[]{:S(2)}) collective-permute-start(f32[16,144,128]{2,1,0:T(8,128)S(1)} %get-tuple-element.48), channel_id=1, source_target_pairs={{0,16},{1,17},{2,18},{3,19},{4,20},{5,21},{6,22},{7,23},{8,24},{9,... | collective-permute-start | bytes 3538952 | tf_op jit(solution)/shard_map/ppermute | solution.py:453
  7.9 0.1 reshape.26
  8.0 0.1 concatenate.18
  8.2 0.7 %pad_add_fusion.2 = s32[16,24]{1,0:T(8,128)} fusion(s32[16,8]{1,0:T(8,128)S(1)} %bitcast.18, s32[16,8]{1,0:T(8,128)S(1)} %bitcast.17, s32[16,8]{1,0:T(8,128)S(1)} %concatenate.18), kind=kLoop, calls=%fused_computation.2 | loop fusion | flops 768 | bytes 3072 | tf_op jit(solution)/shard_map/concatenate | solution.py:448
  8.8 0.6 %collective-permute-done.4 = f32[16,144,128]{2,1,0:T(8,128)} collective-permute-done((f32[16,144,128]{2,1,0:T(8,128)S(1)}, f32[16,144,128]{2,1,0:T(8,128)}, u32[]{:S(2)}, u32[]{:S(2)}) %collective-permute-start.4) | collective-permute-done | bytes 1179680 | tf_op jit(solution)/shard_map/ppermute | solution.py:453
  9.5 0.0 copy-done.3
  9.5 17.2 %conditional.2 = (f32[16,144,128]{2,1,0:T(8,128)}, s32[16,24]{1,0:T(8,128)S(1)}, f32[128,128]{1,0:T(8,128)S(1)}, f32[34,128]{1,0:T(8,128)}, f32[34,128]{1,0:T(8,128)}) conditional(s32[]{:T(128)} %convert_element_type.4, (s32[16,24]{1,0:T(8,128)}, f32[128,128]{1,0:T(8,128)S(1)}) %tuple.19, (f32[16,144,128]{2,1,0:T(8,128)}, f32[128,128]{1,0:T(8,128)S(1)}, ...), branch_computations={%region_0.1_spmd, %region_1.2_spmd} | conditional | bytes 4205800 | solution.py:472
  9.5 8.3 %all-to-all-start = ((s32[16,1,24]{2,1,0:T(1,128)}), s32[16,1,24]{2,1,0:T(1,128)S(1)}, u32[]{:S(2)}, u32[]{:S(2)}) async-start(s32[16,1,24]{2,1,0:T(1,128)} %bitcast), calls=%async_computation | async-start | bytes 16384 | tf_op jit(solution)/shard_map/cond/branch_0_fun/all_to_all | solution.py:455
  17.8 0.6 %slice.14 = f32[34,128]{1,0:T(8,128)} slice(f32[128,128]{1,0:T(8,128)S(1)} %get-tuple-element.68), slice={[0:34], [0:128]} | slice | bytes 34816 | tf_op jit(solution)/shard_map/cond/branch_0_fun/slice | solution.py:469
  18.4 1.3 %copy.9 = f32[34,128]{1,0:T(8,128)} copy(f32[34,128]{1,0:T(8,128)} %slice.14) | data formatting | bytes 34816 | tf_op jit(solution)/shard_map/cond
  19.8 5.8 %all-to-all-done = s32[16,1,24]{2,1,0:T(1,128)S(1)} async-done(((s32[16,1,24]{2,1,0:T(1,128)}), s32[16,1,24]{2,1,0:T(1,128)S(1)}, u32[]{:S(2)}, u32[]{:S(2)}) %all-to-all-start) | async-done | bytes 1568 | tf_op jit(solution)/shard_map/cond/branch_0_fun/all_to_all | solution.py:455
  25.6 1.1 %broadcast.7 = f32[16,144,128]{2,1,0:T(8,128)} broadcast(f32[]{:T(128)} %constant.18.clone), dimensions={} | broadcast | bytes 1179652 | tf_op jit(solution)/shard_map/broadcast.3
  26.7 7.3 %collective-permute-start.5 = (s32[16,24]{1,0:T(8,128)S(1)}, s32[16,24]{1,0:T(8,128)S(1)}, u32[]{:S(2)}, u32[]{:S(2)}) collective-permute-start(s32[16,24]{1,0:T(8,128)S(1)} %get-tuple-element.50), channel_id=1, source_target_pairs={{0,16},{16,0},{1,17},{17,1},{2,18},{18,2},{3,19},{19,3},{4,20},{20... | collective-permute-start | bytes 4616 | tf_op jit(solution)/shard_map/ppermute | solution.py:473
  34.0 1.3 %prep.1 = (f32[5,2,2,136,128]{4,3,2,1,0:T(8,128)S(1)}, f32[5,2,2,136,128]{4,3,2,1,0:T(8,128)S(1)}) custom-call(f32[7,128,256]{2,1,0:T(8,128)S(1)} %bitcast.16, f32[128,256]{1,0:T(8,128)S(1)} %get-tuple-element.49.active, f32[128,128]{1,0:T(8,128)S(1)} %get-tuple-element.52.sides, f32[34,128]{1,0:T(8,128)} %get-tuple-element.53.below, ...), custom_call_target="tpu_custom_call" | custom-call | tf_op jit(solution)/shard_map/prep/pallas_call | solution.py:227
  35.3 0.0 collective-permute-done.5.ids
  35.4 6.7 %ice_step.1 = (f32[16,48,128]{2,1,0:T(8,128)S(1)}, f32[2,128,256]{2,1,0:T(8,128)S(1)}) custom-call(s32[16,24]{1,0:T(8,128)S(1)} %collective-permute-done.5.ids, f32[16,144,128]{2,1,0:T(8,128)} %get-tuple-element.51.recv, f32[5,2,2,136,128]{4,3,2,1,0:T(8,128)S(1)} %get-tuple-element.55.begin, f32[5,2,2,136,128]{4,3,2,1,0:T(8,128)S(1)} %get-tuple-element.56.still), custom_call_target="tpu_custom_call" | custom-call | tf_op jit(solution)/shard_map/ice_step/pallas_call | solution.py:398
  42.1 1.3 %collective-permute-start.6 = (f32[16,48,128]{2,1,0:T(8,128)S(1)}, f32[16,48,128]{2,1,0:T(8,128)S(1)}, u32[]{:S(2)}, u32[]{:S(2)}) collective-permute-start(f32[16,48,128]{2,1,0:T(8,128)S(1)} %get-tuple-element.76), channel_id=1, source_target_pairs={{16,0},{17,1},{18,2},{19,3},{20,4},{21,5},{22,6},{23,7},{24,8},{25... | collective-permute-start | bytes 1179656 | tf_op jit(solution)/shard_map/ppermute | solution.py:477
  43.4 14.6 %collective-permute-done.6.got = f32[16,48,128]{2,1,0:T(8,128)S(1)} collective-permute-done((f32[16,48,128]{2,1,0:T(8,128)S(1)}, f32[16,48,128]{2,1,0:T(8,128)S(1)}, u32[]{:S(2)}, u32[]{:S(2)}) %collective-permute-start.6) | collective-permute-done | bytes 393248 | tf_op jit(solution)/shard_map/ppermute | solution.py:477
  58.0 0.8 %final.1 = f32[2,16,8,256]{3,2,1,0:T(8,128)} custom-call(s32[1]{0:T(128)} %bitcast.2.flag, f32[16,48,128]{2,1,0:T(8,128)S(1)} %collective-permute-done.6.got, f32[16,4,8,128]{3,2,1,0:T(8,128)S(1)} %get-tuple-element.58.opened, f32[2,16,8,256]{3,2,1,0:T(8,128)S(1)} %bitcast.11), custom_call_target="tpu_custom_call" | custom-call | tf_op jit(solution)/shard_map/final/pallas_call | solution.py:429
  (5 shorter events, 0.1 us)
Async XLA Ops:
  0.0 0.9 %copy-start = (s32[128,256]{1,0:T(8,128)S(1)}, s32[128,256]{1,0:T(8,128)}, u32[]{:S(2)}) copy-start(s32[128,256]{1,0:T(8,128)} %land.1) | copy-start | bytes 393220
  0.9 0.7 %copy-start.1 = (s32[128]{0:T(128)S(1)}, s32[128]{0:T(128)}, u32[]{:S(2)}) copy-start(s32[128]{0:T(128)} %param.10) | copy-start | bytes 1540
  1.6 0.7 %copy-start.2 = (s32[128]{0:T(128)S(1)}, s32[128]{0:T(128)}, u32[]{:S(2)}) copy-start(s32[128]{0:T(128)} %param.9) | copy-start | bytes 1540
  2.2 7.3 %copy-start.3 = (f32[1,7,128,256]{3,2,1,0:T(8,128)S(1)}, f32[1,7,128,256]{3,2,1,0:T(8,128)}, u32[]{:S(2)}) copy-start(f32[1,7,128,256]{3,2,1,0:T(8,128)} %param.8) | copy-start | bytes 2752516
  5.6 3.9 %collective-permute-start.4 = (f32[16,144,128]{2,1,0:T(8,128)S(1)}, f32[16,144,128]{2,1,0:T(8,128)}, u32[]{:S(2)}, u32[]{:S(2)}) collective-permute-start(f32[16,144,128]{2,1,0:T(8,128)S(1)} %get-tuple-element.48), channel_id=1, source_target_pairs={{0,16},{1,17},{2,18},{3,19},{4,20},{5,21},{6,22},{7,23},{8,24},{9,... | collective-permute-start | bytes 3538952 | tf_op jit(solution)/shard_map/ppermute | solution.py:453
  9.5 16.1 %all-to-all-start = ((s32[16,1,24]{2,1,0:T(1,128)}), s32[16,1,24]{2,1,0:T(1,128)S(1)}, u32[]{:S(2)}, u32[]{:S(2)}) async-start(s32[16,1,24]{2,1,0:T(1,128)} %bitcast), calls=%async_computation | async-start | bytes 16384 | tf_op jit(solution)/shard_map/cond/branch_0_fun/all_to_all | solution.py:455
  26.7 8.7 %collective-permute-start.5 = (s32[16,24]{1,0:T(8,128)S(1)}, s32[16,24]{1,0:T(8,128)S(1)}, u32[]{:S(2)}, u32[]{:S(2)}) collective-permute-start(s32[16,24]{1,0:T(8,128)S(1)} %get-tuple-element.50), channel_id=1, source_target_pairs={{0,16},{16,0},{1,17},{17,1},{2,18},{18,2},{3,19},{19,3},{4,20},{20... | collective-permute-start | bytes 4616 | tf_op jit(solution)/shard_map/ppermute | solution.py:473
  42.1 15.9 %collective-permute-start.6 = (f32[16,48,128]{2,1,0:T(8,128)S(1)}, f32[16,48,128]{2,1,0:T(8,128)S(1)}, u32[]{:S(2)}, u32[]{:S(2)}) collective-permute-start(f32[16,48,128]{2,1,0:T(8,128)S(1)} %get-tuple-element.76), channel_id=1, source_target_pairs={{16,0},{17,1},{18,2},{19,3},{20,4},{21,5},{22,6},{23,7},{24,8},{25... | collective-permute-start | bytes 1179656 | tf_op jit(solution)/shard_map/ppermute | solution.py:477

commit v4 on v3

v4 whole, which is shorter than its diff:
```python
import functools

import jax
import jax.numpy as jnp
from jax import lax
from jax.experimental import pallas as pl
from jax.experimental.pallas import tpu as pltpu
from jax.sharding import PartitionSpec as P

BX = 128
NSUB = 4
FRONT = 8
STEP = 13
REPLY = 7
PARTS = 4

CD_ICE = 0.1
CW = 1.5
CSTAR = 2.0
CORIO = 0.3
DRAG_FLOOR = 0.1

VMEM = pl.BlockSpec(memory_space=pltpu.VMEM)
SMEM = pl.BlockSpec(memory_space=pltpu.SMEM)


def params(mib):
    return pltpu.CompilerParams(vmem_limit_bytes=mib * 1024 * 1024)


def f32(*shape):
    return jax.ShapeDtypeStruct(shape, jnp.float32)


def lanes(rows):
    return lax.broadcasted_iota(jnp.int32, (rows, BX), 1)


def roll(x, by):
    return pltpu.roll(x, by % BX, 1)


def at_end(q, west, east):
    return jnp.where(q, west, east)


def column(row):
    parts = []
    for lo in range(0, row.shape[1], BX):
        diag = lax.broadcasted_iota(jnp.int32, (BX, BX), 0) == lanes(BX)
        parts.append(jnp.sum(jnp.where(diag, row[:, lo : lo + BX].astype(jnp.float32), 0.0), axis=1, keepdims=True))
    return jnp.concatenate(parts, 0) if len(parts) > 1 else parts[0]


def pack_body(nlat, nlon, per, count, raw, owner, pay, opened, edge, rim, idb, parts, field):
    n = nlat * nlon
    idb[...] = jnp.broadcast_to(column(owner[...]), (count, BX)).astype(jnp.int32)
    lane = lanes(per)
    group = lane // 8
    lat_base = 13 * per

    def tile(t, _):
        def half(ch, y):
            return raw[ch, t, :, y * BX : (y + 1) * BX]

        planes = [None] * 12
        for y in range(2):
            wx, wy, rho = half(0, y), half(1, y), half(6, y)
            scale = rho * CD_ICE * jnp.sqrt(wx * wx + wy * wy + 1.0)
            planes[y] = scale * wx
            planes[2 + y] = scale * wy
            for ch in range(2, 6):
                planes[2 * ch + y] = half(ch, y)
            rx, ry = wx - planes[4 + y], wy - planes[6 + y]
            speed = jnp.sqrt(rx * rx + ry * ry + 1.0)
            rate = rho * (0.1 + 0.05 * speed) * speed
            opened[t, 2 * y] = rate * rx
            opened[t, 2 * y + 1] = rate * ry
        ends = jnp.zeros((per, BX), jnp.float32)
        for p in range(12):
            pay[t, pl.ds(p, per, stride=12), :] = planes[p]
            ends = jnp.where(group == p, roll(planes[p], 8 * p + 4), ends)
        edge[t] = ends
        spot = t * per
        ids = idb[pl.ds(pl.multiple_of(spot, per), per), :] - t * count

        def pick(block, value):
            return jnp.sum(jnp.where(ids == block, value, 0.0), axis=0, keepdims=True)

        rows = [pick(0, x) for x in planes] + [pick(1, x) for x in planes[0::2]]
        rows += [pick(count - 1, x) for x in planes]
        rows += [pick(count - 2, x) for x in planes[1::2]]
        rows += [pick(b, ends) for b in (0, 1, count - 1, count - 2)]
        for k, row in enumerate(rows):
            rim[t, k : k + 1, :] = row
        return 0

    for c in range(parts):
        field(c).wait()
        lax.fori_loop(c * (n // parts), (c + 1) * (n // parts), tile, 0)

    def dest(d, _):
        i, j = d // nlon, d % nlon
        jw, je = (j + nlon - 1) % nlon, (j + 1) % nlon
        q8 = (lane % 8) < 4
        pay[d, 12 * per : 13 * per, :] = at_end(q8, edge[i * nlon + jw], edge[i * nlon + je])
        for ii, ok, lo, c in (
            (jnp.minimum(i + 1, nlat - 1), i + 1 < nlat, 0, 36),
            (jnp.maximum(i - 1, 0), i > 0, 18, 38),
        ):
            scale = jnp.where(ok, 1.0, 0.0)
            pay[d, lat_base + lo : lat_base + lo + 18, :] = rim[ii * nlon + j, lo : lo + 18, :] * scale
            q2 = (lanes(2) % 8) < 4
            corner = at_end(q2, rim[ii * nlon + jw, c : c + 2, :], rim[ii * nlon + je, c : c + 2, :])
            pay[d, lat_base + c : lat_base + c + 2, :] = corner * scale
        return 0

    lax.fori_loop(0, n, dest, 0)


def ends_body(ice, covered, land, active, ends):
    count = covered.shape[1]
    lane = lanes(count)
    group = lane // 8
    total = jnp.zeros((count, BX), jnp.float32)
    cover = column(covered[...])
    for y in range(2):
        cells = slice(y * BX, (y + 1) * BX)
        act = cover * (1 - land[:, cells]).astype(jnp.float32)
        active[:, cells] = act
        for ch in range(8):
            x = act if ch == 7 else ice[ch, :, :, cells].reshape(count, BX)
            p = 2 * ch + y
            total = jnp.where(group == p, roll(x, 8 * p + 4), total)
    ends[...] = total


def first_kernel(nlat, nlon, per, raw_in, owner_in, cover_in, land_in, pay, opened, active, ends,
                 raw, owner, cover, land, edge, rim, idb, sems):
    n = nlat * nlon
    parts = PARTS if n % PARTS == 0 else 1
    step = n // parts

    def field(c):
        at = pl.ds(c * step, step)
        return pltpu.make_async_copy(raw_in.at[:, at], raw.at[:, at], sems.at[c])

    is_ocean = lax.axis_index("comp") == 0

    @pl.when(is_ocean)
    def _():
        ids = pltpu.make_async_copy(owner_in, owner, sems.at[PARTS])
        ids.start()
        for c in range(parts):
            field(c).start()
        ids.wait()
        pack_body(nlat, nlon, per, n * per, raw, owner, pay, opened, edge, rim, idb, parts, field)

    @pl.when(jnp.logical_not(is_ocean))
    def _():
        mask = pltpu.make_async_copy(land_in, land, sems.at[PARTS + 1])
        blocks = pltpu.make_async_copy(cover_in, cover, sems.at[PARTS + 2])
        blocks.start()
        mask.start()
        for c in range(parts):
            field(c).start()
        blocks.wait()
        mask.wait()
        for c in range(parts):
            field(c).wait()
        ends_body(raw, cover, land, active, ends)


def first(raw, owner, covered, land, nlat, nlon):
    _, n, per, cells = raw.shape
    count = n * per
    return pl.pallas_call(
        functools.partial(first_kernel, nlat, nlon, per),
        out_shape=[f32(n, 13 * per + 40, BX), f32(n, 4, per, BX), f32(count, cells), f32(count, BX)],
        in_specs=[pl.BlockSpec(memory_space=pltpu.HBM)] * 4,
        out_specs=[VMEM] * 4,
        scratch_shapes=[
            pltpu.VMEM(raw.shape, jnp.float32),
            pltpu.VMEM((1, count), jnp.int32),
            pltpu.VMEM((1, count), jnp.int32),
            pltpu.VMEM((count, cells), jnp.int32),
            pltpu.VMEM((n, per, BX), jnp.float32),
            pltpu.VMEM((n, 40, BX), jnp.float32),
            pltpu.VMEM((count, BX), jnp.int32),
            pltpu.SemaphoreType.DMA((PARTS + 3,)),
        ],
        compiler_params=params(12),
        name="first",
    )(raw, owner, covered, land)


def rows_kernel(ice, active, west, east, sides, north, south):
    count = active.shape[0]
    q = (lanes(count) % 8) < 4
    sides[...] = jnp.where(q, west[...], east[...])
    for out, lo in ((north, count - 2), (south, 0)):
        for y in range(2):
            cells = slice(y * BX, (y + 1) * BX)
            for ch in range(8):
                p = 2 * ch + y
                x = active[lo : lo + 2, cells] if ch == 7 else ice[ch, lo : lo + 2, cells]
                out[2 * p : 2 * p + 2, :] = x
        out[32:34, :] = sides[lo : lo + 2, :]


def ice_rows(ice, active, west, east):
    count = active.shape[0]
    return pl.pallas_call(
        rows_kernel,
        out_shape=[f32(count, BX), f32(34, BX), f32(34, BX)],
        in_specs=[VMEM] * 4,
        out_specs=[VMEM] * 3,
        compiler_params=params(8),
        name="ice_rows",
    )(ice, active, west, east)


def middle(rows):
    lane = lanes(rows)
    return (lane >= BX // 4) & (lane < 3 * BX // 4)


def side_plane(ends, ch, mid):
    odd = roll(ends, BX // 2 - (8 * (2 * ch + 1) + 4))
    return jnp.where(mid, odd, roll(ends, -(16 * ch + 4)))


def prep_kernel(count, height, ice, active, sides, below, above, begin, still, grid):
    mid, mid2 = middle(count), middle(2)
    pad = jnp.zeros((height - count - 4, BX), jnp.float32)
    for ch in range(8):
        for y in range(2):
            cells = slice(y * BX, (y + 1) * BX)
            grid[ch, y, 2 : 2 + count, :] = active[:, cells] if ch == 7 else ice[ch, :, cells]
            p = 2 * ch + y
            for lo, msg in ((0, below), (count + 2, above)):
                grid[ch, y, lo : lo + 2, :] = msg[2 * p : 2 * p + 2, :]
        grid[ch, 2, 2 : 2 + count, :] = side_plane(sides[...], ch, mid)
        for lo, msg in ((0, below), (count + 2, above)):
            grid[ch, 2, lo : lo + 2, :] = side_plane(msg[32:34, :], ch, mid2)
        for z in range(3):
            grid[ch, z, count + 4 :, :] = pad

    for r in range(height // 8):
        at = slice(8 * r, 8 * r + 8)
        for z in range(3):
            u, v, mass, conc, s1, s2, s12, act = [grid[ch, z, at, :] for ch in range(8)]
            for k, x in enumerate((u, v, 0.5 * s1, 0.5 * s2, s12)):
                begin[k, z, at, :] = x
            still[0, z, at, :] = mass * jnp.exp(CSTAR * (conc - 1.0)) * act * (1.0 / 6.0)
            still[1, z, at, :] = 2.0 * mass
            still[2, z, at, :] = CW * conc * act
            still[3, z, at, :] = act
            still[4, z, at, :] = conc


def prep(ice, active, sides, below, above):
    count = active.shape[0]
    height = (count + 4 + 7) // 8 * 8
    return pl.pallas_call(
        functools.partial(prep_kernel, count, height),
        out_shape=[f32(5, 3, height, BX)] * 2,
        in_specs=[VMEM] * 5,
        out_specs=[VMEM] * 2,
        scratch_shapes=[pltpu.VMEM((8, 3, height, BX), jnp.float32)],
        compiler_params=params(12),
        name="prep",
    )(ice, active, sides, below, above)


def east_of(even, odd, side, at127, at63):
    e, o, s = roll(even, -1), roll(odd, -1), roll(side, -1)
    wide = jnp.where(at127, e, jnp.where(at63, roll(odd, 63), s))
    return jnp.where(at127, s, e), jnp.where(at127, roll(side, 63), o), wide


def west_of(even, odd, side, at0, at64):
    e, o, s = roll(even, 1), roll(odd, 1), roll(side, 1)
    wide = jnp.where(at0, e, jnp.where(at64, roll(odd, 65), s))
    return jnp.where(at0, s, e), jnp.where(at0, roll(side, -63), o), wide


def ice_kernel(n, per, count, ids, recv, begin, still, back, moved,
               spot, hw, he, speed, state, forced, out8):
    tiles = (count + 4 + 7) // 8
    height = tiles * 8
    blank = jnp.zeros((8, BX), jnp.float32)
    for k in (0, 8):
        spot[k : k + 8, :] = blank
    for k in range((count + 3) * STEP, height * STEP, 8):
        spot[k : k + 8, :] = blank
    for k in (0, height - 8):
        hw[k : k + 8, :] = blank
        he[k : k + 8, :] = blank

    def place(o, acc):
        for j in range(per):
            b = (ids[o, j] + 2) * STEP
            spot[pl.ds(b, 12), :] = recv[o, 12 * j : 12 * j + 12, :]
            row = recv[o, 12 * per + j : 12 * per + j + 1, :]
            hw[pl.ds(ids[o, per + j] + 2, 1), :] = row
            he[pl.ds(ids[o, 2 * per + j] + 2, 1), :] = row
        return acc + recv[o, 13 * per : 13 * per + 40, :]

    rim = lax.fori_loop(0, n, place, jnp.zeros((40, BX), jnp.float32))
    up, down = (count + 2) * STEP, STEP
    spot[up : up + 12, :] = rim[0:12]
    spot[down : down + 12, :] = rim[18:30]
    for ch in range(6):
        k = up + STEP + 2 * ch
        spot[k : k + 1, :] = rim[12 + ch : 13 + ch]
        k = 2 * ch + 1
        spot[k : k + 1, :] = rim[30 + ch : 31 + ch]
    for ref in (hw, he):
        ref[count + 2 : count + 4, :] = rim[36:38]
        ref[1:2, :] = rim[38:39]
        ref[0:1, :] = rim[39:40]

    q, mid = (lanes(8) % 8) < 4, middle(8)
    for r in range(tiles):
        at = slice(8 * r, 8 * r + 8)
        to = slice(FRONT + 8 * r, FRONT + 8 * r + 8)
        ends = jnp.where(q, hw[at, :], he[at, :])
        for z in range(3):
            if z < 2:
                f = [spot[pl.ds(8 * r * STEP + 2 * ch + z, 8, stride=STEP), :] for ch in range(6)]
            else:
                f = [side_plane(ends, ch, mid) for ch in range(6)]
            for k in range(2):
                speed[k, z, to, :] = begin[k, z, at, :]
            for k in range(3):
                state[k, z, to, :] = begin[2 + k, z, at, :]
            mass, act, conc = [still[k, z, at, :] for k in (1, 3, 4)]
            mass = 0.5 * mass
            forced[0, z, at, :] = act * (conc * f[0] - mass * f[4])
            forced[1, z, at, :] = act * (conc * f[1] - mass * f[5])
            forced[2, z, at, :] = f[2]
            forced[3, z, at, :] = f[3]

    tail = FRONT + height
    for z in range(3):
        for k in range(2):
            speed[k, z, tail : tail + 8, :] = blank
        for k in range(3):
            state[k, z, 0:8, :] = blank

    lane = lanes(8)
    ends_at = [lane == k for k in (BX - 1, BX // 2 - 1, 0, BX // 2)]
    at127, at63, at0, at64 = ends_at

    def rows_of(r):
        row = 8 * r
        return pl.ds(row, 8), pl.ds(row + FRONT, 8), pl.ds(row + FRONT + 1, 8), pl.ds(row + FRONT - 1, 8)

    def stresses(r):
        at, to, up1, _ = rows_of(r)
        u = [speed[0, z, to, :] for z in range(3)]
        v = [speed[1, z, to, :] for z in range(3)]

        def north(k, x):
            return x[1], speed[k, 0, up1, :], roll(jnp.where(mid, x[2], speed[k, 2, up1, :]), BX // 2)

        un, vn = north(0, u), north(1, v)
        ue = east_of(*u, at127, at63)
        ve = east_of(*v, at127, at63)
        for z in range(3):
            sxx = ue[z] - u[z]
            syy = vn[z] - v[z]
            shear = (un[z] - u[z]) + (ve[z] - v[z])
            div, ten = sxx + syy, sxx - syy
            twice = div + div
            inv = lax.rsqrt(twice * twice + (ten * ten + shear * shear) + 1.0)
            hard = still[0, z, at, :]
            kr = hard * inv
            half = 0.5 * kr
            state[0, z, to, :] = (state[0, z, to, :] * (2.0 / 3.0) - hard) + kr * twice
            state[1, z, to, :] = state[1, z, to, :] * (2.0 / 3.0) + half * ten
            state[2, z, to, :] = state[2, z, to, :] * (2.0 / 3.0) + half * shear

    def speeds(r):
        at, to, _, down1 = rows_of(r)
        s1, s2, s12 = [[state[k, z, to, :] for z in range(3)] for k in range(3)]
        a = [x + y for x, y in zip(s1, s2)]
        c = [x - y for x, y in zip(s1, s2)]
        aw = west_of(*a, at0, at64)
        sw = west_of(*s12, at0, at64)

        def south(x, lower):
            return lower(1), x[0], roll(jnp.where(mid, lower(2), x[2]), BX // 2)

        ss = south(s12, lambda z: state[2, z, down1, :])
        cs = south(c, lambda z: state[0, z, down1, :] - state[1, z, down1, :])
        for z in range(3):
            u, v = speed[0, z, to, :], speed[1, z, to, :]
            fx = (a[z] - aw[z]) + (s12[z] - ss[z])
            fy = (s12[z] - sw[z]) + (c[z] - cs[z])
            m2, base = still[1, z, at, :], still[2, z, at, :]
            cx, cy = forced[2, z, at, :], forced[3, z, at, :]
            dx, dy = cx - u, cy - v
            y2 = dx * dx + dy * dy + DRAG_FLOOR
            drag = base * (y2 * lax.rsqrt(y2))
            part = still[3, z, at, :] * (1.0 / (jnp.maximum(m2, 1.0) + drag))
            mc = (0.5 * CORIO) * m2
            speed[0, z, to, :] = part * (m2 * u + fx + forced[0, z, at, :] + drag * cx + mc * v)
            speed[1, z, to, :] = part * (m2 * v + fy + forced[1, z, at, :] + drag * cy - mc * u)

    def subcycle(_, carry):
        for r in range(tiles):
            stresses(r)
        for r in range(tiles):
            speeds(r)
        return carry

    lax.fori_loop(0, NSUB, subcycle, 0)

    for r in range(tiles):
        at = slice(8 * r, 8 * r + 8)
        to = slice(FRONT + 8 * r, FRONT + 8 * r + 8)
        for y in range(2):
            base = still[2, y, at, :]
            dx = speed[0, y, to, :] - forced[2, y, at, :]
            dy = speed[1, y, to, :] - forced[3, y, at, :]
            y2 = dx * dx + dy * dy + DRAG_FLOOR
            factor = base * (y2 * lax.rsqrt(y2))
            for k, x in enumerate((factor * dx, factor * dy, base * (1.0 / CW))):
                out8[pl.ds(8 * r * REPLY + 2 * k + y, 8, stride=REPLY), :] = x
    for y in range(2):
        for k in range(2):
            moved[k, :, y * BX : (y + 1) * BX] = speed[k, y, FRONT + 2 : FRONT + 2 + count, :]

    def answer(o, _):
        for j in range(per):
            b = (ids[o, j] + 2) * REPLY
            back[o, 6 * j : 6 * j + 6, :] = out8[pl.ds(b, 6), :]
        return 0

    lax.fori_loop(0, n, answer, 0)


def ice_step(ids, recv, begin, still):
    n, per = ids.shape[0], ids.shape[1] // 3
    count = n * per
    height = (count + 4 + 7) // 8 * 8
    tall = height + 2 * FRONT
    scratch = [
        (height * STEP + 8, BX), (height, BX), (height, BX),
        (2, 3, tall, BX), (3, 3, tall, BX), (4, 3, height, BX), (height * REPLY + 8, BX),
    ]
    return pl.pallas_call(
        functools.partial(ice_kernel, n, per, count),
        out_shape=[f32(n, 6 * per, BX), f32(2, count, 2 * BX)],
        in_specs=[SMEM] + [VMEM] * 3,
        out_specs=[VMEM] * 2,
        scratch_shapes=[pltpu.VMEM(s, jnp.float32) for s in scratch],
        compiler_params=params(12),
        name="ice_step",
    )(ids, recv, begin, still)


def final_kernel(n, per, got, opened, moved, out):
    is_ocean = lax.axis_index("comp") == 0

    @pl.when(is_ocean)
    def _():
        def tile(t, _):
            for y in range(2):
                cells = slice(y * BX, (y + 1) * BX)
                gx, gy, gc = [got[t, pl.ds(2 * k + y, per, stride=6), :] for k in range(3)]
                out[0, t, :, cells] = gx + (1.0 - gc) * opened[t, 2 * y]
                out[1, t, :, cells] = gy + (1.0 - gc) * opened[t, 2 * y + 1]
            return 0

        lax.fori_loop(0, n, tile, 0)

    @pl.when(jnp.logical_not(is_ocean))
    def _():
        out[...] = moved[...]


def final(got, opened, moved):
    n, _, per, _ = opened.shape
    return pl.pallas_call(
        functools.partial(final_kernel, n, per),
        out_shape=f32(2, n, per, 2 * BX),
        in_specs=[VMEM] * 3,
        out_specs=VMEM,
        compiler_params=params(8),
        name="final",
    )(got, opened, moved)


def per_device(fields, block_owner, ice_covered, land_mask):
    nlat, nlon = lax.axis_size("lat"), lax.axis_size("lon")
    n = nlat * nlon
    count = block_owner.shape[0]
    per = count // n
    side = lax.axis_index("comp")
    fields = fields[0]
    local = (block_owner % count).reshape(nlat, nlon, per)
    ids = jnp.concatenate([local, jnp.roll(local, 1, 1), jnp.roll(local, -1, 1)], 2).reshape(n, 3 * per)
    split = fields.reshape(7, n, per, 2 * BX)
    pay, opened, active, ends = first(
        split, block_owner.reshape(1, count), ice_covered.reshape(1, count), land_mask, nlat, nlon
    )
    pay = lax.ppermute(pay, "comp", [(0, 1), (1, 0)])
    def everyone(x):
        return lax.all_to_all(x, ("lat", "lon"), split_axis=0, concat_axis=0, tiled=True)

    def ice_side(pay, ids, active, ends):
        recv = everyone(pay)
        ring = [(i, (i + 1) % nlon) for i in range(nlon)]
        west = lax.ppermute(ends, "lon", ring)
        east = lax.ppermute(ends, "lon", [(j, i) for i, j in ring])
        sides, north, south = ice_rows(fields, active, west, east)
        line = [(i, i + 1) for i in range(nlat - 1)]
        below = lax.ppermute(north, "lat", line)
        above = lax.ppermute(south, "lat", [(j, i) for i, j in line])
        return recv, ids, sides, below, above

    def ocean_side(pay, ids, active, ends):
        row = ends[:34]
        return jnp.zeros(pay.shape, jnp.float32), everyone(ids), ends, row, row

    recv, owner, sides, below, above = lax.cond(side == 1, ice_side, ocean_side, pay, ids, active, ends)
    swap = lax.ppermute(owner, "comp", [(0, 1), (1, 0)])
    begin, still = prep(fields, active, sides, below, above)
    back, moved = ice_step(swap, recv, begin, still)
    back = lax.cond(side == 1, everyone, lambda x: x, back)
    got = lax.ppermute(back, "comp", [(0, 1), (1, 0)])
    out = final(got, opened, moved.reshape(2, n, per, 2 * BX))
    return out.reshape(1, 2, count, 2 * BX)


def solution(mesh):
    placed = (
        P("comp", None, ("lat", "lon"), None),
        P(("lat", "lon")),
        P(("lat", "lon")),
        P(("lat", "lon"), None),
    )
    return jax.shard_map(
        per_device,
        mesh=mesh,
        in_specs=placed,
        out_specs=P("comp", None, ("lat", "lon"), None),
        check_vma=False,
    )
```

time: 59.3 us -> 54.9 us (0.926)
  waiting for transfers between devices: 21 us -> 10.6 us
  starting transfers between devices: 19.3 us -> 27.6 us
  Pallas kernels: 12.2 us -> 10.1 us
    ppermute x2, waiting for transfers between devices: 15.2 us -> 3.39 us  [the longest x1 2.04 us: per_device(): pay = lax.ppermute(pay, 'comp', [(0, 1), (1, 0)])]
    ppermute x2, starting transfers between devices: 3.63 us -> 13.5 us  [the longest x1 13.4 us: per_device(): got = lax.ppermute(back, 'comp', [(0, 1), (1, 0)])]
    pallas_call x1, Pallas kernels: 6.75 us -> 4.93 us  [ice_step(): pl.pallas_call(functools.partial(ice_kernel, n, per, count), out_shape=[f...]
    ppermute x1, starting transfers between devices: 7.35 us -> 5.75 us  [per_device(): swap = lax.ppermute(owner, 'comp', [(0, 1), (1, 0)])]
    all_to_all x1, waiting for transfers between devices: 5.81 us -> 7.17 us  [everyone(): lax.all_to_all(x, ('lat', 'lon'), split_axis=0, concat_axis=0, tiled=True)]
where the time goes in v4:
time: 54.9 us; the launch traced here: 54.5 us
  starting transfers between devices  27.6 us (50%)
  waiting for transfers between devices  10.6 us (19%)
  Pallas kernels  10.1 us (18%)
  local copies, waits for them, and re-layouts  5.42 us (10%)
  other arithmetic  0.7 us (1%)
    ppermute x1, starting transfers between devices, per_device(): got = lax.ppermute(back, 'comp', [(0, 1), (1, 0)])  13.4 us
    all_to_all x1, starting transfers between devices, everyone(): lax.all_to_all(x, ('lat', 'lon'), split_axis=0, concat_axis=0, tiled=True)  8.34 us
    all_to_all x1, waiting for transfers between devices, everyone(): lax.all_to_all(x, ('lat', 'lon'), split_axis=0, concat_axis=0, tiled=True)  7.17 us
    ppermute x1, starting transfers between devices, per_device(): swap = lax.ppermute(owner, 'comp', [(0, 1), (1, 0)])  5.75 us
    pallas_call x1, Pallas kernels, ice_step(): pl.pallas_call(functools.partial(ice_kernel, n, per, count), out_shape=[f...  4.93 us
    pallas_call x1, Pallas kernels, first(): pl.pallas_call(functools.partial(first_kernel, nlat, nlon, per), out_shap...  3.08 us
    unnamed x8, local copies, waits for them, and re-layouts  2.22 us
    ppermute x1, waiting for transfers between devices, per_device(): pay = lax.ppermute(pay, 'comp', [(0, 1), (1, 0)])  2.04 us
  transfers between devices with their start and end apart: 4, of which 3 were waited for; matrix products, arithmetic and copies ran while one was open for 5% of the time, Pallas kernels for 2%

profile of v4, /device:TPU:0, one launch (start us, length us, event | category | flops | bytes accessed | tf_op | source)
XLA Modules:
  0.0 54.5 jit_solution(16971733560437372375)
XLA Ops:
  0.0 0.0 copy-start
  0.0 0.9 %copy-done = s32[128,256]{1,0:T(8,128)S(1)} copy-done((s32[128,256]{1,0:T(8,128)S(1)}, s32[128,256]{1,0:T(8,128)}, u32[]{:S(2)}) %copy-start) | copy-done | bytes 131096
  0.9 0.0 copy-start.1
  0.9 0.7 %copy-done.1 = s32[128]{0:T(128)S(1)} copy-done((s32[128]{0:T(128)S(1)}, s32[128]{0:T(128)}, u32[]{:S(2)}) %copy-start.1) | copy-done | bytes 536
  1.6 0.0 copy-start.2
  1.6 0.7 %copy-done.2 = s32[128]{0:T(128)S(1)} copy-done((s32[128]{0:T(128)S(1)}, s32[128]{0:T(128)}, u32[]{:S(2)}) %copy-start.2) | copy-done | bytes 536
  2.2 0.0 copy-start.3
  2.2 3.1 %first.1 = (f32[16,144,128]{2,1,0:T(8,128)S(1)}, f32[16,4,8,128]{3,2,1,0:T(8,128)S(1)}, f32[128,256]{1,0:T(8,128)S(1)}, f32[128,128]{1,0:T(8,128)S(1)}) custom-call(f32[7,16,8,256]{3,2,1,0:T(8,128)} %bitcast.13, s32[1,128]{1,0:T(1,128)S(1)} %bitcast.12, s32[1,128]{1,0:T(1,128)S(1)} %bitcast.11, s32[128,256]{1,0:T(8,128)S(1)} %copy-done), custom_call_target="tpu_custom_call" | custom-call | tf_op jit(solution)/shard_map/first/pallas_call | solution.py:177
  5.3 0.1 collective-permute-start.4
  5.4 0.1 reshape.22
  5.5 0.1 concatenate.18
  5.6 0.7 %pad_add_fusion.2 = s32[16,24]{1,0:T(8,128)} fusion(s32[16,8]{1,0:T(8,128)S(1)} %bitcast.17, s32[16,8]{1,0:T(8,128)S(1)} %bitcast.16, s32[16,8]{1,0:T(8,128)S(1)} %concatenate.18), kind=kLoop, calls=%fused_computation.2 | loop fusion | flops 768 | bytes 3072 | tf_op jit(solution)/shard_map/concatenate | solution.py:505
  6.3 2.0 %collective-permute-done.4 = f32[16,144,128]{2,1,0:T(8,128)} collective-permute-done((f32[16,144,128]{2,1,0:T(8,128)S(1)}, f32[16,144,128]{2,1,0:T(8,128)}, u32[]{:S(2)}, u32[]{:S(2)}) %collective-permute-start.4) | collective-permute-done | bytes 1179680 | tf_op jit(solution)/shard_map/ppermute | solution.py:510
  8.4 0.0 copy-done.3
  8.4 18.5 %conditional.2 = (f32[16,144,128]{2,1,0:T(8,128)}, s32[16,24]{1,0:T(8,128)S(1)}, f32[128,128]{1,0:T(8,128)S(1)}, f32[34,128]{1,0:T(8,128)}, f32[34,128]{1,0:T(8,128)}) conditional(s32[]{:T(128)} %convert_element_type.4, (s32[16,24]{1,0:T(8,128)}, f32[128,128]{1,0:T(8,128)S(1)}) %tuple.19, (f32[16,144,128]{2,1,0:T(8,128)}, f32[128,128]{1,0:T(8,128)S(1)}, ...), branch_computations={%region_0.1_spmd, %region_1.2_spmd} | conditional | bytes 4205800 | solution.py:529
  8.4 8.3 %all-to-all-start = ((s32[16,1,24]{2,1,0:T(1,128)}), s32[16,1,24]{2,1,0:T(1,128)S(1)}, u32[]{:S(2)}, u32[]{:S(2)}) async-start(s32[16,1,24]{2,1,0:T(1,128)} %bitcast), calls=%async_computation | async-start | bytes 16384 | tf_op jit(solution)/shard_map/cond/branch_0_fun/all_to_all | solution.py:512
  16.7 0.6 %slice.14 = f32[34,128]{1,0:T(8,128)} slice(f32[128,128]{1,0:T(8,128)S(1)} %get-tuple-element.68), slice={[0:34], [0:128]} | slice | bytes 34816 | tf_op jit(solution)/shard_map/cond/branch_0_fun/slice | solution.py:526
  17.3 1.3 %copy.9 = f32[34,128]{1,0:T(8,128)} copy(f32[34,128]{1,0:T(8,128)} %slice.14) | data formatting | bytes 34816 | tf_op jit(solution)/shard_map/cond
  18.6 7.2 %all-to-all-done = s32[16,1,24]{2,1,0:T(1,128)S(1)} async-done(((s32[16,1,24]{2,1,0:T(1,128)}), s32[16,1,24]{2,1,0:T(1,128)S(1)}, u32[]{:S(2)}, u32[]{:S(2)}) %all-to-all-start) | async-done | bytes 1568 | tf_op jit(solution)/shard_map/cond/branch_0_fun/all_to_all | solution.py:512
  25.8 1.1 %broadcast.7 = f32[16,144,128]{2,1,0:T(8,128)} broadcast(f32[]{:T(128)} %constant.18.clone), dimensions={} | broadcast | bytes 1179652 | tf_op jit(solution)/shard_map/broadcast.3
  26.9 5.8 %collective-permute-start.5 = (s32[16,24]{1,0:T(8,128)S(1)}, s32[16,24]{1,0:T(8,128)S(1)}, u32[]{:S(2)}, u32[]{:S(2)}) collective-permute-start(s32[16,24]{1,0:T(8,128)S(1)} %get-tuple-element.50), channel_id=1, source_target_pairs={{0,16},{16,0},{1,17},{17,1},{2,18},{18,2},{3,19},{19,3},{4,20},{20... | collective-permute-start | bytes 4616 | tf_op jit(solution)/shard_map/ppermute | solution.py:530
  32.6 1.3 %prep.1 = (f32[5,3,136,128]{3,2,1,0:T(8,128)S(1)}, f32[5,3,136,128]{3,2,1,0:T(8,128)S(1)}) custom-call(f32[7,128,256]{2,1,0:T(8,128)S(1)} %bitcast.15, f32[128,256]{1,0:T(8,128)S(1)} %get-tuple-element.49.active, f32[128,128]{1,0:T(8,128)S(1)} %get-tuple-element.52.sides, f32[34,128]{1,0:T(8,128)} %get-tuple-element.53.below, f32[34,128]{1,0:T(8,128)} %get-tuple-element.54.above), custom_call_target="tpu_custom_call" | custom-call | tf_op jit(solution)/shard_map/prep/pallas_call | solution.py:265
  33.9 0.0 collective-permute-done.5.ids
  33.9 4.9 %ice_step.1 = (f32[16,48,128]{2,1,0:T(8,128)S(1)}, f32[2,128,256]{2,1,0:T(8,128)S(1)}) custom-call(s32[16,24]{1,0:T(8,128)S(1)} %collective-permute-done.5.ids, f32[16,144,128]{2,1,0:T(8,128)} %get-tuple-element.51.recv, f32[5,3,136,128]{3,2,1,0:T(8,128)S(1)} %get-tuple-element.55.begin, f32[5,3,136,128]{3,2,1,0:T(8,128)S(1)} %get-tuple-element.56.still), custom_call_target="tpu_custom_call" | custom-call | tf_op jit(solution)/shard_map/ice_step/pallas_call | solution.py:454
  38.9 13.4 %collective-permute-start.6 = (f32[16,48,128]{2,1,0:T(8,128)S(1)}, f32[16,48,128]{2,1,0:T(8,128)S(1)}, u32[]{:S(2)}, u32[]{:S(2)}) collective-permute-start(f32[16,48,128]{2,1,0:T(8,128)S(1)} %get-tuple-element.76), channel_id=1, source_target_pairs={{0,16},{16,0},{1,17},{17,1},{2,18},{18,2},{3,19},{19,3},{4,20},{20... | collective-permute-start | bytes 1179656 | tf_op jit(solution)/shard_map/ppermute | solution.py:534
  52.3 1.3 %collective-permute-done.6.got = f32[16,48,128]{2,1,0:T(8,128)S(1)} collective-permute-done((f32[16,48,128]{2,1,0:T(8,128)S(1)}, f32[16,48,128]{2,1,0:T(8,128)S(1)}, u32[]{:S(2)}, u32[]{:S(2)}) %collective-permute-start.6) | collective-permute-done | bytes 393248 | tf_op jit(solution)/shard_map/ppermute | solution.py:534
  53.7 0.8 %final.1 = f32[2,16,8,256]{3,2,1,0:T(8,128)} custom-call(f32[16,48,128]{2,1,0:T(8,128)S(1)} %collective-permute-done.6.got, f32[16,4,8,128]{3,2,1,0:T(8,128)S(1)} %get-tuple-element.58.opened, f32[2,16,8,256]{3,2,1,0:T(8,128)S(1)} %bitcast.10), custom_call_target="tpu_custom_call" | custom-call | tf_op jit(solution)/shard_map/final/pallas_call | solution.py:487
  (5 shorter events, 0.1 us)
Async XLA Ops:
  0.0 0.9 %copy-start = (s32[128,256]{1,0:T(8,128)S(1)}, s32[128,256]{1,0:T(8,128)}, u32[]{:S(2)}) copy-start(s32[128,256]{1,0:T(8,128)} %land_in.1) | copy-start | bytes 393220
  0.9 0.7 %copy-start.1 = (s32[128]{0:T(128)S(1)}, s32[128]{0:T(128)}, u32[]{:S(2)}) copy-start(s32[128]{0:T(128)} %param.10) | copy-start | bytes 1540
  1.6 0.7 %copy-start.2 = (s32[128]{0:T(128)S(1)}, s32[128]{0:T(128)}, u32[]{:S(2)}) copy-start(s32[128]{0:T(128)} %param.9) | copy-start | bytes 1540
  2.2 6.1 %copy-start.3 = (f32[1,7,128,256]{3,2,1,0:T(8,128)S(1)}, f32[1,7,128,256]{3,2,1,0:T(8,128)}, u32[]{:S(2)}) copy-start(f32[1,7,128,256]{3,2,1,0:T(8,128)} %param.8) | copy-start | bytes 2752516
  5.3 3.0 %collective-permute-start.4 = (f32[16,144,128]{2,1,0:T(8,128)S(1)}, f32[16,144,128]{2,1,0:T(8,128)}, u32[]{:S(2)}, u32[]{:S(2)}) collective-permute-start(f32[16,144,128]{2,1,0:T(8,128)S(1)} %get-tuple-element.48), channel_id=1, source_target_pairs={{0,16},{16,0},{1,17},{17,1},{2,18},{18,2},{3,19},{19,3},{4,20},{20... | collective-permute-start | bytes 3538952 | tf_op jit(solution)/shard_map/ppermute | solution.py:510
  8.4 17.4 %all-to-all-start = ((s32[16,1,24]{2,1,0:T(1,128)}), s32[16,1,24]{2,1,0:T(1,128)S(1)}, u32[]{:S(2)}, u32[]{:S(2)}) async-start(s32[16,1,24]{2,1,0:T(1,128)} %bitcast), calls=%async_computation | async-start | bytes 16384 | tf_op jit(solution)/shard_map/cond/branch_0_fun/all_to_all | solution.py:512
  26.9 7.0 %collective-permute-start.5 = (s32[16,24]{1,0:T(8,128)S(1)}, s32[16,24]{1,0:T(8,128)S(1)}, u32[]{:S(2)}, u32[]{:S(2)}) collective-permute-start(s32[16,24]{1,0:T(8,128)S(1)} %get-tuple-element.50), channel_id=1, source_target_pairs={{0,16},{16,0},{1,17},{17,1},{2,18},{18,2},{3,19},{19,3},{4,20},{20... | collective-permute-start | bytes 4616 | tf_op jit(solution)/shard_map/ppermute | solution.py:530
  38.9 14.8 %collective-permute-start.6 = (f32[16,48,128]{2,1,0:T(8,128)S(1)}, f32[16,48,128]{2,1,0:T(8,128)S(1)}, u32[]{:S(2)}, u32[]{:S(2)}) collective-permute-start(f32[16,48,128]{2,1,0:T(8,128)S(1)} %get-tuple-element.76), channel_id=1, source_target_pairs={{0,16},{16,0},{1,17},{17,1},{2,18},{18,2},{3,19},{19,3},{4,20},{20... | collective-permute-start | bytes 1179656 | tf_op jit(solution)/shard_map/ppermute | solution.py:534

commit v5 on v4

--- a/solution.py
+++ b/solution.py
@@ -52,11 +52,19 @@
     return jnp.concatenate(parts, 0) if len(parts) > 1 else parts[0]
 
 
-def pack_body(nlat, nlon, per, count, raw, owner, pay, opened, edge, rim, idb, parts, field):
+def steps(lo, hi, body):
+    if hi - lo <= 32:
+        for k in range(lo, hi):
+            body(k, 0)
+    else:
+        lax.fori_loop(lo, hi, body, 0)
+
+
+def pack_body(nlat, nlon, per, count, raw, owner, pay, opened, edge, rim, parts, field):
     n = nlat * nlon
-    idb[...] = jnp.broadcast_to(column(owner[...]), (count, BX)).astype(jnp.int32)
     lane = lanes(per)
     group = lane // 8
+    slot = lax.broadcasted_iota(jnp.int32, (per, BX), 0)
     lat_base = 13 * per
 
     def tile(t, _):
@@ -81,8 +89,9 @@
             pay[t, pl.ds(p, per, stride=12), :] = planes[p]
             ends = jnp.where(group == p, roll(planes[p], 8 * p + 4), ends)
         edge[t] = ends
-        spot = t * per
-        ids = idb[pl.ds(pl.multiple_of(spot, per), per), :] - t * count
+        ids = jnp.zeros((per, BX), jnp.int32)
+        for j in range(per):
+            ids = jnp.where(slot == j, owner[0, t * per + j] - t * count, ids)
 
         def pick(block, value):
             return jnp.sum(jnp.where(ids == block, value, 0.0), axis=0, keepdims=True)
@@ -97,7 +106,7 @@
 
     for c in range(parts):
         field(c).wait()
-        lax.fori_loop(c * (n // parts), (c + 1) * (n // parts), tile, 0)
+        steps(c * (n // parts), (c + 1) * (n // parts), tile)
 
     def dest(d, _):
         i, j = d // nlon, d % nlon
@@ -115,10 +124,20 @@
             pay[d, lat_base + c : lat_base + c + 2, :] = corner * scale
         return 0
 
-    lax.fori_loop(0, n, dest, 0)
-
-
-def ends_body(ice, covered, land, active, ends):
+    steps(0, n, dest)
+
+
+def ends_kernel(nlat, nlon, per, ice, covered, land, owner, active, ends, ids):
+    def tile(t, _):
+        i, j = t // nlon, t % nlon
+        near = [t, i * nlon + (j + nlon - 1) % nlon, i * nlon + (j + 1) % nlon]
+        for k, other in enumerate(near):
+            for slot in range(per):
+                ids[t, k * per + slot] = owner[0, other * per + slot] - other * (nlat * nlon * per)
+        return 0
+
+    steps(0, nlat * nlon, tile)
+
     count = covered.shape[1]
     lane = lanes(count)
     group = lane // 8
@@ -129,14 +148,13 @@
         act = cover * (1 - land[:, cells]).astype(jnp.float32)
         active[:, cells] = act
         for ch in range(8):
-            x = act if ch == 7 else ice[ch, :, :, cells].reshape(count, BX)
+            x = act if ch == 7 else ice[ch, :, cells]
             p = 2 * ch + y
             total = jnp.where(group == p, roll(x, 8 * p + 4), total)
     ends[...] = total
 
 
-def first_kernel(nlat, nlon, per, raw_in, owner_in, cover_in, land_in, pay, opened, active, ends,
-                 raw, owner, cover, land, edge, rim, idb, sems):
+def pack_kernel(nlat, nlon, per, raw_in, owner, pay, opened, raw, edge, rim, sems):
     n = nlat * nlon
     parts = PARTS if n % PARTS == 0 else 1
     step = n // parts
@@ -145,53 +163,43 @@
         at = pl.ds(c * step, step)
         return pltpu.make_async_copy(raw_in.at[:, at], raw.at[:, at], sems.at[c])
 
-    is_ocean = lax.axis_index("comp") == 0
-
-    @pl.when(is_ocean)
+    @pl.when(lax.axis_index("comp") == 0)
     def _():
-        ids = pltpu.make_async_copy(owner_in, owner, sems.at[PARTS])
-        ids.start()
         for c in range(parts):
             field(c).start()
-        ids.wait()
-        pack_body(nlat, nlon, per, n * per, raw, owner, pay, opened, edge, rim, idb, parts, field)
-
-    @pl.when(jnp.logical_not(is_ocean))
-    def _():
-        mask = pltpu.make_async_copy(land_in, land, sems.at[PARTS + 1])
-        blocks = pltpu.make_async_copy(cover_in, cover, sems.at[PARTS + 2])
-        blocks.start()
-        mask.start()
-        for c in range(parts):
-            field(c).start()
-        blocks.wait()
-        mask.wait()
-        for c in range(parts):
-            field(c).wait()
-        ends_body(raw, cover, land, active, ends)
-
-
-def first(raw, owner, covered, land, nlat, nlon):
-    _, n, per, cells = raw.shape
-    count = n * per
+        pack_body(nlat, nlon, per, n * per, raw, owner, pay, opened, edge, rim, parts, field)
+
+
+def pack(raw, owner, nlat, nlon):
+    _, n, per, _ = raw.shape
     return pl.pallas_call(
-        functools.partial(first_kernel, nlat, nlon, per),
-        out_shape=[f32(n, 13 * per + 40, BX), f32(n, 4, per, BX), f32(count, cells), f32(count, BX)],
-        in_specs=[pl.BlockSpec(memory_space=pltpu.HBM)] * 4,
-        out_specs=[VMEM] * 4,
+        functools.partial(pack_kernel, nlat, nlon, per),
+        out_shape=[f32(n, 13 * per + 40, BX), f32(n, 4, per, BX)],
+        in_specs=[pl.BlockSpec(memory_space=pltpu.HBM), SMEM],
+        out_specs=[VMEM] * 2,
         scratch_shapes=[
             pltpu.VMEM(raw.shape, jnp.float32),
-            pltpu.VMEM((1, count), jnp.int32),
-            pltpu.VMEM((1, count), jnp.int32),
-            pltpu.VMEM((count, cells), jnp.int32),
             pltpu.VMEM((n, per, BX), jnp.float32),
             pltpu.VMEM((n, 40, BX), jnp.float32),
-            pltpu.VMEM((count, BX), jnp.int32),
-            pltpu.SemaphoreType.DMA((PARTS + 3,)),
+            pltpu.SemaphoreType.DMA((PARTS,)),
         ],
         compiler_params=params(12),
-        name="first",
-    )(raw, owner, covered, land)
+        name="pack",
+    )(raw, owner)
+
+
+def ice_ends(ice, covered, land, owner, nlat, nlon):
+    count = land.shape[0]
+    n = nlat * nlon
+    per = count // n
+    return pl.pallas_call(
+        functools.partial(ends_kernel, nlat, nlon, per),
+        out_shape=[f32(count, 2 * BX), f32(count, BX), jax.ShapeDtypeStruct((n, 3 * per), jnp.int32)],
+        in_specs=[VMEM] * 3 + [SMEM],
+        out_specs=[VMEM] * 2 + [SMEM],
+        compiler_params=params(8),
+        name="ice_ends",
+    )(ice, covered, land, owner)
 
 
 def rows_kernel(ice, active, west, east, sides, north, south):
@@ -230,23 +238,25 @@
     return jnp.where(mid, odd, roll(ends, -(16 * ch + 4)))
 
 
-def prep_kernel(count, height, ice, active, sides, below, above, begin, still, grid):
+def prep_kernel(count, height, ice, active, sides, below_in, above_in, recv_in, begin, still, recv,
+                grid, below, above, sems):
+    copies = [
+        pltpu.make_async_copy(x, y, sems.at[k])
+        for k, (x, y) in enumerate(((below_in, below), (above_in, above), (recv_in, recv)))
+    ]
+    for copy in copies:
+        copy.start()
     mid, mid2 = middle(count), middle(2)
     pad = jnp.zeros((height - count - 4, BX), jnp.float32)
     for ch in range(8):
         for y in range(2):
             cells = slice(y * BX, (y + 1) * BX)
             grid[ch, y, 2 : 2 + count, :] = active[:, cells] if ch == 7 else ice[ch, :, cells]
-            p = 2 * ch + y
-            for lo, msg in ((0, below), (count + 2, above)):
-                grid[ch, y, lo : lo + 2, :] = msg[2 * p : 2 * p + 2, :]
         grid[ch, 2, 2 : 2 + count, :] = side_plane(sides[...], ch, mid)
-        for lo, msg in ((0, below), (count + 2, above)):
-            grid[ch, 2, lo : lo + 2, :] = side_plane(msg[32:34, :], ch, mid2)
         for z in range(3):
             grid[ch, z, count + 4 :, :] = pad
 
-    for r in range(height // 8):
+    def convert(r):
         at = slice(8 * r, 8 * r + 8)
         for z in range(3):
             u, v, mass, conc, s1, s2, s12, act = [grid[ch, z, at, :] for ch in range(8)]
@@ -258,19 +268,40 @@
             still[3, z, at, :] = act
             still[4, z, at, :] = conc
 
-
-def prep(ice, active, sides, below, above):
+    outer = [0] + list(range((count + 2) // 8, height // 8))
+    for r in range(height // 8):
+        if r not in outer:
+            convert(r)
+    copies[0].wait()
+    copies[1].wait()
+    for lo, msg in ((0, below), (count + 2, above)):
+        for ch in range(8):
+            for y in range(2):
+                p = 2 * ch + y
+                grid[ch, y, lo : lo + 2, :] = msg[2 * p : 2 * p + 2, :]
+            grid[ch, 2, lo : lo + 2, :] = side_plane(msg[32:34, :], ch, mid2)
+    for r in outer:
+        convert(r)
+    copies[2].wait()
+
+
+def prep(ice, active, sides, below, above, recv):
     count = active.shape[0]
     height = (count + 4 + 7) // 8 * 8
     return pl.pallas_call(
         functools.partial(prep_kernel, count, height),
-        out_shape=[f32(5, 3, height, BX)] * 2,
-        in_specs=[VMEM] * 5,
-        out_specs=[VMEM] * 2,
-        scratch_shapes=[pltpu.VMEM((8, 3, height, BX), jnp.float32)],
+        out_shape=[f32(5, 3, height, BX)] * 2 + [f32(*recv.shape)],
+        in_specs=[VMEM] * 3 + [pl.BlockSpec(memory_space=pl.ANY)] * 3,
+        out_specs=[VMEM] * 3,
+        scratch_shapes=[
+            pltpu.VMEM((8, 3, height, BX), jnp.float32),
+            pltpu.VMEM(below.shape, jnp.float32),
+            pltpu.VMEM(above.shape, jnp.float32),
+            pltpu.SemaphoreType.DMA((3,)),
+        ],
         compiler_params=params(12),
         name="prep",
-    )(ice, active, sides, below, above)
+    )(ice, active, sides, below, above, recv)
 
 
 def east_of(even, odd, side, at127, at63):
@@ -501,13 +532,12 @@
     per = count // n
     side = lax.axis_index("comp")
     fields = fields[0]
-    local = (block_owner % count).reshape(nlat, nlon, per)
-    ids = jnp.concatenate([local, jnp.roll(local, 1, 1), jnp.roll(local, -1, 1)], 2).reshape(n, 3 * per)
     split = fields.reshape(7, n, per, 2 * BX)
-    pay, opened, active, ends = first(
-        split, block_owner.reshape(1, count), ice_covered.reshape(1, count), land_mask, nlat, nlon
-    )
+    owner = block_owner.reshape(1, count)
+    pay, opened = pack(split, owner, nlat, nlon)
     pay = lax.ppermute(pay, "comp", [(0, 1), (1, 0)])
+    active, ends, ids = ice_ends(fields, ice_covered.reshape(1, count), land_mask, owner, nlat, nlon)
+
     def everyone(x):
         return lax.all_to_all(x, ("lat", "lon"), split_axis=0, concat_axis=0, tiled=True)
 
@@ -526,9 +556,9 @@
         row = ends[:34]
         return jnp.zeros(pay.shape, jnp.float32), everyone(ids), ends, row, row
 
-    recv, owner, sides, below, above = lax.cond(side == 1, ice_side, ocean_side, pay, ids, active, ends)
-    swap = lax.ppermute(owner, "comp", [(0, 1), (1, 0)])
-    begin, still = prep(fields, active, sides, below, above)
+    recv, owned, sides, below, above = lax.cond(side == 1, ice_side, ocean_side, pay, ids, active, ends)
+    swap = lax.ppermute(owned, "comp", [(0, 1), (1, 0)])
+    begin, still, recv = prep(fields, active, sides, below, above, recv)
     back, moved = ice_step(swap, recv, begin, still)
     back = lax.cond(side == 1, everyone, lambda x: x, back)
     got = lax.ppermute(back, "comp", [(0, 1), (1, 0)])

time: 54.9 us -> 53.6 us (0.976)
  waiting for transfers between devices: 10.6 us -> 7.18 us
  starting transfers between devices: 27.6 us -> 29.3 us
  Pallas kernels: 10.1 us -> 10.8 us
  other arithmetic: 0.7 us -> 0 us
    ppermute x1, waiting for transfers between devices: 2.04 us -> 0.01 us  [per_device(): pay = lax.ppermute(pay, 'comp', [(0, 1), (1, 0)])]
    ppermute x1, starting transfers between devices: 5.75 us -> 7.39 us  [per_device(): swap = lax.ppermute(owned, 'comp', [(0, 1), (1, 0)])]
    all_to_all x1, waiting for transfers between devices: 7.17 us -> 5.83 us  [everyone(): lax.all_to_all(x, ('lat', 'lon'), split_axis=0, concat_axis=0, tiled=True)]
    pallas_call x1 -> x2, Pallas kernels: 3.08 us -> 4.01 us  [the longest x1 2.36 us: pack(): pl.pallas_call(functools.partial(pack_kernel, nlat, nlon, per), out_shape...]
    concatenate x2 -> x0, other arithmetic: 0.69 us -> none  [the longest x1 0.68 us: per_device(): jnp.concatenate([local, jnp.roll(local, 1, 1), jnp.roll(local, -1, 1)], 2)]
    unnamed x8 -> x10, local copies, waits for them, and re-layouts: 2.22 us -> 2.87 us
    pallas_call x1, Pallas kernels: 4.93 us -> 4.32 us  [ice_step(): pl.pallas_call(functools.partial(ice_kernel, n, per, count), out_shape=[f...]
  transfers between devices with their start and end apart: 4 -> 4, of which waited for: 3 -> 2; matrix products, arithmetic and copies ran while one was open for 5% -> 4% of each run, Pallas kernels for 2% -> 6%
where the time goes in v5:
time: 53.6 us; the launch traced here: 53.2 us
  starting transfers between devices  29.3 us (55%)
  Pallas kernels  10.8 us (20%)
  waiting for transfers between devices  7.18 us (13%)
  local copies, waits for them, and re-layouts  5.91 us (11%)
    ppermute x1, starting transfers between devices, per_device(): got = lax.ppermute(back, 'comp', [(0, 1), (1, 0)])  13.5 us
    all_to_all x1, starting transfers between devices, everyone(): lax.all_to_all(x, ('lat', 'lon'), split_axis=0, concat_axis=0, tiled=True)  8.35 us
    ppermute x1, starting transfers between devices, per_device(): swap = lax.ppermute(owned, 'comp', [(0, 1), (1, 0)])  7.39 us
    all_to_all x1, waiting for transfers between devices, everyone(): lax.all_to_all(x, ('lat', 'lon'), split_axis=0, concat_axis=0, tiled=True)  5.83 us
    pallas_call x1, Pallas kernels, ice_step(): pl.pallas_call(functools.partial(ice_kernel, n, per, count), out_shape=[f...  4.32 us
    unnamed x10, local copies, waits for them, and re-layouts  2.87 us
    pallas_call x1, Pallas kernels, pack(): pl.pallas_call(functools.partial(pack_kernel, nlat, nlon, per), out_shape...  2.36 us
    pallas_call x1, Pallas kernels, ice_ends(): pl.pallas_call(functools.partial(ends_kernel, nlat, nlon, per), out_shape...  1.64 us
  transfers between devices with their start and end apart: 4, of which 2 were waited for; matrix products, arithmetic and copies ran while one was open for 4% of the time, Pallas kernels for 6%

profile of v5, /device:TPU:0, one launch (start us, length us, event | category | flops | bytes accessed | tf_op | source)
XLA Modules:
  0.0 53.2 jit_solution(6907682202379768424)
XLA Ops:
  0.0 0.0 copy-start.1
  0.0 0.7 %copy-done.1 = s32[128]{0:T(128)S(1)} copy-done((s32[128]{0:T(128)S(1)}, s32[128]{0:T(128)}, u32[]{:S(2)}) %copy-start.1) | copy-done | bytes 536
  0.7 0.0 copy-start.4
  0.7 2.4 %pack.1 = (f32[16,144,128]{2,1,0:T(8,128)S(1)}, f32[16,4,8,128]{3,2,1,0:T(8,128)S(1)}) custom-call(f32[7,16,8,256]{3,2,1,0:T(8,128)} %bitcast.12, s32[1,128]{1,0:T(1,128)S(1)} %bitcast.9), custom_call_target="tpu_custom_call" | custom-call | tf_op jit(solution)/shard_map/pack/pallas_call | solution.py:175
  3.0 0.1 collective-permute-start.4
  3.1 0.0 copy-done.4
  3.1 0.0 copy-start
  3.1 0.9 %copy-done = s32[128,256]{1,0:T(8,128)S(1)} copy-done((s32[128,256]{1,0:T(8,128)S(1)}, s32[128,256]{1,0:T(8,128)}, u32[]{:S(2)}) %copy-start) | copy-done | bytes 131096
  4.0 0.0 copy-start.2
  4.0 0.7 %copy-done.2 = s32[128]{0:T(128)S(1)} copy-done((s32[128]{0:T(128)S(1)}, s32[128]{0:T(128)}, u32[]{:S(2)}) %copy-start.2) | copy-done | bytes 536
  4.7 0.0 copy-start.3
  4.7 0.7 %copy-done.3 = s32[128]{0:T(128)S(1)} copy-done((s32[128]{0:T(128)S(1)}, s32[128]{0:T(128)}, u32[]{:S(2)}) %copy-start.3) | copy-done | bytes 536
  5.3 1.6 %ice_ends.1 = (f32[128,256]{1,0:T(8,128)S(1)}, f32[128,128]{1,0:T(8,128)S(1)}, s32[16,24]{1,0:T(8,128)}) custom-call(f32[7,128,256]{2,1,0:T(8,128)S(1)} %bitcast.13, s32[1,128]{1,0:T(1,128)S(1)} %bitcast.11, s32[128,256]{1,0:T(8,128)S(1)} %copy-done, s32[1,128]{1,0:T(1,128)S(1)} %bitcast.10), custom_call_target="tpu_custom_call" | custom-call | tf_op jit(solution)/shard_map/ice_ends/pallas_call | solution.py:195
  7.0 0.0 collective-permute-done.4
  7.0 17.2 %conditional.2 = (f32[16,144,128]{2,1,0:T(8,128)}, s32[16,24]{1,0:T(8,128)S(1)}, f32[128,128]{1,0:T(8,128)S(1)}, f32[34,128]{1,0:T(8,128)}, f32[34,128]{1,0:T(8,128)}) conditional(s32[]{:T(128)} %convert_element_type.4, (s32[16,24]{1,0:T(8,128)}, f32[128,128]{1,0:T(8,128)S(1)}) %tuple.19, (f32[16,144,128]{2,1,0:T(8,128)}, f32[128,128]{1,0:T(8,128)S(1)}, ...), branch_computations={%region_0.0_spmd, %region_1.0_spmd} | conditional | bytes 4205800 | solution.py:559
  7.0 8.4 %all-to-all-start = ((s32[16,1,24]{2,1,0:T(1,128)}), s32[16,1,24]{2,1,0:T(1,128)S(1)}, u32[]{:S(2)}, u32[]{:S(2)}) async-start(s32[16,1,24]{2,1,0:T(1,128)} %bitcast), calls=%async_computation | async-start | bytes 16384 | tf_op jit(solution)/shard_map/cond/branch_0_fun/all_to_all | solution.py:542
  15.4 0.6 %slice.2 = f32[34,128]{1,0:T(8,128)} slice(f32[128,128]{1,0:T(8,128)S(1)} %get-tuple-element.66), slice={[0:34], [0:128]} | slice | bytes 34816 | tf_op jit(solution)/shard_map/cond/branch_0_fun/slice | solution.py:556
  16.0 1.3 %copy.9 = f32[34,128]{1,0:T(8,128)} copy(f32[34,128]{1,0:T(8,128)} %slice.2) | data formatting | bytes 34816 | tf_op jit(solution)/shard_map/cond
  17.3 5.8 %all-to-all-done = s32[16,1,24]{2,1,0:T(1,128)S(1)} async-done(((s32[16,1,24]{2,1,0:T(1,128)}), s32[16,1,24]{2,1,0:T(1,128)S(1)}, u32[]{:S(2)}, u32[]{:S(2)}) %all-to-all-start) | async-done | bytes 1568 | tf_op jit(solution)/shard_map/cond/branch_0_fun/all_to_all | solution.py:542
  23.2 1.1 %broadcast.2 = f32[16,144,128]{2,1,0:T(8,128)} broadcast(f32[]{:T(128)} %constant.2.clone), dimensions={} | broadcast | bytes 1179652 | tf_op jit(solution)/shard_map/broadcast.1
  24.2 7.4 %collective-permute-start.5 = (s32[16,24]{1,0:T(8,128)S(1)}, s32[16,24]{1,0:T(8,128)S(1)}, u32[]{:S(2)}, u32[]{:S(2)}) collective-permute-start(s32[16,24]{1,0:T(8,128)S(1)} %get-tuple-element.53), channel_id=1, source_target_pairs={{0,16},{16,0},{1,17},{17,1},{2,18},{18,2},{3,19},{19,3},{4,20},{20... | collective-permute-start | bytes 4616 | tf_op jit(solution)/shard_map/ppermute | solution.py:560
  31.6 1.6 %prep.1 = (f32[5,3,136,128]{3,2,1,0:T(8,128)S(1)}, f32[5,3,136,128]{3,2,1,0:T(8,128)S(1)}, f32[16,144,128]{2,1,0:T(8,128)S(1)}) custom-call(f32[7,128,256]{2,1,0:T(8,128)S(1)} %bitcast.15, f32[128,256]{1,0:T(8,128)S(1)} %get-tuple-element.52.active, f32[128,128]{1,0:T(8,128)S(1)} %get-tuple-element.54.sides, f32[34,128]{1,0:T(8,128)} %get-tuple-element.55.below_in, ...), custom_call_target="tpu_custom_call" | custom-call | tf_op jit(solution)/shard_map/prep/pallas_call | solution.py:291
  33.3 0.0 collective-permute-done.5.ids
  33.3 4.3 %ice_step.1 = (f32[16,48,128]{2,1,0:T(8,128)S(1)}, f32[2,128,256]{2,1,0:T(8,128)S(1)}) custom-call(s32[16,24]{1,0:T(8,128)S(1)} %collective-permute-done.5.ids, f32[16,144,128]{2,1,0:T(8,128)S(1)} %get-tuple-element.58.recv, f32[5,3,136,128]{3,2,1,0:T(8,128)S(1)} %get-tuple-element.59.begin, f32[5,3,136,128]{3,2,1,0:T(8,128)S(1)} %get-tuple-element.60.still), custom_call_target="tpu_custom_call" | custom-call | tf_op jit(solution)/shard_map/ice_step/pallas_call | solution.py:485
  37.6 13.5 %collective-permute-start.6 = (f32[16,48,128]{2,1,0:T(8,128)S(1)}, f32[16,48,128]{2,1,0:T(8,128)S(1)}, u32[]{:S(2)}, u32[]{:S(2)}) collective-permute-start(f32[16,48,128]{2,1,0:T(8,128)S(1)} %get-tuple-element.74), channel_id=1, source_target_pairs={{0,16},{16,0},{1,17},{17,1},{2,18},{18,2},{3,19},{19,3},{4,20},{20... | collective-permute-start | bytes 1179656 | tf_op jit(solution)/shard_map/ppermute | solution.py:564
  51.1 1.3 %collective-permute-done.6.got = f32[16,48,128]{2,1,0:T(8,128)S(1)} collective-permute-done((f32[16,48,128]{2,1,0:T(8,128)S(1)}, f32[16,48,128]{2,1,0:T(8,128)S(1)}, u32[]{:S(2)}, u32[]{:S(2)}) %collective-permute-start.6) | collective-permute-done | bytes 393248 | tf_op jit(solution)/shard_map/ppermute | solution.py:564
  52.4 0.8 %final.1 = f32[2,16,8,256]{3,2,1,0:T(8,128)} custom-call(f32[16,48,128]{2,1,0:T(8,128)S(1)} %collective-permute-done.6.got, f32[16,4,8,128]{3,2,1,0:T(8,128)S(1)} %get-tuple-element.62.opened, f32[2,16,8,256]{3,2,1,0:T(8,128)S(1)} %bitcast.8), custom_call_target="tpu_custom_call" | custom-call | tf_op jit(solution)/shard_map/final/pallas_call | solution.py:518
  (1 shorter events, 0.0 us)
Async XLA Ops:
  0.0 0.7 %copy-start.1 = (s32[128]{0:T(128)S(1)}, s32[128]{0:T(128)}, u32[]{:S(2)}) copy-start(s32[128]{0:T(128)} %param.9) | copy-start | bytes 1540
  0.7 2.5 %copy-start.4 = (f32[1,7,128,256]{3,2,1,0:T(8,128)S(1)}, f32[1,7,128,256]{3,2,1,0:T(8,128)}, u32[]{:S(2)}) copy-start(f32[1,7,128,256]{3,2,1,0:T(8,128)} %param.8) | copy-start | bytes 2752516
  3.0 4.0 %collective-permute-start.4 = (f32[16,144,128]{2,1,0:T(8,128)S(1)}, f32[16,144,128]{2,1,0:T(8,128)}, u32[]{:S(2)}, u32[]{:S(2)}) collective-permute-start(f32[16,144,128]{2,1,0:T(8,128)S(1)} %get-tuple-element.51), channel_id=1, source_target_pairs={{0,16},{16,0},{1,17},{17,1},{2,18},{18,2},{3,19},{19,3},{4,20},{20... | collective-permute-start | bytes 3538952 | tf_op jit(solution)/shard_map/ppermute | solution.py:538
  3.1 0.9 %copy-start = (s32[128,256]{1,0:T(8,128)S(1)}, s32[128,256]{1,0:T(8,128)}, u32[]{:S(2)}) copy-start(s32[128,256]{1,0:T(8,128)} %land.1) | copy-start | bytes 393220
  4.0 0.7 %copy-start.2 = (s32[128]{0:T(128)S(1)}, s32[128]{0:T(128)}, u32[]{:S(2)}) copy-start(s32[128]{0:T(128)} %param.9) | copy-start | bytes 1540
  4.7 0.7 %copy-start.3 = (s32[128]{0:T(128)S(1)}, s32[128]{0:T(128)}, u32[]{:S(2)}) copy-start(s32[128]{0:T(128)} %param.10) | copy-start | bytes 1540
  7.0 16.1 %all-to-all-start = ((s32[16,1,24]{2,1,0:T(1,128)}), s32[16,1,24]{2,1,0:T(1,128)S(1)}, u32[]{:S(2)}, u32[]{:S(2)}) async-start(s32[16,1,24]{2,1,0:T(1,128)} %bitcast), calls=%async_computation | async-start | bytes 16384 | tf_op jit(solution)/shard_map/cond/branch_0_fun/all_to_all | solution.py:542
  24.2 9.0 %collective-permute-start.5 = (s32[16,24]{1,0:T(8,128)S(1)}, s32[16,24]{1,0:T(8,128)S(1)}, u32[]{:S(2)}, u32[]{:S(2)}) collective-permute-start(s32[16,24]{1,0:T(8,128)S(1)} %get-tuple-element.53), channel_id=1, source_target_pairs={{0,16},{16,0},{1,17},{17,1},{2,18},{18,2},{3,19},{19,3},{4,20},{20... | collective-permute-start | bytes 4616 | tf_op jit(solution)/shard_map/ppermute | solution.py:560
  37.6 14.8 %collective-permute-start.6 = (f32[16,48,128]{2,1,0:T(8,128)S(1)}, f32[16,48,128]{2,1,0:T(8,128)S(1)}, u32[]{:S(2)}, u32[]{:S(2)}) collective-permute-start(f32[16,48,128]{2,1,0:T(8,128)S(1)} %get-tuple-element.74), channel_id=1, source_target_pairs={{0,16},{16,0},{1,17},{17,1},{2,18},{18,2},{3,19},{19,3},{4,20},{20... | collective-permute-start | bytes 1179656 | tf_op jit(solution)/shard_map/ppermute | solution.py:564

commit v6 on v5

--- a/solution.py
+++ b/solution.py
@@ -127,17 +127,7 @@
     steps(0, n, dest)
 
 
-def ends_kernel(nlat, nlon, per, ice, covered, land, owner, active, ends, ids):
-    def tile(t, _):
-        i, j = t // nlon, t % nlon
-        near = [t, i * nlon + (j + nlon - 1) % nlon, i * nlon + (j + 1) % nlon]
-        for k, other in enumerate(near):
-            for slot in range(per):
-                ids[t, k * per + slot] = owner[0, other * per + slot] - other * (nlat * nlon * per)
-        return 0
-
-    steps(0, nlat * nlon, tile)
-
+def ends_kernel(ice, covered, land, active, ends):
     count = covered.shape[1]
     lane = lanes(count)
     group = lane // 8
@@ -188,18 +178,41 @@
     )(raw, owner)
 
 
-def ice_ends(ice, covered, land, owner, nlat, nlon):
+def ice_ends(ice, covered, land):
     count = land.shape[0]
-    n = nlat * nlon
-    per = count // n
-    return pl.pallas_call(
-        functools.partial(ends_kernel, nlat, nlon, per),
-        out_shape=[f32(count, 2 * BX), f32(count, BX), jax.ShapeDtypeStruct((n, 3 * per), jnp.int32)],
-        in_specs=[VMEM] * 3 + [SMEM],
-        out_specs=[VMEM] * 2 + [SMEM],
+    return pl.pallas_call(
+        ends_kernel,
+        out_shape=[f32(count, 2 * BX), f32(count, BX)],
+        in_specs=[VMEM] * 3,
+        out_specs=[VMEM] * 2,
         compiler_params=params(8),
         name="ice_ends",
-    )(ice, covered, land, owner)
+    )(ice, covered, land)
+
+
+def table_kernel(nlat, nlon, per, owner, ids):
+    def tile(t, _):
+        i, j = t // nlon, t % nlon
+        near = [t, i * nlon + (j + nlon - 1) % nlon, i * nlon + (j + 1) % nlon]
+        for k, other in enumerate(near):
+            for slot in range(per):
+                ids[t, k * per + slot] = owner[0, other * per + slot] - other * (nlat * nlon * per)
+        return 0
+
+    steps(0, nlat * nlon, tile)
+
+
+def table(owner, nlat, nlon):
+    n = nlat * nlon
+    per = owner.shape[1] // n
+    return pl.pallas_call(
+        functools.partial(table_kernel, nlat, nlon, per),
+        out_shape=jax.ShapeDtypeStruct((n, 3 * per), jnp.int32),
+        in_specs=[SMEM],
+        out_specs=SMEM,
+        compiler_params=params(4),
+        name="table",
+    )(owner)
 
 
 def rows_kernel(ice, active, west, east, sides, north, south):
@@ -238,70 +251,64 @@
     return jnp.where(mid, odd, roll(ends, -(16 * ch + 4)))
 
 
-def prep_kernel(count, height, ice, active, sides, below_in, above_in, recv_in, begin, still, recv,
-                grid, below, above, sems):
-    copies = [
-        pltpu.make_async_copy(x, y, sems.at[k])
-        for k, (x, y) in enumerate(((below_in, below), (above_in, above), (recv_in, recv)))
-    ]
-    for copy in copies:
-        copy.start()
-    mid, mid2 = middle(count), middle(2)
-    pad = jnp.zeros((height - count - 4, BX), jnp.float32)
+def statics(mass, conc, act):
+    return mass * jnp.exp(CSTAR * (conc - 1.0)) * act * (1.0 / 6.0), 2.0 * mass, CW * conc * act, act, conc
+
+
+def prep_kernel(count, height, ice, active, sides, begin, still, grid):
+    mid = middle(count)
     for ch in range(8):
         for y in range(2):
             cells = slice(y * BX, (y + 1) * BX)
             grid[ch, y, 2 : 2 + count, :] = active[:, cells] if ch == 7 else ice[ch, :, cells]
         grid[ch, 2, 2 : 2 + count, :] = side_plane(sides[...], ch, mid)
         for z in range(3):
-            grid[ch, z, count + 4 :, :] = pad
-
-    def convert(r):
+            grid[ch, z, 0:2, :] = jnp.zeros((2, BX), jnp.float32)
+            grid[ch, z, count + 2 :, :] = jnp.zeros((height - count - 2, BX), jnp.float32)
+
+    for r in range(height // 8):
         at = slice(8 * r, 8 * r + 8)
         for z in range(3):
             u, v, mass, conc, s1, s2, s12, act = [grid[ch, z, at, :] for ch in range(8)]
             for k, x in enumerate((u, v, 0.5 * s1, 0.5 * s2, s12)):
                 begin[k, z, at, :] = x
-            still[0, z, at, :] = mass * jnp.exp(CSTAR * (conc - 1.0)) * act * (1.0 / 6.0)
-            still[1, z, at, :] = 2.0 * mass
-            still[2, z, at, :] = CW * conc * act
-            still[3, z, at, :] = act
-            still[4, z, at, :] = conc
-
-    outer = [0] + list(range((count + 2) // 8, height // 8))
-    for r in range(height // 8):
-        if r not in outer:
-            convert(r)
-    copies[0].wait()
-    copies[1].wait()
-    for lo, msg in ((0, below), (count + 2, above)):
-        for ch in range(8):
-            for y in range(2):
-                p = 2 * ch + y
-                grid[ch, y, lo : lo + 2, :] = msg[2 * p : 2 * p + 2, :]
-            grid[ch, 2, lo : lo + 2, :] = side_plane(msg[32:34, :], ch, mid2)
-    for r in outer:
-        convert(r)
-    copies[2].wait()
-
-
-def prep(ice, active, sides, below, above, recv):
+            for k, x in enumerate(statics(mass, conc, act)):
+                still[k, z, at, :] = x
+
+
+def prep(ice, active, sides):
     count = active.shape[0]
     height = (count + 4 + 7) // 8 * 8
     return pl.pallas_call(
         functools.partial(prep_kernel, count, height),
-        out_shape=[f32(5, 3, height, BX)] * 2 + [f32(*recv.shape)],
-        in_specs=[VMEM] * 3 + [pl.BlockSpec(memory_space=pl.ANY)] * 3,
-        out_specs=[VMEM] * 3,
-        scratch_shapes=[
-            pltpu.VMEM((8, 3, height, BX), jnp.float32),
-            pltpu.VMEM(below.shape, jnp.float32),
-            pltpu.VMEM(above.shape, jnp.float32),
-            pltpu.SemaphoreType.DMA((3,)),
-        ],
+        out_shape=[f32(5, 3, height, BX)] * 2,
+        in_specs=[VMEM] * 3,
+        out_specs=[VMEM] * 2,
+        scratch_shapes=[pltpu.VMEM((8, 3, height, BX), jnp.float32)],
         compiler_params=params(12),
         name="prep",
-    )(ice, active, sides, below, above, recv)
+    )(ice, active, sides)
+
+
+def fetch_kernel(*refs):
+    k = len(refs) // 2
+    copies = [pltpu.make_async_copy(refs[i], refs[k + i], refs[-1].at[i]) for i in range(k)]
+    for copy in copies:
+        copy.start()
+    for copy in copies:
+        copy.wait()
+
+
+def fetch(*arrays):
+    return pl.pallas_call(
+        fetch_kernel,
+        out_shape=[f32(*x.shape) for x in arrays],
+        in_specs=[pl.BlockSpec(memory_space=pl.ANY)] * len(arrays),
+        out_specs=[VMEM] * len(arrays),
+        scratch_shapes=[pltpu.SemaphoreType.DMA((len(arrays),))],
+        compiler_params=params(4),
+        name="fetch",
+    )(*arrays)
 
 
 def east_of(even, odd, side, at127, at63):
@@ -316,8 +323,8 @@
     return jnp.where(at0, s, e), jnp.where(at0, roll(side, -63), o), wide
 
 
-def ice_kernel(n, per, count, ids, recv, begin, still, back, moved,
-               spot, hw, he, speed, state, forced, out8):
+def ice_kernel(n, per, count, ids, recv, begin, fixed, below, above, back, moved,
+               spot, hw, he, speed, state, forced, out8, still):
     tiles = (count + 4 + 7) // 8
     height = tiles * 8
     blank = jnp.zeros((8, BX), jnp.float32)
@@ -352,20 +359,41 @@
         ref[1:2, :] = rim[38:39]
         ref[0:1, :] = rim[39:40]
 
-    q, mid = (lanes(8) % 8) < 4, middle(8)
+    q, mid, mid2 = (lanes(8) % 8) < 4, middle(8), middle(2)
     for r in range(tiles):
         at = slice(8 * r, 8 * r + 8)
         to = slice(FRONT + 8 * r, FRONT + 8 * r + 8)
+        for z in range(3):
+            for k in range(2):
+                speed[k, z, to, :] = begin[k, z, at, :]
+            for k in range(3):
+                state[k, z, to, :] = begin[2 + k, z, at, :]
+            for k in range(5):
+                still[k, z, at, :] = fixed[k, z, at, :]
+    for lo, msg in ((0, below), (count + 2, above)):
+        at, to = slice(lo, lo + 2), slice(FRONT + lo, FRONT + lo + 2)
+        for z in range(3):
+            if z < 2:
+                raw = [msg[4 * ch + 2 * z : 4 * ch + 2 * z + 2, :] for ch in range(8)]
+            else:
+                raw = [side_plane(msg[32:34, :], ch, mid2) for ch in range(8)]
+            u, v, mass, conc, s1, s2, s12, act = raw
+            speed[0, z, to, :] = u
+            speed[1, z, to, :] = v
+            state[0, z, to, :] = 0.5 * s1
+            state[1, z, to, :] = 0.5 * s2
+            state[2, z, to, :] = s12
+            for k, x in enumerate(statics(mass, conc, act)):
+                still[k, z, at, :] = x
+
+    for r in range(tiles):
+        at = slice(8 * r, 8 * r + 8)
         ends = jnp.where(q, hw[at, :], he[at, :])
         for z in range(3):
             if z < 2:
                 f = [spot[pl.ds(8 * r * STEP + 2 * ch + z, 8, stride=STEP), :] for ch in range(6)]
             else:
                 f = [side_plane(ends, ch, mid) for ch in range(6)]
-            for k in range(2):
-                speed[k, z, to, :] = begin[k, z, at, :]
-            for k in range(3):
-                state[k, z, to, :] = begin[2 + k, z, at, :]
             mass, act, conc = [still[k, z, at, :] for k in (1, 3, 4)]
             mass = 0.5 * mass
             forced[0, z, at, :] = act * (conc * f[0] - mass * f[4])
@@ -473,24 +501,24 @@
     lax.fori_loop(0, n, answer, 0)
 
 
-def ice_step(ids, recv, begin, still):
+def ice_step(ids, recv, begin, fixed, below, above):
     n, per = ids.shape[0], ids.shape[1] // 3
     count = n * per
     height = (count + 4 + 7) // 8 * 8
     tall = height + 2 * FRONT
     scratch = [
         (height * STEP + 8, BX), (height, BX), (height, BX),
-        (2, 3, tall, BX), (3, 3, tall, BX), (4, 3, height, BX), (height * REPLY + 8, BX),
+        (2, 3, tall, BX), (3, 3, tall, BX), (4, 3, height, BX), (height * REPLY + 8, BX), (5, 3, height, BX),
     ]
     return pl.pallas_call(
         functools.partial(ice_kernel, n, per, count),
         out_shape=[f32(n, 6 * per, BX), f32(2, count, 2 * BX)],
-        in_specs=[SMEM] + [VMEM] * 3,
+        in_specs=[SMEM] + [VMEM] * 5,
         out_specs=[VMEM] * 2,
         scratch_shapes=[pltpu.VMEM(s, jnp.float32) for s in scratch],
-        compiler_params=params(12),
+        compiler_params=params(16),
         name="ice_step",
-    )(ids, recv, begin, still)
+    )(ids, recv, begin, fixed, below, above)
 
 
 def final_kernel(n, per, got, opened, moved, out):
@@ -536,13 +564,14 @@
     owner = block_owner.reshape(1, count)
     pay, opened = pack(split, owner, nlat, nlon)
     pay = lax.ppermute(pay, "comp", [(0, 1), (1, 0)])
-    active, ends, ids = ice_ends(fields, ice_covered.reshape(1, count), land_mask, owner, nlat, nlon)
-
     def everyone(x):
         return lax.all_to_all(x, ("lat", "lon"), split_axis=0, concat_axis=0, tiled=True)
 
-    def ice_side(pay, ids, active, ends):
+    height = (count + 4 + 7) // 8 * 8
+
+    def ice_side(pay, fields, covered, land, owner):
         recv = everyone(pay)
+        active, ends = ice_ends(fields, covered, land)
         ring = [(i, (i + 1) % nlon) for i in range(nlon)]
         west = lax.ppermute(ends, "lon", ring)
         east = lax.ppermute(ends, "lon", [(j, i) for i, j in ring])
@@ -550,16 +579,20 @@
         line = [(i, i + 1) for i in range(nlat - 1)]
         below = lax.ppermute(north, "lat", line)
         above = lax.ppermute(south, "lat", [(j, i) for i, j in line])
-        return recv, ids, sides, below, above
-
-    def ocean_side(pay, ids, active, ends):
-        row = ends[:34]
-        return jnp.zeros(pay.shape, jnp.float32), everyone(ids), ends, row, row
-
-    recv, owned, sides, below, above = lax.cond(side == 1, ice_side, ocean_side, pay, ids, active, ends)
+        begin, fixed = prep(fields, active, sides)
+        return recv, jnp.zeros((n, 3 * per), jnp.int32), below, above, begin, fixed
+
+    def ocean_side(pay, fields, covered, land, owner):
+        row = jnp.zeros((34, BX), jnp.float32)
+        blank = jnp.zeros((5, 3, height, BX), jnp.float32)
+        return jnp.zeros(pay.shape, jnp.float32), everyone(table(owner, nlat, nlon)), row, row, blank, blank
+
+    recv, owned, below, above, begin, fixed = lax.cond(
+        side == 1, ice_side, ocean_side, pay, fields, ice_covered.reshape(1, count), land_mask, owner
+    )
     swap = lax.ppermute(owned, "comp", [(0, 1), (1, 0)])
-    begin, still, recv = prep(fields, active, sides, below, above, recv)
-    back, moved = ice_step(swap, recv, begin, still)
+    recv, below, above = fetch(recv, below, above)
+    back, moved = ice_step(swap, recv, begin, fixed, below, above)
     back = lax.cond(side == 1, everyone, lambda x: x, back)
     got = lax.ppermute(back, "comp", [(0, 1), (1, 0)])
     out = final(got, opened, moved.reshape(2, n, per, 2 * BX))

time: 53.6 us -> 51.4 us (0.959)
  blocking collectives: 0 us -> 16.1 us
  starting transfers between devices: 29.3 us -> 17.8 us
  local copies, waits for them, and re-layouts: 5.91 us -> 2.42 us
  waiting for transfers between devices: 7.18 us -> 4.31 us
    all_to_all x0 -> x1, blocking collectives: none -> 16.1 us  [everyone(): lax.all_to_all(x, ('lat', 'lon'), split_axis=0, concat_axis=0, tiled=True)]
    all_to_all x1 -> x0, starting transfers between devices: 8.35 us -> none  [everyone(): lax.all_to_all(x, ('lat', 'lon'), split_axis=0, concat_axis=0, tiled=True)]
    all_to_all x1 -> x0, waiting for transfers between devices: 5.83 us -> none  [everyone(): lax.all_to_all(x, ('lat', 'lon'), split_axis=0, concat_axis=0, tiled=True)]
    ppermute x1, starting transfers between devices: 7.39 us -> 4.3 us  [per_device(): swap = lax.ppermute(owned, 'comp', [(0, 1), (1, 0)])]
    ppermute x1, waiting for transfers between devices: 0.01 us -> 2.96 us  [per_device(): pay = lax.ppermute(pay, 'comp', [(0, 1), (1, 0)])]
    unnamed x10 -> x0, local copies, waits for them, and re-layouts: 2.87 us -> none
    cond x1 -> x0, local copies, waits for them, and re-layouts: 1.34 us -> none
    another operation x1 -> x5, local copies, waits for them, and re-layouts: 1.09 us -> 2.42 us
  transfers between devices with their start and end apart: 4 -> 3, of which waited for: 2 -> 2; matrix products, arithmetic and copies ran while one was open for 4% -> 0% of each run, Pallas kernels for 6% -> 3%
where the time goes in v6:
time: 51.4 us; the launch traced here: 51.1 us
  starting transfers between devices  17.8 us (35%)
  blocking collectives  16.1 us (31%)
  Pallas kernels  10.4 us (20%)
  waiting for transfers between devices  4.31 us (8%)
  local copies, waits for them, and re-layouts  2.42 us (5%)
    all_to_all x1, blocking collectives, everyone(): lax.all_to_all(x, ('lat', 'lon'), split_axis=0, concat_axis=0, tiled=True)  16.1 us
    ppermute x1, starting transfers between devices, per_device(): got = lax.ppermute(back, 'comp', [(0, 1), (1, 0)])  13.4 us
    ppermute x1, starting transfers between devices, per_device(): swap = lax.ppermute(owned, 'comp', [(0, 1), (1, 0)])  4.3 us
    pallas_call x1, Pallas kernels, ice_step(): pl.pallas_call(functools.partial(ice_kernel, n, per, count), out_shape=[f...  4.2 us
    ppermute x1, waiting for transfers between devices, per_device(): pay = lax.ppermute(pay, 'comp', [(0, 1), (1, 0)])  2.96 us
    pallas_call x1, Pallas kernels, pack(): pl.pallas_call(functools.partial(pack_kernel, nlat, nlon, per), out_shape...  2.49 us
    another operation x5, local copies, waits for them, and re-layouts  2.42 us
    pallas_call x1, Pallas kernels, table(): pl.pallas_call(functools.partial(table_kernel, nlat, nlon, per), out_shap...  1.6 us
  transfers between devices with their start and end apart: 3, of which 2 were waited for; matrix products, arithmetic and copies ran while one was open for 0% of the time, Pallas kernels for 3%

profile of v6, /device:TPU:0, one launch (start us, length us, event | category | flops | bytes accessed | tf_op | source)
XLA Modules:
  0.0 51.1 jit_solution(14081298894634624112)
XLA Ops:
  0.0 2.5 %pack.1 = (f32[16,144,128]{2,1,0:T(8,128)S(1)}, f32[16,4,8,128]{3,2,1,0:T(8,128)S(1)}) custom-call(f32[7,16,8,256]{3,2,1,0:T(8,128)} %bitcast.12, s32[1,128]{1,0:T(1,128)} %bitcast.17), custom_call_target="tpu_custom_call" | custom-call | tf_op jit(solution)/shard_map/pack/pallas_call | solution.py:165
  2.5 0.1 collective-permute-start.4
  2.6 3.0 %collective-permute-done.4 = f32[16,144,128]{2,1,0:T(8,128)} collective-permute-done((f32[16,144,128]{2,1,0:T(8,128)S(1)}, f32[16,144,128]{2,1,0:T(8,128)}, u32[]{:S(2)}, u32[]{:S(2)}) %collective-permute-start.4) | collective-permute-done | bytes 1179680 | tf_op jit(solution)/shard_map/ppermute | solution.py:566
  5.5 20.1 %conditional.2 = (f32[16,144,128]{2,1,0:T(8,128)}, s32[16,24]{1,0:T(8,128)S(1)}, f32[34,128]{1,0:T(8,128)}, f32[34,128]{1,0:T(8,128)}, f32[5,3,136,128]{3,2,1,0:T(8,128)S(1)}, /*index=5*/f32[5,3,136,128]{3,2,1,0:T(8,128)S(1)}) conditional(s32[]{:T(128)} %convert_element_type.4, s32[1,128]{1,0:T(1,128)} %bitcast.18, (f32[16,144,128]{2,1,0:T(8,128)}, ...), branch_computations={%region_0.0_spmd, %region_1.0_spmd} | conditional | bytes 8400712 | solution.py:590
  5.5 1.6 %table.1 = s32[16,24]{1,0:T(8,128)S(1)} custom-call(s32[1,128]{1,0:T(1,128)} %owner), custom_call_target="tpu_custom_call" | custom-call | tf_op jit(solution)/shard_map/cond/branch_0_fun/table/pallas_call | solution.py:208
  7.1 16.1 %all_to_all.17 = s32[16,1,24]{2,1,0:T(1,128)S(1)} all-to-all(s32[16,1,24]{2,1,0:T(1,128)S(1)} %bitcast.11), channel_id=1, replica_groups=mesh['comp'=2,'lat'=4,'lon'=4] {'lat','lon'}, dimensions={0} | all-to-all | bytes 3072 | tf_op jit(solution)/shard_map/cond/branch_0_fun/all_to_all | solution.py:568
  23.2 0.6 %broadcast.9.clone = f32[34,128]{1,0:T(8,128)} broadcast(f32[]{:T(128)} %constant.4.clone), dimensions={} | broadcast | bytes 17412 | tf_op jit(solution)/shard_map/broadcast.4
  23.8 0.6 %broadcast.9 = f32[34,128]{1,0:T(8,128)} broadcast(f32[]{:T(128)} %constant.4.clone), dimensions={} | broadcast | bytes 17412 | tf_op jit(solution)/shard_map/broadcast.4
  24.5 0.1 broadcast.10.clone
  24.5 0.1 broadcast.10
  24.6 1.1 %broadcast.8 = f32[16,144,128]{2,1,0:T(8,128)} broadcast(f32[]{:T(128)} %constant.4.clone), dimensions={} | broadcast | bytes 1179652 | tf_op jit(solution)/shard_map/broadcast.5
  25.7 4.3 %collective-permute-start.5 = (s32[16,24]{1,0:T(8,128)S(1)}, s32[16,24]{1,0:T(8,128)S(1)}, u32[]{:S(2)}, u32[]{:S(2)}) collective-permute-start(s32[16,24]{1,0:T(8,128)S(1)} %get-tuple-element.46), channel_id=1, source_target_pairs={{0,16},{16,0},{1,17},{17,1},{2,18},{18,2},{3,19},{19,3},{4,20},{20... | collective-permute-start | bytes 4616 | tf_op jit(solution)/shard_map/ppermute | solution.py:593
  30.0 1.3 %fetch.1 = (f32[16,144,128]{2,1,0:T(8,128)S(1)}, f32[34,128]{1,0:T(8,128)S(1)}, f32[34,128]{1,0:T(8,128)S(1)}) custom-call(f32[16,144,128]{2,1,0:T(8,128)} %get-tuple-element.47.refs_0_, f32[34,128]{1,0:T(8,128)} %get-tuple-element.48.refs_1_, f32[34,128]{1,0:T(8,128)} %get-tuple-element.49.refs_2_), custom_call_target="tpu_custom_call" | custom-call | tf_op jit(solution)/shard_map/fetch/pallas_call | solution.py:303
  31.3 0.0 collective-permute-done.5.ids
  31.3 4.2 %ice_step.1 = (f32[16,48,128]{2,1,0:T(8,128)S(1)}, f32[2,128,256]{2,1,0:T(8,128)S(1)}) custom-call(s32[16,24]{1,0:T(8,128)S(1)} %collective-permute-done.5.ids, f32[16,144,128]{2,1,0:T(8,128)S(1)} %get-tuple-element.50.recv, f32[5,3,136,128]{3,2,1,0:T(8,128)S(1)} %get-tuple-element.51.begin, f32[5,3,136,128]{3,2,1,0:T(8,128)S(1)} %get-tuple-element.52.fixed, ...), custom_call_target="tpu_custom_call" | custom-call | tf_op jit(solution)/shard_map/ice_step/pallas_call | solution.py:513
  35.5 13.4 %collective-permute-start.6 = (f32[16,48,128]{2,1,0:T(8,128)S(1)}, f32[16,48,128]{2,1,0:T(8,128)S(1)}, u32[]{:S(2)}, u32[]{:S(2)}) collective-permute-start(f32[16,48,128]{2,1,0:T(8,128)S(1)} %get-tuple-element.74), channel_id=1, source_target_pairs={{0,16},{16,0},{1,17},{17,1},{2,18},{18,2},{3,19},{19,3},{4,20},{20... | collective-permute-start | bytes 1179656 | tf_op jit(solution)/shard_map/ppermute | solution.py:597
  48.9 1.3 %collective-permute-done.6.got = f32[16,48,128]{2,1,0:T(8,128)S(1)} collective-permute-done((f32[16,48,128]{2,1,0:T(8,128)S(1)}, f32[16,48,128]{2,1,0:T(8,128)S(1)}, u32[]{:S(2)}, u32[]{:S(2)}) %collective-permute-start.6) | collective-permute-done | bytes 393248 | tf_op jit(solution)/shard_map/ppermute | solution.py:597
  50.3 0.8 %final.1 = f32[2,16,8,256]{3,2,1,0:T(8,128)} custom-call(f32[16,48,128]{2,1,0:T(8,128)S(1)} %collective-permute-done.6.got, f32[16,4,8,128]{3,2,1,0:T(8,128)S(1)} %get-tuple-element.56.opened, f32[2,16,8,256]{3,2,1,0:T(8,128)S(1)} %bitcast.10), custom_call_target="tpu_custom_call" | custom-call | tf_op jit(solution)/shard_map/final/pallas_call | solution.py:546
  (1 shorter events, 0.0 us)
Async XLA Ops:
  2.5 3.0 %collective-permute-start.4 = (f32[16,144,128]{2,1,0:T(8,128)S(1)}, f32[16,144,128]{2,1,0:T(8,128)}, u32[]{:S(2)}, u32[]{:S(2)}) collective-permute-start(f32[16,144,128]{2,1,0:T(8,128)S(1)} %get-tuple-element.45), channel_id=1, source_target_pairs={{0,16},{16,0},{1,17},{17,1},{2,18},{18,2},{3,19},{19,3},{4,20},{20... | collective-permute-start | bytes 3538952 | tf_op jit(solution)/shard_map/ppermute | solution.py:566
  25.7 5.6 %collective-permute-start.5 = (s32[16,24]{1,0:T(8,128)S(1)}, s32[16,24]{1,0:T(8,128)S(1)}, u32[]{:S(2)}, u32[]{:S(2)}) collective-permute-start(s32[16,24]{1,0:T(8,128)S(1)} %get-tuple-element.46), channel_id=1, source_target_pairs={{0,16},{16,0},{1,17},{17,1},{2,18},{18,2},{3,19},{19,3},{4,20},{20... | collective-permute-start | bytes 4616 | tf_op jit(solution)/shard_map/ppermute | solution.py:593
  35.5 14.8 %collective-permute-start.6 = (f32[16,48,128]{2,1,0:T(8,128)S(1)}, f32[16,48,128]{2,1,0:T(8,128)S(1)}, u32[]{:S(2)}, u32[]{:S(2)}) collective-permute-start(f32[16,48,128]{2,1,0:T(8,128)S(1)} %get-tuple-element.74), channel_id=1, source_target_pairs={{0,16},{16,0},{1,17},{17,1},{2,18},{18,2},{3,19},{19,3},{4,20},{20... | collective-permute-start | bytes 1179656 | tf_op jit(solution)/shard_map/ppermute | solution.py:597

commit v7 on v6

--- a/solution.py
+++ b/solution.py
@@ -12,7 +12,6 @@
 FRONT = 8
 STEP = 13
 REPLY = 7
-PARTS = 4
 
 CD_ICE = 0.1
 CW = 1.5
@@ -60,7 +59,7 @@
         lax.fori_loop(lo, hi, body, 0)
 
 
-def pack_body(nlat, nlon, per, count, raw, owner, pay, opened, edge, rim, parts, field):
+def pack_body(nlat, nlon, per, count, raw, owner, pay, edge, rim):
     n = nlat * nlon
     lane = lanes(per)
     group = lane // 8
@@ -79,11 +78,6 @@
             planes[2 + y] = scale * wy
             for ch in range(2, 6):
                 planes[2 * ch + y] = half(ch, y)
-            rx, ry = wx - planes[4 + y], wy - planes[6 + y]
-            speed = jnp.sqrt(rx * rx + ry * ry + 1.0)
-            rate = rho * (0.1 + 0.05 * speed) * speed
-            opened[t, 2 * y] = rate * rx
-            opened[t, 2 * y + 1] = rate * ry
         ends = jnp.zeros((per, BX), jnp.float32)
         for p in range(12):
             pay[t, pl.ds(p, per, stride=12), :] = planes[p]
@@ -104,9 +98,7 @@
             rim[t, k : k + 1, :] = row
         return 0
 
-    for c in range(parts):
-        field(c).wait()
-        steps(c * (n // parts), (c + 1) * (n // parts), tile)
+    steps(0, n, tile)
 
     def dest(d, _):
         i, j = d // nlon, d % nlon
@@ -144,38 +136,51 @@
     ends[...] = total
 
 
-def pack_kernel(nlat, nlon, per, raw_in, owner, pay, opened, raw, edge, rim, sems):
-    n = nlat * nlon
-    parts = PARTS if n % PARTS == 0 else 1
-    step = n // parts
-
-    def field(c):
-        at = pl.ds(c * step, step)
-        return pltpu.make_async_copy(raw_in.at[:, at], raw.at[:, at], sems.at[c])
-
+def pack_kernel(nlat, nlon, per, raw, owner, pay, edge, rim):
+    @pl.when(lax.axis_index("comp") == 1)
+    def _():
+        pack_body(nlat, nlon, per, nlat * nlon * per, raw, owner, pay, edge, rim)
+
+
+def pack(raw, owner, nlat, nlon):
+    _, n, per, _ = raw.shape
+    return pl.pallas_call(
+        functools.partial(pack_kernel, nlat, nlon, per),
+        out_shape=f32(n, 13 * per + 40, BX),
+        in_specs=[VMEM, SMEM],
+        out_specs=VMEM,
+        scratch_shapes=[pltpu.VMEM((n, per, BX), jnp.float32), pltpu.VMEM((n, 40, BX), jnp.float32)],
+        compiler_params=params(24),
+        name="pack",
+    )(raw, owner)
+
+
+def open_kernel(n, per, raw, opened):
     @pl.when(lax.axis_index("comp") == 0)
     def _():
-        for c in range(parts):
-            field(c).start()
-        pack_body(nlat, nlon, per, n * per, raw, owner, pay, opened, edge, rim, parts, field)
-
-
-def pack(raw, owner, nlat, nlon):
+        def tile(t, _):
+            for y in range(2):
+                wx, wy, cx, cy, rho = [raw[ch, t, :, y * BX : (y + 1) * BX] for ch in (0, 1, 2, 3, 6)]
+                rx, ry = wx - cx, wy - cy
+                speed = jnp.sqrt(rx * rx + ry * ry + 1.0)
+                rate = rho * (0.1 + 0.05 * speed) * speed
+                opened[t, 2 * y] = rate * rx
+                opened[t, 2 * y + 1] = rate * ry
+            return 0
+
+        steps(0, n, tile)
+
+
+def open_stress(raw):
     _, n, per, _ = raw.shape
     return pl.pallas_call(
-        functools.partial(pack_kernel, nlat, nlon, per),
-        out_shape=[f32(n, 13 * per + 40, BX), f32(n, 4, per, BX)],
-        in_specs=[pl.BlockSpec(memory_space=pltpu.HBM), SMEM],
-        out_specs=[VMEM] * 2,
-        scratch_shapes=[
-            pltpu.VMEM(raw.shape, jnp.float32),
-            pltpu.VMEM((n, per, BX), jnp.float32),
-            pltpu.VMEM((n, 40, BX), jnp.float32),
-            pltpu.SemaphoreType.DMA((PARTS,)),
-        ],
-        compiler_params=params(12),
-        name="pack",
-    )(raw, owner)
+        functools.partial(open_kernel, n, per),
+        out_shape=f32(n, 4, per, BX),
+        in_specs=[VMEM],
+        out_specs=VMEM,
+        compiler_params=params(24),
+        name="open_stress",
+    )(raw)
 
 
 def ice_ends(ice, covered, land):
@@ -562,8 +567,9 @@
     fields = fields[0]
     split = fields.reshape(7, n, per, 2 * BX)
     owner = block_owner.reshape(1, count)
-    pay, opened = pack(split, owner, nlat, nlon)
-    pay = lax.ppermute(pay, "comp", [(0, 1), (1, 0)])
+    other = lax.ppermute(split, "comp", [(0, 1), (1, 0)])
+    opened = open_stress(split)
+    pay = pack(other, owner, nlat, nlon)
     def everyone(x):
         return lax.all_to_all(x, ("lat", "lon"), split_axis=0, concat_axis=0, tiled=True)
 

time: 51.4 us -> 51.6 us (level)
  local copies, waits for them, and re-layouts: 2.42 us -> 3.42 us
  waiting for transfers between devices: 4.31 us -> 3.57 us
  blocking collectives: 16.1 us -> 16.7 us
    another operation x5, local copies, waits for them, and re-layouts: 2.42 us -> 3.41 us
    ppermute x1, starting transfers between devices: 4.3 us -> 3.32 us  [per_device(): swap = lax.ppermute(owned, 'comp', [(0, 1), (1, 0)])]
    pallas_call x1, Pallas kernels: 2.49 us -> 1.72 us  [pack(): pl.pallas_call(functools.partial(pack_kernel, nlat, nlon, per), out_shape...]
    ppermute x1, waiting for transfers between devices: 2.96 us -> 2.31 us  [per_device(): other = lax.ppermute(split, 'comp', [(0, 1), (1, 0)])]
    all_to_all x1, blocking collectives: 16.1 us -> 16.7 us  [everyone(): lax.all_to_all(x, ('lat', 'lon'), split_axis=0, concat_axis=0, tiled=True)]
    pallas_call x1, Pallas kernels: 4.2 us -> 4.74 us  [ice_step(): pl.pallas_call(functools.partial(ice_kernel, n, per, count), out_shape=[f...]
where the time goes in v7:
time: 51.6 us; the launch traced here: 51.2 us
  starting transfers between devices  17.3 us (34%)
  blocking collectives  16.7 us (32%)
  Pallas kernels  10.1 us (20%)
  waiting for transfers between devices  3.57 us (7%)
  local copies, waits for them, and re-layouts  3.42 us (7%)
    all_to_all x1, blocking collectives, everyone(): lax.all_to_all(x, ('lat', 'lon'), split_axis=0, concat_axis=0, tiled=True)  16.7 us
    ppermute x1, starting transfers between devices, per_device(): got = lax.ppermute(back, 'comp', [(0, 1), (1, 0)])  13.4 us
    pallas_call x1, Pallas kernels, ice_step(): pl.pallas_call(functools.partial(ice_kernel, n, per, count), out_shape=[f...  4.74 us
    another operation x5, local copies, waits for them, and re-layouts  3.41 us
    ppermute x1, starting transfers between devices, per_device(): swap = lax.ppermute(owned, 'comp', [(0, 1), (1, 0)])  3.32 us
    ppermute x1, waiting for transfers between devices, per_device(): other = lax.ppermute(split, 'comp', [(0, 1), (1, 0)])  2.31 us
    pallas_call x1, Pallas kernels, pack(): pl.pallas_call(functools.partial(pack_kernel, nlat, nlon, per), out_shape...  1.72 us
    pallas_call x1, Pallas kernels, table(): pl.pallas_call(functools.partial(table_kernel, nlat, nlon, per), out_shap...  1.48 us
  transfers between devices with their start and end apart: 3, of which 2 were waited for; matrix products, arithmetic and copies ran while one was open for 0% of the time, Pallas kernels for 3%

profile of v7, /device:TPU:0, one launch (start us, length us, event | category | flops | bytes accessed | tf_op | source)
XLA Modules:
  0.0 51.2 jit_solution(6016050250961636243)
XLA Ops:
  0.0 0.0 copy-start
  0.0 0.0 copy-start.2
  0.0 0.0 copy-start.3
  0.0 0.0 copy-start.1
  0.0 0.6 %collective-permute-start.4 = (f32[7,16,8,256]{3,2,1,0:T(8,128)}, f32[7,16,8,256]{3,2,1,0:T(8,128)S(1)}, u32[]{:S(2)}, u32[]{:S(2)}) collective-permute-start(f32[7,16,8,256]{3,2,1,0:T(8,128)} %bitcast.12), channel_id=1, source_target_pairs={{0,16},{16,0},{1,17},{17,1},{2,18},{18,2},{3,19},{19,3},{4,20},{20... | collective-permute-start | bytes 2752520 | tf_op jit(solution)/shard_map/ppermute | solution.py:570
  0.6 2.3 %collective-permute-done.4.raw = f32[7,16,8,256]{3,2,1,0:T(8,128)S(1)} collective-permute-done((f32[7,16,8,256]{3,2,1,0:T(8,128)}, f32[7,16,8,256]{3,2,1,0:T(8,128)S(1)}, u32[]{:S(2)}, u32[]{:S(2)}) %collective-permute-start.4) | collective-permute-done | bytes 917536 | tf_op jit(solution)/shard_map/ppermute | solution.py:570
  2.9 1.7 %pack.1 = f32[16,144,128]{2,1,0:T(8,128)} custom-call(f32[7,16,8,256]{3,2,1,0:T(8,128)S(1)} %collective-permute-done.4.raw, s32[1,128]{1,0:T(1,128)} %bitcast.18), custom_call_target="tpu_custom_call" | custom-call | tf_op jit(solution)/shard_map/pack/pallas_call | solution.py:147
  4.6 0.0 copy-done
  4.6 0.0 copy-done.2
  4.6 0.0 copy-done.3
  4.6 0.0 copy-done.1
  4.6 21.6 %conditional.2 = (f32[16,144,128]{2,1,0:T(8,128)}, s32[16,24]{1,0:T(8,128)S(1)}, f32[34,128]{1,0:T(8,128)}, f32[34,128]{1,0:T(8,128)}, f32[5,3,136,128]{3,2,1,0:T(8,128)S(1)}, /*index=5*/f32[5,3,136,128]{3,2,1,0:T(8,128)}) conditional(s32[]{:T(128)} %convert_element_type.4, s32[1,128]{1,0:T(1,128)S(1)} %bitcast.19, (f32[16,144,128]{2,1,0:T(8,128)}, ...), branch_computations={%region_0.0_spmd, %region_1.0_spmd} | conditional | bytes 4204276 | solution.py:596
  4.6 1.5 %table.1 = s32[16,24]{1,0:T(8,128)S(1)} custom-call(s32[1,128]{1,0:T(1,128)S(1)} %owner), custom_call_target="tpu_custom_call" | custom-call | tf_op jit(solution)/shard_map/cond/branch_0_fun/table/pallas_call | solution.py:213
  6.1 16.7 %all_to_all.17 = s32[16,1,24]{2,1,0:T(1,128)S(1)} all-to-all(s32[16,1,24]{2,1,0:T(1,128)S(1)} %bitcast.11), channel_id=1, replica_groups=mesh['comp'=2,'lat'=4,'lon'=4] {'lat','lon'}, dimensions={0} | all-to-all | bytes 3072 | tf_op jit(solution)/shard_map/cond/branch_0_fun/all_to_all | solution.py:574
  22.8 1.1 %broadcast.8 = f32[16,144,128]{2,1,0:T(8,128)} broadcast(f32[]{:T(128)} %constant.4.clone), dimensions={} | broadcast | bytes 1179652 | tf_op jit(solution)/shard_map/broadcast.5
  23.9 0.1 broadcast.10
  24.0 1.1 %broadcast.10.clone = f32[5,3,136,128]{3,2,1,0:T(8,128)} broadcast(f32[]{:T(128)} %constant.4.clone), dimensions={} | broadcast | bytes 1044484 | tf_op jit(solution)/shard_map/broadcast.3
  25.0 0.6 %broadcast.9 = f32[34,128]{1,0:T(8,128)} broadcast(f32[]{:T(128)} %constant.4.clone), dimensions={} | broadcast | bytes 17412 | tf_op jit(solution)/shard_map/broadcast.4
  25.6 0.6 %broadcast.9.clone = f32[34,128]{1,0:T(8,128)} broadcast(f32[]{:T(128)} %constant.4.clone), dimensions={} | broadcast | bytes 17412 | tf_op jit(solution)/shard_map/broadcast.4
  26.3 3.3 %collective-permute-start.5 = (s32[16,24]{1,0:T(8,128)S(1)}, s32[16,24]{1,0:T(8,128)S(1)}, u32[]{:S(2)}, u32[]{:S(2)}) collective-permute-start(s32[16,24]{1,0:T(8,128)S(1)} %get-tuple-element.43), channel_id=1, source_target_pairs={{0,16},{16,0},{1,17},{17,1},{2,18},{18,2},{3,19},{19,3},{4,20},{20... | collective-permute-start | bytes 4616 | tf_op jit(solution)/shard_map/ppermute | solution.py:599
  29.6 1.3 %fetch.1 = (f32[16,144,128]{2,1,0:T(8,128)S(1)}, f32[34,128]{1,0:T(8,128)S(1)}, f32[34,128]{1,0:T(8,128)S(1)}) custom-call(f32[16,144,128]{2,1,0:T(8,128)} %get-tuple-element.44.refs_0_, f32[34,128]{1,0:T(8,128)} %get-tuple-element.45.refs_1_, f32[34,128]{1,0:T(8,128)} %get-tuple-element.46.refs_2_), custom_call_target="tpu_custom_call" | custom-call | tf_op jit(solution)/shard_map/fetch/pallas_call | solution.py:308
  30.9 0.0 collective-permute-done.5.ids
  30.9 4.7 %ice_step.1 = (f32[16,48,128]{2,1,0:T(8,128)S(1)}, f32[2,128,256]{2,1,0:T(8,128)S(1)}) custom-call(s32[16,24]{1,0:T(8,128)S(1)} %collective-permute-done.5.ids, f32[16,144,128]{2,1,0:T(8,128)S(1)} %get-tuple-element.47.recv, f32[5,3,136,128]{3,2,1,0:T(8,128)S(1)} %get-tuple-element.48.begin, f32[5,3,136,128]{3,2,1,0:T(8,128)} %get-tuple-element.49.fixed, ...), custom_call_target="tpu_custom_call" | custom-call | tf_op jit(solution)/shard_map/ice_step/pallas_call | solution.py:518
  35.7 13.4 %collective-permute-start.6 = (f32[16,48,128]{2,1,0:T(8,128)S(1)}, f32[16,48,128]{2,1,0:T(8,128)S(1)}, u32[]{:S(2)}, u32[]{:S(2)}) collective-permute-start(f32[16,48,128]{2,1,0:T(8,128)S(1)} %get-tuple-element.70), channel_id=1, source_target_pairs={{0,16},{16,0},{1,17},{17,1},{2,18},{18,2},{3,19},{19,3},{4,20},{20... | collective-permute-start | bytes 1179656 | tf_op jit(solution)/shard_map/ppermute | solution.py:603
  49.1 0.1 open_stress.1.opened
  49.2 1.3 %collective-permute-done.6.got = f32[16,48,128]{2,1,0:T(8,128)S(1)} collective-permute-done((f32[16,48,128]{2,1,0:T(8,128)S(1)}, f32[16,48,128]{2,1,0:T(8,128)S(1)}, u32[]{:S(2)}, u32[]{:S(2)}) %collective-permute-start.6) | collective-permute-done | bytes 393248 | tf_op jit(solution)/shard_map/ppermute | solution.py:603
  50.4 0.8 %final.1 = f32[2,16,8,256]{3,2,1,0:T(8,128)} custom-call(f32[16,48,128]{2,1,0:T(8,128)S(1)} %collective-permute-done.6.got, f32[16,4,8,128]{3,2,1,0:T(8,128)S(1)} %open_stress.1.opened, f32[2,16,8,256]{3,2,1,0:T(8,128)S(1)} %bitcast.10), custom_call_target="tpu_custom_call" | custom-call | tf_op jit(solution)/shard_map/final/pallas_call | solution.py:551
  (1 shorter events, 0.0 us)
Async XLA Ops:
  0.0 4.6 %copy-start = (f32[1,7,128,256]{3,2,1,0:T(8,128)S(1)}, f32[1,7,128,256]{3,2,1,0:T(8,128)}, u32[]{:S(2)}) copy-start(f32[1,7,128,256]{3,2,1,0:T(8,128)} %param.8) | copy-start | bytes 2752516
  0.0 4.6 %copy-start.2 = (s32[128]{0:T(128)S(1)}, s32[128]{0:T(128)}, u32[]{:S(2)}) copy-start(s32[128]{0:T(128)} %param.9) | copy-start | bytes 1540
  0.0 4.6 %copy-start.3 = (s32[128]{0:T(128)S(1)}, s32[128]{0:T(128)}, u32[]{:S(2)}) copy-start(s32[128]{0:T(128)} %param.10) | copy-start | bytes 1540
  0.0 4.6 %copy-start.1 = (s32[128,256]{1,0:T(8,128)S(1)}, s32[128,256]{1,0:T(8,128)}, u32[]{:S(2)}) copy-start(s32[128,256]{1,0:T(8,128)} %param.11) | copy-start | bytes 393220
  0.0 2.9 %collective-permute-start.4 = (f32[7,16,8,256]{3,2,1,0:T(8,128)}, f32[7,16,8,256]{3,2,1,0:T(8,128)S(1)}, u32[]{:S(2)}, u32[]{:S(2)}) collective-permute-start(f32[7,16,8,256]{3,2,1,0:T(8,128)} %bitcast.12), channel_id=1, source_target_pairs={{0,16},{16,0},{1,17},{17,1},{2,18},{18,2},{3,19},{19,3},{4,20},{20... | collective-permute-start | bytes 2752520 | tf_op jit(solution)/shard_map/ppermute | solution.py:570
  26.3 4.6 %collective-permute-start.5 = (s32[16,24]{1,0:T(8,128)S(1)}, s32[16,24]{1,0:T(8,128)S(1)}, u32[]{:S(2)}, u32[]{:S(2)}) collective-permute-start(s32[16,24]{1,0:T(8,128)S(1)} %get-tuple-element.43), channel_id=1, source_target_pairs={{0,16},{16,0},{1,17},{17,1},{2,18},{18,2},{3,19},{19,3},{4,20},{20... | collective-permute-start | bytes 4616 | tf_op jit(solution)/shard_map/ppermute | solution.py:599
  35.7 14.8 %collective-permute-start.6 = (f32[16,48,128]{2,1,0:T(8,128)S(1)}, f32[16,48,128]{2,1,0:T(8,128)S(1)}, u32[]{:S(2)}, u32[]{:S(2)}) collective-permute-start(f32[16,48,128]{2,1,0:T(8,128)S(1)} %get-tuple-element.70), channel_id=1, source_target_pairs={{0,16},{16,0},{1,17},{17,1},{2,18},{18,2},{3,19},{19,3},{4,20},{20... | collective-permute-start | bytes 1179656 | tf_op jit(solution)/shard_map/ppermute | solution.py:603

commit v8 on v7

--- a/solution.py
+++ b/solution.py
@@ -59,8 +59,15 @@
         lax.fori_loop(lo, hi, body, 0)
 
 
-def pack_body(nlat, nlon, per, count, raw, owner, pay, edge, rim):
+def pack_kernel(nlat, nlon, per, raw, owner, out, pay, edge, rim, sems):
     n = nlat * nlon
+    count = n * per
+    cut = 12 * per if (12 * per) % 8 == 0 else 0
+
+    def send(d, k):
+        at = pl.ds(0, cut) if k == 0 else pl.ds(cut, 13 * per + 40 - cut)
+        return pltpu.make_async_copy(pay.at[d, at], out.at[d, at], sems.at[k, d])
+
     lane = lanes(per)
     group = lane // 8
     slot = lax.broadcasted_iota(jnp.int32, (per, BX), 0)
@@ -96,6 +103,8 @@
         rows += [pick(b, ends) for b in (0, 1, count - 1, count - 2)]
         for k, row in enumerate(rows):
             rim[t, k : k + 1, :] = row
+        if cut:
+            send(t, 0).start()
         return 0
 
     steps(0, n, tile)
@@ -114,9 +123,17 @@
             q2 = (lanes(2) % 8) < 4
             corner = at_end(q2, rim[ii * nlon + jw, c : c + 2, :], rim[ii * nlon + je, c : c + 2, :])
             pay[d, lat_base + c : lat_base + c + 2, :] = corner * scale
+        send(d, 1).start()
         return 0
 
+    def finish(d, _):
+        if cut:
+            send(d, 0).wait()
+        send(d, 1).wait()
+        return 0
+
     steps(0, n, dest)
+    steps(0, n, finish)
 
 
 def ends_kernel(ice, covered, land, active, ends):
@@ -136,20 +153,20 @@
     ends[...] = total
 
 
-def pack_kernel(nlat, nlon, per, raw, owner, pay, edge, rim):
-    @pl.when(lax.axis_index("comp") == 1)
-    def _():
-        pack_body(nlat, nlon, per, nlat * nlon * per, raw, owner, pay, edge, rim)
-
-
 def pack(raw, owner, nlat, nlon):
     _, n, per, _ = raw.shape
+    rows = 13 * per + 40
     return pl.pallas_call(
         functools.partial(pack_kernel, nlat, nlon, per),
-        out_shape=f32(n, 13 * per + 40, BX),
+        out_shape=f32(n, rows, BX),
         in_specs=[VMEM, SMEM],
-        out_specs=VMEM,
-        scratch_shapes=[pltpu.VMEM((n, per, BX), jnp.float32), pltpu.VMEM((n, 40, BX), jnp.float32)],
+        out_specs=pl.BlockSpec(memory_space=pl.ANY),
+        scratch_shapes=[
+            pltpu.VMEM((n, rows, BX), jnp.float32),
+            pltpu.VMEM((n, per, BX), jnp.float32),
+            pltpu.VMEM((n, 40, BX), jnp.float32),
+            pltpu.SemaphoreType.DMA((2, n)),
+        ],
         compiler_params=params(24),
         name="pack",
     )(raw, owner)
@@ -569,14 +586,13 @@
     owner = block_owner.reshape(1, count)
     other = lax.ppermute(split, "comp", [(0, 1), (1, 0)])
     opened = open_stress(split)
-    pay = pack(other, owner, nlat, nlon)
     def everyone(x):
         return lax.all_to_all(x, ("lat", "lon"), split_axis=0, concat_axis=0, tiled=True)
 
     height = (count + 4 + 7) // 8 * 8
 
-    def ice_side(pay, fields, covered, land, owner):
-        recv = everyone(pay)
+    def ice_side(other, fields, covered, land, owner):
+        recv = everyone(pack(other, owner, nlat, nlon))
         active, ends = ice_ends(fields, covered, land)
         ring = [(i, (i + 1) % nlon) for i in range(nlon)]
         west = lax.ppermute(ends, "lon", ring)
@@ -588,13 +604,13 @@
         begin, fixed = prep(fields, active, sides)
         return recv, jnp.zeros((n, 3 * per), jnp.int32), below, above, begin, fixed
 
-    def ocean_side(pay, fields, covered, land, owner):
+    def ocean_side(other, fields, covered, land, owner):
         row = jnp.zeros((34, BX), jnp.float32)
         blank = jnp.zeros((5, 3, height, BX), jnp.float32)
-        return jnp.zeros(pay.shape, jnp.float32), everyone(table(owner, nlat, nlon)), row, row, blank, blank
+        return jnp.zeros((n, 13 * per + 40, BX), jnp.float32), everyone(table(owner, nlat, nlon)), row, row, blank, blank
 
     recv, owned, below, above, begin, fixed = lax.cond(
-        side == 1, ice_side, ocean_side, pay, fields, ice_covered.reshape(1, count), land_mask, owner
+        side == 1, ice_side, ocean_side, other, fields, ice_covered.reshape(1, count), land_mask, owner
     )
     swap = lax.ppermute(owned, "comp", [(0, 1), (1, 0)])
     recv, below, above = fetch(recv, below, above)

time: 51.6 us -> 51 us (0.988)
  starting transfers between devices: 17.3 us -> 20.7 us
  Pallas kernels: 10.1 us -> 7.98 us
  local copies, waits for them, and re-layouts: 3.42 us -> 2.42 us
  blocking collectives: 16.7 us -> 15.9 us
    ppermute x1, starting transfers between devices: 3.32 us -> 6.72 us  [per_device(): swap = lax.ppermute(owned, 'comp', [(0, 1), (1, 0)])]
    pallas_call x1 -> x0, Pallas kernels: 1.72 us -> none  [pack(): pl.pallas_call(functools.partial(pack_kernel, nlat, nlon, per), out_shape...]
    another operation x5, local copies, waits for them, and re-layouts: 3.41 us -> 2.42 us
    all_to_all x1, blocking collectives: 16.7 us -> 15.9 us  [everyone(): lax.all_to_all(x, ('lat', 'lon'), split_axis=0, concat_axis=0, tiled=True)]
    pallas_call x1, Pallas kernels: 4.74 us -> 4.18 us  [ice_step(): pl.pallas_call(functools.partial(ice_kernel, n, per, count), out_shape=[f...]
where the time goes in v8:
time: 51 us; the launch traced here: 50.7 us
  starting transfers between devices  20.7 us (41%)
  blocking collectives  15.9 us (31%)
  Pallas kernels  7.98 us (16%)
  waiting for transfers between devices  3.56 us (7%)
  local copies, waits for them, and re-layouts  2.42 us (5%)
    all_to_all x1, blocking collectives, everyone(): lax.all_to_all(x, ('lat', 'lon'), split_axis=0, concat_axis=0, tiled=True)  15.9 us
    ppermute x1, starting transfers between devices, per_device(): got = lax.ppermute(back, 'comp', [(0, 1), (1, 0)])  13.5 us
    ppermute x1, starting transfers between devices, per_device(): swap = lax.ppermute(owned, 'comp', [(0, 1), (1, 0)])  6.72 us
    pallas_call x1, Pallas kernels, ice_step(): pl.pallas_call(functools.partial(ice_kernel, n, per, count), out_shape=[f...  4.18 us
    another operation x5, local copies, waits for them, and re-layouts  2.42 us
    ppermute x1, waiting for transfers between devices, per_device(): other = lax.ppermute(split, 'comp', [(0, 1), (1, 0)])  2.31 us
    pallas_call x1, Pallas kernels, table(): pl.pallas_call(functools.partial(table_kernel, nlat, nlon, per), out_shap...  1.6 us
    pallas_call x1, Pallas kernels, fetch(): pl.pallas_call(fetch_kernel, out_shape=[f32(*x.shape) for x in arrays], i...  1.3 us
  transfers between devices with their start and end apart: 3, of which 2 were waited for; matrix products, arithmetic and copies ran while one was open for 0% of the time, Pallas kernels for 3%

profile of v8, /device:TPU:0, one launch (start us, length us, event | category | flops | bytes accessed | tf_op | source)
XLA Modules:
  0.0 50.7 jit_solution(134167512258906944)
XLA Ops:
  0.0 0.5 collective-permute-start.4
  0.5 2.3 %collective-permute-done.4 = f32[7,16,8,256]{3,2,1,0:T(8,128)S(1)} collective-permute-done((f32[7,16,8,256]{3,2,1,0:T(8,128)}, f32[7,16,8,256]{3,2,1,0:T(8,128)S(1)}, u32[]{:S(2)}, u32[]{:S(2)}) %collective-permute-start.4) | collective-permute-done | bytes 917536 | tf_op jit(solution)/shard_map/ppermute | solution.py:587
  2.8 19.9 %conditional.2 = (f32[16,144,128]{2,1,0:T(8,128)}, s32[16,24]{1,0:T(8,128)S(1)}, f32[34,128]{1,0:T(8,128)}, f32[34,128]{1,0:T(8,128)}, f32[5,3,136,128]{3,2,1,0:T(8,128)S(1)}, /*index=5*/f32[5,3,136,128]{3,2,1,0:T(8,128)S(1)}) conditional(s32[]{:T(128)} %convert_element_type.4, s32[1,128]{1,0:T(1,128)} %bitcast.18, (f32[7,16,8,256]{3,2,1,0:T(8,128)S(1)}, ...), branch_computations={%region_0.0_spmd, %region_1.0_spmd} | conditional | bytes 8400712 | solution.py:612
  2.8 1.6 %table.1 = s32[16,24]{1,0:T(8,128)S(1)} custom-call(s32[1,128]{1,0:T(1,128)} %owner), custom_call_target="tpu_custom_call" | custom-call | tf_op jit(solution)/shard_map/cond/branch_0_fun/table/pallas_call | solution.py:230
  4.4 15.9 %all_to_all.17 = s32[16,1,24]{2,1,0:T(1,128)S(1)} all-to-all(s32[16,1,24]{2,1,0:T(1,128)S(1)} %bitcast.11), channel_id=1, replica_groups=mesh['comp'=2,'lat'=4,'lon'=4] {'lat','lon'}, dimensions={0} | all-to-all | bytes 3072 | tf_op jit(solution)/shard_map/cond/branch_0_fun/all_to_all | solution.py:590
  20.3 1.1 %broadcast.8 = f32[16,144,128]{2,1,0:T(8,128)} broadcast(f32[]{:T(128)} %constant.4.clone), dimensions={} | broadcast | bytes 1179652 | tf_op jit(solution)/shard_map/broadcast.5
  21.4 0.1 broadcast.10
  21.4 0.1 broadcast.10.clone
  21.5 0.6 %broadcast.9 = f32[34,128]{1,0:T(8,128)} broadcast(f32[]{:T(128)} %constant.4.clone), dimensions={} | broadcast | bytes 17412 | tf_op jit(solution)/shard_map/broadcast.4
  22.1 0.6 %broadcast.9.clone = f32[34,128]{1,0:T(8,128)} broadcast(f32[]{:T(128)} %constant.4.clone), dimensions={} | broadcast | bytes 17412 | tf_op jit(solution)/shard_map/broadcast.4
  22.7 6.7 %collective-permute-start.5 = (s32[16,24]{1,0:T(8,128)S(1)}, s32[16,24]{1,0:T(8,128)S(1)}, u32[]{:S(2)}, u32[]{:S(2)}) collective-permute-start(s32[16,24]{1,0:T(8,128)S(1)} %get-tuple-element.46), channel_id=1, source_target_pairs={{0,16},{16,0},{1,17},{17,1},{2,18},{18,2},{3,19},{19,3},{4,20},{20... | collective-permute-start | bytes 4616 | tf_op jit(solution)/shard_map/ppermute | solution.py:615
  29.4 1.3 %fetch.1 = (f32[16,144,128]{2,1,0:T(8,128)S(1)}, f32[34,128]{1,0:T(8,128)S(1)}, f32[34,128]{1,0:T(8,128)S(1)}) custom-call(f32[16,144,128]{2,1,0:T(8,128)} %get-tuple-element.47.refs_0_, f32[34,128]{1,0:T(8,128)} %get-tuple-element.48.refs_1_, f32[34,128]{1,0:T(8,128)} %get-tuple-element.49.refs_2_), custom_call_target="tpu_custom_call" | custom-call | tf_op jit(solution)/shard_map/fetch/pallas_call | solution.py:325
  30.8 0.0 collective-permute-done.5.ids
  30.8 4.2 %ice_step.1 = (f32[16,48,128]{2,1,0:T(8,128)S(1)}, f32[2,128,256]{2,1,0:T(8,128)S(1)}) custom-call(s32[16,24]{1,0:T(8,128)S(1)} %collective-permute-done.5.ids, f32[16,144,128]{2,1,0:T(8,128)S(1)} %get-tuple-element.50.recv, f32[5,3,136,128]{3,2,1,0:T(8,128)S(1)} %get-tuple-element.51.begin, f32[5,3,136,128]{3,2,1,0:T(8,128)S(1)} %get-tuple-element.52.fixed, ...), custom_call_target="tpu_custom_call" | custom-call | tf_op jit(solution)/shard_map/ice_step/pallas_call | solution.py:535
  35.0 0.0 copy-start
  35.0 13.5 %collective-permute-start.6 = (f32[16,48,128]{2,1,0:T(8,128)S(1)}, f32[16,48,128]{2,1,0:T(8,128)S(1)}, u32[]{:S(2)}, u32[]{:S(2)}) collective-permute-start(f32[16,48,128]{2,1,0:T(8,128)S(1)} %get-tuple-element.73), channel_id=1, source_target_pairs={{0,16},{16,0},{1,17},{17,1},{2,18},{18,2},{3,19},{19,3},{4,20},{20... | collective-permute-start | bytes 1179656 | tf_op jit(solution)/shard_map/ppermute | solution.py:619
  48.5 0.0 copy-done
  48.5 0.1 open_stress.1.opened
  48.6 1.3 %collective-permute-done.6.got = f32[16,48,128]{2,1,0:T(8,128)S(1)} collective-permute-done((f32[16,48,128]{2,1,0:T(8,128)S(1)}, f32[16,48,128]{2,1,0:T(8,128)S(1)}, u32[]{:S(2)}, u32[]{:S(2)}) %collective-permute-start.6) | collective-permute-done | bytes 393248 | tf_op jit(solution)/shard_map/ppermute | solution.py:619
  49.9 0.8 %final.1 = f32[2,16,8,256]{3,2,1,0:T(8,128)} custom-call(f32[16,48,128]{2,1,0:T(8,128)S(1)} %collective-permute-done.6.got, f32[16,4,8,128]{3,2,1,0:T(8,128)S(1)} %open_stress.1.opened, f32[2,16,8,256]{3,2,1,0:T(8,128)S(1)} %bitcast.10), custom_call_target="tpu_custom_call" | custom-call | tf_op jit(solution)/shard_map/final/pallas_call | solution.py:568
  (1 shorter events, 0.0 us)
Async XLA Ops:
  0.0 2.8 %collective-permute-start.4 = (f32[7,16,8,256]{3,2,1,0:T(8,128)}, f32[7,16,8,256]{3,2,1,0:T(8,128)S(1)}, u32[]{:S(2)}, u32[]{:S(2)}) collective-permute-start(f32[7,16,8,256]{3,2,1,0:T(8,128)} %bitcast.12), channel_id=1, source_target_pairs={{0,16},{16,0},{1,17},{17,1},{2,18},{18,2},{3,19},{19,3},{4,20},{20... | collective-permute-start | bytes 2752520 | tf_op jit(solution)/shard_map/ppermute | solution.py:587
  22.7 8.0 %collective-permute-start.5 = (s32[16,24]{1,0:T(8,128)S(1)}, s32[16,24]{1,0:T(8,128)S(1)}, u32[]{:S(2)}, u32[]{:S(2)}) collective-permute-start(s32[16,24]{1,0:T(8,128)S(1)} %get-tuple-element.46), channel_id=1, source_target_pairs={{0,16},{16,0},{1,17},{17,1},{2,18},{18,2},{3,19},{19,3},{4,20},{20... | collective-permute-start | bytes 4616 | tf_op jit(solution)/shard_map/ppermute | solution.py:615
  35.0 13.6 %copy-start = (f32[1,7,128,256]{3,2,1,0:T(8,128)S(1)}, f32[1,7,128,256]{3,2,1,0:T(8,128)}, u32[]{:S(2)}) copy-start(f32[1,7,128,256]{3,2,1,0:T(8,128)} %param.8) | copy-start | bytes 2752516
  35.0 14.9 %collective-permute-start.6 = (f32[16,48,128]{2,1,0:T(8,128)S(1)}, f32[16,48,128]{2,1,0:T(8,128)S(1)}, u32[]{:S(2)}, u32[]{:S(2)}) collective-permute-start(f32[16,48,128]{2,1,0:T(8,128)S(1)} %get-tuple-element.73), channel_id=1, source_target_pairs={{0,16},{16,0},{1,17},{17,1},{2,18},{18,2},{3,19},{19,3},{4,20},{20... | collective-permute-start | bytes 1179656 | tf_op jit(solution)/shard_map/ppermute | solution.py:619

commit v9 on v8

--- a/solution.py
+++ b/solution.py
@@ -11,7 +11,7 @@
 NSUB = 4
 FRONT = 8
 STEP = 13
-REPLY = 7
+REPLY = 5
 
 CD_ICE = 0.1
 CW = 1.5
@@ -183,6 +183,8 @@
                 rate = rho * (0.1 + 0.05 * speed) * speed
                 opened[t, 2 * y] = rate * rx
                 opened[t, 2 * y + 1] = rate * ry
+                opened[t, 4 + 2 * y] = cx
+                opened[t, 5 + 2 * y] = cy
             return 0
 
         steps(0, n, tile)
@@ -192,7 +194,7 @@
     _, n, per, _ = raw.shape
     return pl.pallas_call(
         functools.partial(open_kernel, n, per),
-        out_shape=f32(n, 4, per, BX),
+        out_shape=f32(n, 8, per, BX),
         in_specs=[VMEM],
         out_specs=VMEM,
         compiler_params=params(24),
@@ -274,10 +276,10 @@
 
 
 def statics(mass, conc, act):
-    return mass * jnp.exp(CSTAR * (conc - 1.0)) * act * (1.0 / 6.0), 2.0 * mass, CW * conc * act, act, conc
-
-
-def prep_kernel(count, height, ice, active, sides, begin, still, grid):
+    return mass * jnp.exp(CSTAR * (conc - 1.0)) * act * (1.0 / 6.0), 2.0 * mass, act, conc
+
+
+def prep_kernel(count, height, ice, active, sides, begin, still, unused, grid):
     mid = middle(count)
     for ch in range(8):
         for y in range(2):
@@ -298,14 +300,14 @@
                 still[k, z, at, :] = x
 
 
-def prep(ice, active, sides):
+def prep(ice, active, sides, spare):
     count = active.shape[0]
     height = (count + 4 + 7) // 8 * 8
     return pl.pallas_call(
         functools.partial(prep_kernel, count, height),
-        out_shape=[f32(5, 3, height, BX)] * 2,
+        out_shape=[f32(5, 3, height, BX), f32(4, 3, height, BX), f32(*spare)],
         in_specs=[VMEM] * 3,
-        out_specs=[VMEM] * 2,
+        out_specs=[VMEM] * 3,
         scratch_shapes=[pltpu.VMEM((8, 3, height, BX), jnp.float32)],
         compiler_params=params(12),
         name="prep",
@@ -345,7 +347,7 @@
     return jnp.where(at0, s, e), jnp.where(at0, roll(side, -63), o), wide
 
 
-def ice_kernel(n, per, count, ids, recv, begin, fixed, below, above, back, moved,
+def ice_kernel(n, per, count, ids, recv, begin, fixed, below, above, back, moved, unused,
                spot, hw, he, speed, state, forced, out8, still):
     tiles = (count + 4 + 7) // 8
     height = tiles * 8
@@ -390,8 +392,9 @@
                 speed[k, z, to, :] = begin[k, z, at, :]
             for k in range(3):
                 state[k, z, to, :] = begin[2 + k, z, at, :]
-            for k in range(5):
-                still[k, z, at, :] = fixed[k, z, at, :]
+            hard, m2, act, conc = [fixed[k, z, at, :] for k in range(4)]
+            for k, x in enumerate((hard, m2, CW * conc * act, act, conc)):
+                still[k, z, at, :] = x
     for lo, msg in ((0, below), (count + 2, above)):
         at, to = slice(lo, lo + 2), slice(FRONT + lo, FRONT + lo + 2)
         for z in range(3):
@@ -405,7 +408,8 @@
             state[0, z, to, :] = 0.5 * s1
             state[1, z, to, :] = 0.5 * s2
             state[2, z, to, :] = s12
-            for k, x in enumerate(statics(mass, conc, act)):
+            hard, m2, act, conc = statics(mass, conc, act)
+            for k, x in enumerate((hard, m2, CW * conc * act, act, conc)):
                 still[k, z, at, :] = x
 
     for r in range(tiles):
@@ -500,16 +504,10 @@
     lax.fori_loop(0, NSUB, subcycle, 0)
 
     for r in range(tiles):
-        at = slice(8 * r, 8 * r + 8)
         to = slice(FRONT + 8 * r, FRONT + 8 * r + 8)
         for y in range(2):
-            base = still[2, y, at, :]
-            dx = speed[0, y, to, :] - forced[2, y, at, :]
-            dy = speed[1, y, to, :] - forced[3, y, at, :]
-            y2 = dx * dx + dy * dy + DRAG_FLOOR
-            factor = base * (y2 * lax.rsqrt(y2))
-            for k, x in enumerate((factor * dx, factor * dy, base * (1.0 / CW))):
-                out8[pl.ds(8 * r * REPLY + 2 * k + y, 8, stride=REPLY), :] = x
+            for k in range(2):
+                out8[pl.ds(8 * r * REPLY + 2 * k + y, 8, stride=REPLY), :] = speed[k, y, to, :]
     for y in range(2):
         for k in range(2):
             moved[k, :, y * BX : (y + 1) * BX] = speed[k, y, FRONT + 2 : FRONT + 2 + count, :]
@@ -517,7 +515,7 @@
     def answer(o, _):
         for j in range(per):
             b = (ids[o, j] + 2) * REPLY
-            back[o, 6 * j : 6 * j + 6, :] = out8[pl.ds(b, 6), :]
+            back[o, 4 * j : 4 * j + 4, :] = out8[pl.ds(b, 4), :]
         return 0
 
     lax.fori_loop(0, n, answer, 0)
@@ -534,16 +532,46 @@
     ]
     return pl.pallas_call(
         functools.partial(ice_kernel, n, per, count),
-        out_shape=[f32(n, 6 * per, BX), f32(2, count, 2 * BX)],
+        out_shape=[f32(n, 4 * per, BX), f32(2, count, 2 * BX), f32(n, 2 * per, BX)],
         in_specs=[SMEM] + [VMEM] * 5,
-        out_specs=[VMEM] * 2,
+        out_specs=[VMEM] * 3,
         scratch_shapes=[pltpu.VMEM(s, jnp.float32) for s in scratch],
         compiler_params=params(16),
         name="ice_step",
     )(ids, recv, begin, fixed, below, above)
 
 
-def final_kernel(n, per, got, opened, moved, out):
+def cover_kernel(n, per, ids, conc, covered, land, out, spot):
+    count = n * per
+    cover = column(covered[...])
+    for y in range(2):
+        cells = slice(y * BX, (y + 1) * BX)
+        act = cover * (1 - land[:, cells]).astype(jnp.float32)
+        spot[pl.ds(y, count, stride=2), :] = conc[:, cells] * act
+
+    def tile(o, _):
+        for j in range(per):
+            out[o, 2 * j : 2 * j + 2, :] = spot[pl.ds(2 * ids[o, j], 2), :]
+        return 0
+
+    lax.fori_loop(0, n, tile, 0)
+
+
+def slot_cover(ids, conc, covered, land):
+    n, per = ids.shape[0], ids.shape[1] // 3
+    count = n * per
+    return pl.pallas_call(
+        functools.partial(cover_kernel, n, per),
+        out_shape=f32(n, 2 * per, BX),
+        in_specs=[SMEM] + [VMEM] * 3,
+        out_specs=VMEM,
+        scratch_shapes=[pltpu.VMEM((2 * count, BX), jnp.float32)],
+        compiler_params=params(8),
+        name="slot_cover",
+    )(ids, conc, covered, land)
+
+
+def final_kernel(n, per, got, cover, opened, moved, out):
     is_ocean = lax.axis_index("comp") == 0
 
     @pl.when(is_ocean)
@@ -551,28 +579,32 @@
         def tile(t, _):
             for y in range(2):
                 cells = slice(y * BX, (y + 1) * BX)
-                gx, gy, gc = [got[t, pl.ds(2 * k + y, per, stride=6), :] for k in range(3)]
-                out[0, t, :, cells] = gx + (1.0 - gc) * opened[t, 2 * y]
-                out[1, t, :, cells] = gy + (1.0 - gc) * opened[t, 2 * y + 1]
+                u, v = [got[t, pl.ds(2 * k + y, per, stride=4), :] for k in range(2)]
+                part = cover[t, pl.ds(y, per, stride=2), :]
+                dx, dy = u - opened[t, 4 + 2 * y], v - opened[t, 5 + 2 * y]
+                factor = (CW * part) * jnp.sqrt(dx * dx + dy * dy + DRAG_FLOOR)
+                rest = 1.0 - part
+                out[0, t, :, cells] = factor * dx + rest * opened[t, 2 * y]
+                out[1, t, :, cells] = factor * dy + rest * opened[t, 2 * y + 1]
             return 0
 
-        lax.fori_loop(0, n, tile, 0)
+        steps(0, n, tile)
 
     @pl.when(jnp.logical_not(is_ocean))
     def _():
         out[...] = moved[...]
 
 
-def final(got, opened, moved):
+def final(got, cover, opened, moved):
     n, _, per, _ = opened.shape
     return pl.pallas_call(
         functools.partial(final_kernel, n, per),
         out_shape=f32(2, n, per, 2 * BX),
-        in_specs=[VMEM] * 3,
+        in_specs=[VMEM] * 4,
         out_specs=VMEM,
-        compiler_params=params(8),
+        compiler_params=params(12),
         name="final",
-    )(got, opened, moved)
+    )(got, cover, opened, moved)
 
 
 def per_device(fields, block_owner, ice_covered, land_mask):
@@ -601,23 +633,34 @@
         line = [(i, i + 1) for i in range(nlat - 1)]
         below = lax.ppermute(north, "lat", line)
         above = lax.ppermute(south, "lat", [(j, i) for i, j in line])
-        begin, fixed = prep(fields, active, sides)
-        return recv, jnp.zeros((n, 3 * per), jnp.int32), below, above, begin, fixed
+        begin, fixed, mine = prep(fields, active, sides, (n, 2 * per, BX))
+        return recv, jnp.zeros((n, 3 * per), jnp.int32), below, above, begin, fixed, mine
 
     def ocean_side(other, fields, covered, land, owner):
         row = jnp.zeros((34, BX), jnp.float32)
         blank = jnp.zeros((5, 3, height, BX), jnp.float32)
-        return jnp.zeros((n, 13 * per + 40, BX), jnp.float32), everyone(table(owner, nlat, nlon)), row, row, blank, blank
-
-    recv, owned, below, above, begin, fixed = lax.cond(
+        owned = everyone(table(owner, nlat, nlon))
+        mine = slot_cover(owned, other.reshape(7, count, 2 * BX)[3], covered, land)
+        return jnp.zeros((n, 13 * per + 40, BX), jnp.float32), owned, row, row, blank, blank[:4], mine
+
+    recv, owned, below, above, begin, fixed, mine = lax.cond(
         side == 1, ice_side, ocean_side, other, fields, ice_covered.reshape(1, count), land_mask, owner
     )
     swap = lax.ppermute(owned, "comp", [(0, 1), (1, 0)])
     recv, below, above = fetch(recv, below, above)
-    back, moved = ice_step(swap, recv, begin, fixed, below, above)
+
+    def ice_work(ids, recv, begin, fixed, below, above, mine):
+        return ice_step(ids, recv, begin, fixed, below, above)
+
+    def ocean_work(ids, recv, begin, fixed, below, above, mine):
+        return jnp.zeros((n, 4 * per, BX), jnp.float32), jnp.zeros((2, count, 2 * BX), jnp.float32), everyone(mine)
+
+    back, moved, cover = lax.cond(
+        side == 1, ice_work, ocean_work, swap, recv, begin, fixed, below, above, mine
+    )
     back = lax.cond(side == 1, everyone, lambda x: x, back)
     got = lax.ppermute(back, "comp", [(0, 1), (1, 0)])
-    out = final(got, opened, moved.reshape(2, n, per, 2 * BX))
+    out = final(got, cover, opened, moved.reshape(2, n, per, 2 * BX))
     return out.reshape(1, 2, count, 2 * BX)
 
 

time: 51 us -> 49.6 us (0.973)
  waiting for transfers between devices: 3.56 us -> 11.1 us
  starting transfers between devices: 20.7 us -> 17.4 us
  Pallas kernels: 7.98 us -> 4.96 us
  blocking collectives: 15.9 us -> 13.2 us
    ppermute x1, starting transfers between devices: 13.5 us -> 3.29 us  [per_device(): got = lax.ppermute(back, 'comp', [(0, 1), (1, 0)])]
    all_to_all x0 -> x1, starting transfers between devices: none -> 8.23 us  [everyone(): lax.all_to_all(x, ('lat', 'lon'), split_axis=0, concat_axis=0, tiled=True)]
    all_to_all x0 -> x1, waiting for transfers between devices: none -> 7.77 us  [everyone(): lax.all_to_all(x, ('lat', 'lon'), split_axis=0, concat_axis=0, tiled=True)]
    pallas_call x2, Pallas kernels: 4.28 us -> 1.34 us  [the longest x1 1.24 us: slot_cover(): pl.pallas_call(functools.partial(cover_kernel, n, per), out_shape=f32(n,...]
    all_to_all x1, blocking collectives: 15.9 us -> 13.2 us  [everyone(): lax.all_to_all(x, ('lat', 'lon'), split_axis=0, concat_axis=0, tiled=True)]
    ppermute x1, starting transfers between devices: 6.72 us -> 5.43 us  [per_device(): swap = lax.ppermute(owned, 'comp', [(0, 1), (1, 0)])]
    another operation x5 -> x6, local copies, waits for them, and re-layouts: 2.42 us -> 2.43 us
  transfers between devices with their start and end apart: 3 -> 4, of which waited for: 2 -> 3; matrix products, arithmetic and copies ran while one was open for 0% -> 0% of each run, Pallas kernels for 3% -> 3%
where the time goes in v9:
time: 49.6 us; the launch traced here: 49.4 us
  starting transfers between devices  17.4 us (35%)
  blocking collectives  13.2 us (27%)
  waiting for transfers between devices  11.1 us (22%)
  Pallas kernels  4.96 us (10%)
  local copies, waits for them, and re-layouts  2.47 us (5%)
    all_to_all x1, blocking collectives, everyone(): lax.all_to_all(x, ('lat', 'lon'), split_axis=0, concat_axis=0, tiled=True)  13.2 us
    all_to_all x1, starting transfers between devices, everyone(): lax.all_to_all(x, ('lat', 'lon'), split_axis=0, concat_axis=0, tiled=True)  8.23 us
    all_to_all x1, waiting for transfers between devices, everyone(): lax.all_to_all(x, ('lat', 'lon'), split_axis=0, concat_axis=0, tiled=True)  7.77 us
    ppermute x1, starting transfers between devices, per_device(): swap = lax.ppermute(owned, 'comp', [(0, 1), (1, 0)])  5.43 us
    ppermute x1, starting transfers between devices, per_device(): got = lax.ppermute(back, 'comp', [(0, 1), (1, 0)])  3.29 us
    another operation x6, local copies, waits for them, and re-layouts  2.43 us
    ppermute x1, waiting for transfers between devices, per_device(): other = lax.ppermute(split, 'comp', [(0, 1), (1, 0)])  2.31 us
    pallas_call x1, Pallas kernels, table(): pl.pallas_call(functools.partial(table_kernel, nlat, nlon, per), out_shap...  1.52 us
  transfers between devices with their start and end apart: 4, of which 3 were waited for; matrix products, arithmetic and copies ran while one was open for 0% of the time, Pallas kernels for 3%

profile of v9, /device:TPU:0, one launch (start us, length us, event | category | flops | bytes accessed | tf_op | source)
XLA Modules:
  0.0 49.4 jit_solution(11399462695958286754)
XLA Ops:
  0.0 0.5 collective-permute-start.4
  0.5 2.3 %collective-permute-done.4 = f32[7,16,8,256]{3,2,1,0:T(8,128)S(1)} collective-permute-done((f32[7,16,8,256]{3,2,1,0:T(8,128)}, f32[7,16,8,256]{3,2,1,0:T(8,128)S(1)}, u32[]{:S(2)}, u32[]{:S(2)}) %collective-permute-start.4) | collective-permute-done | bytes 917536 | tf_op jit(solution)/shard_map/ppermute | solution.py:619
  2.8 21.2 %conditional.3 = (f32[16,144,128]{2,1,0:T(8,128)}, s32[16,24]{1,0:T(8,128)S(1)}, f32[34,128]{1,0:T(8,128)}, f32[34,128]{1,0:T(8,128)}, f32[5,3,136,128]{3,2,1,0:...) conditional(s32[]{:T(128)} %convert_element_type.2, (s32[1,128]{1,0:T(1,128)}, ...), branch_computations={%region_0.0_spmd, %region_1.0_spmd} | conditional | bytes 8400720 | solution.py:646
  2.8 1.5 %table.1 = s32[16,24]{1,0:T(8,128)} custom-call(s32[1,128]{1,0:T(1,128)} %get-tuple-element.48.owner), custom_call_target="tpu_custom_call" | custom-call | tf_op jit(solution)/shard_map/cond/branch_0_fun/table/pallas_call | solution.py:232
  4.3 8.2 %all-to-all-start.3 = ((s32[16,1,24]{2,1,0:T(1,128)}), s32[16,1,24]{2,1,0:T(1,128)S(1)}, u32[]{:S(2)}, u32[]{:S(2)}) async-start(s32[16,1,24]{2,1,0:T(1,128)} %bitcast.1), calls=%async_computation.3 | async-start | bytes 16384 | tf_op jit(solution)/shard_map/cond/branch_0_fun/all_to_all | solution.py:622
  12.6 7.8 %all-to-all-done.3 = s32[16,1,24]{2,1,0:T(1,128)S(1)} async-done(((s32[16,1,24]{2,1,0:T(1,128)}), s32[16,1,24]{2,1,0:T(1,128)S(1)}, u32[]{:S(2)}, u32[]{:S(2)}) %all-to-all-start.3) | async-done | bytes 1568 | tf_op jit(solution)/shard_map/cond/branch_0_fun/all_to_all | solution.py:622
  20.4 1.2 %slot_cover.1 = f32[16,16,128]{2,1,0:T(8,128)S(1)} custom-call(s32[16,24]{1,0:T(8,128)S(1)} %bitcast.18, f32[128,256]{1,0:T(8,128)S(1)} %slice_bitcast_fusion.conc, s32[1,128]{1,0:T(1,128)} %get-tuple-element.50.covered, s32[128,256]{1,0:T(8,128)} %get-tuple-element.51.land), custom_call_target="tpu_custom_call" | custom-call | tf_op jit(solution)/shard_map/cond/branch_0_fun/slot_cover/pallas_call | solution.py:563
  21.6 1.1 %broadcast.15 = f32[16,144,128]{2,1,0:T(8,128)} broadcast(f32[]{:T(128)} %constant.4.clone), dimensions={} | broadcast | bytes 1179652 | tf_op jit(solution)/shard_map/broadcast.7
  22.7 0.1 broadcast.17
  22.8 0.1 broadcast.18
  22.8 0.6 %broadcast.16 = f32[34,128]{1,0:T(8,128)} broadcast(f32[]{:T(128)} %constant.4.clone), dimensions={} | broadcast | bytes 17412 | tf_op jit(solution)/shard_map/broadcast.6
  23.4 0.6 %broadcast.16.clone = f32[34,128]{1,0:T(8,128)} broadcast(f32[]{:T(128)} %constant.4.clone), dimensions={} | broadcast | bytes 17412 | tf_op jit(solution)/shard_map/broadcast.6
  24.0 5.4 %collective-permute-start.5 = (s32[16,24]{1,0:T(8,128)S(1)}, s32[16,24]{1,0:T(8,128)S(1)}, u32[]{:S(2)}, u32[]{:S(2)}) collective-permute-start(s32[16,24]{1,0:T(8,128)S(1)} %get-tuple-element.88), channel_id=1, source_target_pairs={{0,16},{16,0},{1,17},{17,1},{2,18},{18,2},{3,19},{19,3},{4,20},{20... | collective-permute-start | bytes 4616 | tf_op jit(solution)/shard_map/ppermute | solution.py:649
  29.5 1.3 %fetch.1 = (f32[16,144,128]{2,1,0:T(8,128)S(1)}, f32[34,128]{1,0:T(8,128)S(1)}, f32[34,128]{1,0:T(8,128)S(1)}) custom-call(f32[16,144,128]{2,1,0:T(8,128)} %get-tuple-element.89.refs_0_, f32[34,128]{1,0:T(8,128)} %get-tuple-element.90.refs_1_, f32[34,128]{1,0:T(8,128)} %get-tuple-element.91.refs_2_), custom_call_target="tpu_custom_call" | custom-call | tf_op jit(solution)/shard_map/fetch/pallas_call | solution.py:327
  30.8 0.0 collective-permute-done.5
  30.8 13.3 %conditional.4 = (f32[16,16,128]{2,1,0:T(8,128)S(1)}, f32[16,32,128]{2,1,0:T(8,128)S(1)}, f32[2,16,8,256]{3,2,1,0:T(8,128)S(1)}) conditional(s32[]{:T(128)} %convert_element_type.2, f32[16,16,128]{2,1,0:T(8,128)S(1)} %get-tuple-element.87, (s32[16,24]{1,0:T(8,128)S(1)}, f32[16,144,128]{2,1,0:T(8,128)S(1)}, f32[5,3,136,128]{3,2,1,0:T(8,128)S(1)}, ...), branch_computations={%region_2.0_spmd, %region_3.0_spmd} | conditional | bytes 786464 | solution.py:658
  30.8 13.2 %all_to_all.20 = f32[16,16,128]{2,1,0:T(8,128)S(1)} all-to-all(f32[16,16,128]{2,1,0:T(8,128)S(1)} %param.2), channel_id=1, replica_groups=mesh['comp'=2,'lat'=4,'lon'=4] {'lat','lon'}, dimensions={0} | all-to-all | bytes 262144 | tf_op jit(solution)/shard_map/cond/branch_0_fun/all_to_all | solution.py:622
  44.1 0.0 copy-start
  44.1 3.3 %collective-permute-start.6 = (f32[16,32,128]{2,1,0:T(8,128)S(1)}, f32[16,32,128]{2,1,0:T(8,128)S(1)}, u32[]{:S(2)}, u32[]{:S(2)}) collective-permute-start(f32[16,32,128]{2,1,0:T(8,128)S(1)} %get-tuple-element.120), channel_id=1, source_target_pairs={{0,16},{16,0},{1,17},{17,1},{2,18},{18,2},{3,19},{19,3},{4,20},{20... | collective-permute-start | bytes 786440 | tf_op jit(solution)/shard_map/ppermute | solution.py:662
  47.4 0.0 copy-done
  47.4 0.1 open_stress.1.opened
  47.5 1.1 %collective-permute-done.6.got = f32[16,32,128]{2,1,0:T(8,128)S(1)} collective-permute-done((f32[16,32,128]{2,1,0:T(8,128)S(1)}, f32[16,32,128]{2,1,0:T(8,128)S(1)}, u32[]{:S(2)}, u32[]{:S(2)}) %collective-permute-start.6) | collective-permute-done | bytes 262176 | tf_op jit(solution)/shard_map/ppermute | solution.py:662
  48.6 0.8 %final.1 = f32[2,16,8,256]{3,2,1,0:T(8,128)} custom-call(f32[16,32,128]{2,1,0:T(8,128)S(1)} %collective-permute-done.6.got, f32[16,16,128]{2,1,0:T(8,128)S(1)} %get-tuple-element.98.cover, f32[16,8,8,128]{3,2,1,0:T(8,128)S(1)} %open_stress.1.opened, f32[2,16,8,256]{3,2,1,0:T(8,128)S(1)} %get-tuple-element.99.moved), custom_call_target="tpu_custom_call" | custom-call | tf_op jit(solution)/shard_map/final/pallas_call | solution.py:600
  (4 shorter events, 0.1 us)
Async XLA Ops:
  0.0 2.8 %collective-permute-start.4 = (f32[7,16,8,256]{3,2,1,0:T(8,128)}, f32[7,16,8,256]{3,2,1,0:T(8,128)S(1)}, u32[]{:S(2)}, u32[]{:S(2)}) collective-permute-start(f32[7,16,8,256]{3,2,1,0:T(8,128)} %bitcast.12), channel_id=1, source_target_pairs={{0,16},{16,0},{1,17},{17,1},{2,18},{18,2},{3,19},{19,3},{4,20},{20... | collective-permute-start | bytes 2752520 | tf_op jit(solution)/shard_map/ppermute | solution.py:619
  4.3 16.0 %all-to-all-start.3 = ((s32[16,1,24]{2,1,0:T(1,128)}), s32[16,1,24]{2,1,0:T(1,128)S(1)}, u32[]{:S(2)}, u32[]{:S(2)}) async-start(s32[16,1,24]{2,1,0:T(1,128)} %bitcast.1), calls=%async_computation.3 | async-start | bytes 16384 | tf_op jit(solution)/shard_map/cond/branch_0_fun/all_to_all | solution.py:622
  24.0 6.7 %collective-permute-start.5 = (s32[16,24]{1,0:T(8,128)S(1)}, s32[16,24]{1,0:T(8,128)S(1)}, u32[]{:S(2)}, u32[]{:S(2)}) collective-permute-start(s32[16,24]{1,0:T(8,128)S(1)} %get-tuple-element.88), channel_id=1, source_target_pairs={{0,16},{16,0},{1,17},{17,1},{2,18},{18,2},{3,19},{19,3},{4,20},{20... | collective-permute-start | bytes 4616 | tf_op jit(solution)/shard_map/ppermute | solution.py:649
  44.1 3.3 %copy-start = (f32[1,7,128,256]{3,2,1,0:T(8,128)S(1)}, f32[1,7,128,256]{3,2,1,0:T(8,128)}, u32[]{:S(2)}) copy-start(f32[1,7,128,256]{3,2,1,0:T(8,128)} %param.10) | copy-start | bytes 2752516
  44.1 4.4 %collective-permute-start.6 = (f32[16,32,128]{2,1,0:T(8,128)S(1)}, f32[16,32,128]{2,1,0:T(8,128)S(1)}, u32[]{:S(2)}, u32[]{:S(2)}) collective-permute-start(f32[16,32,128]{2,1,0:T(8,128)S(1)} %get-tuple-element.120), channel_id=1, source_target_pairs={{0,16},{16,0},{1,17},{17,1},{2,18},{18,2},{3,19},{19,3},{4,20},{20... | collective-permute-start | bytes 786440 | tf_op jit(solution)/shard_map/ppermute | solution.py:662

commit v10 on v9

--- a/solution.py
+++ b/solution.py
@@ -59,7 +59,7 @@
         lax.fori_loop(lo, hi, body, 0)
 
 
-def pack_kernel(nlat, nlon, per, raw, owner, out, pay, edge, rim, sems):
+def pack_kernel(nlat, nlon, per, raw, owner_in, out, pay, edge, rim, owner, sems, ready):
     n = nlat * nlon
     count = n * per
     cut = 12 * per if (12 * per) % 8 == 0 else 0
@@ -68,6 +68,8 @@
         at = pl.ds(0, cut) if k == 0 else pl.ds(cut, 13 * per + 40 - cut)
         return pltpu.make_async_copy(pay.at[d, at], out.at[d, at], sems.at[k, d])
 
+    fetched = pltpu.make_async_copy(owner_in, owner, ready)
+    fetched.start()
     lane = lanes(per)
     group = lane // 8
     slot = lax.broadcasted_iota(jnp.int32, (per, BX), 0)
@@ -90,38 +92,54 @@
             pay[t, pl.ds(p, per, stride=12), :] = planes[p]
             ends = jnp.where(group == p, roll(planes[p], 8 * p + 4), ends)
         edge[t] = ends
+        if cut:
+            send(t, 0).start()
+        return 0
+
+    def rims(t, _):
+        planes = [pay[t, pl.ds(p, per, stride=12), :] for p in range(12)]
+        ends = edge[t]
         ids = jnp.zeros((per, BX), jnp.int32)
         for j in range(per):
             ids = jnp.where(slot == j, owner[0, t * per + j] - t * count, ids)
 
-        def pick(block, value):
-            return jnp.sum(jnp.where(ids == block, value, 0.0), axis=0, keepdims=True)
-
-        rows = [pick(0, x) for x in planes] + [pick(1, x) for x in planes[0::2]]
-        rows += [pick(count - 1, x) for x in planes]
-        rows += [pick(count - 2, x) for x in planes[1::2]]
-        rows += [pick(b, ends) for b in (0, 1, count - 1, count - 2)]
-        for k, row in enumerate(rows):
-            rim[t, k : k + 1, :] = row
-        if cut:
-            send(t, 0).start()
+        edges = (0, 1, count - 1, count - 2)
+        if per == 8:
+            where = [jnp.sum(jnp.where(ids == b, slot + 1, 0), axis=0, keepdims=True) for b in edges]
+            spot = jnp.zeros((per, BX), jnp.int32)
+            for k, x in enumerate(where):
+                spot = jnp.where(slot == k, x, spot)
+            held, spot = spot > 0, jnp.maximum(spot - 1, 0)
+            for p, x in enumerate(planes + [ends]):
+                rim[t, 8 * p : 8 * p + 8, :] = jnp.where(held, jnp.take_along_axis(x, spot, axis=0), 0.0)
+        else:
+            for p, x in enumerate(planes + [ends]):
+                for k, b in enumerate(edges):
+                    row = jnp.sum(jnp.where(ids == b, x, 0.0), axis=0, keepdims=True)
+                    rim[t, 8 * p + k : 8 * p + k + 1, :] = row
         return 0
 
     steps(0, n, tile)
+    fetched.wait()
+    steps(0, n, rims)
 
     def dest(d, _):
         i, j = d // nlon, d % nlon
         jw, je = (j + nlon - 1) % nlon, (j + 1) % nlon
         q8 = (lane % 8) < 4
         pay[d, 12 * per : 13 * per, :] = at_end(q8, edge[i * nlon + jw], edge[i * nlon + je])
-        for ii, ok, lo, c in (
-            (jnp.minimum(i + 1, nlat - 1), i + 1 < nlat, 0, 36),
-            (jnp.maximum(i - 1, 0), i > 0, 18, 38),
+        q2 = (lanes(2) % 8) < 4
+        for ii, ok, k, lo, c in (
+            (jnp.minimum(i + 1, nlat - 1), i + 1 < nlat, 0, 0, 36),
+            (jnp.maximum(i - 1, 0), i > 0, 2, 18, 38),
         ):
             scale = jnp.where(ok, 1.0, 0.0)
-            pay[d, lat_base + lo : lat_base + lo + 18, :] = rim[ii * nlon + j, lo : lo + 18, :] * scale
-            q2 = (lanes(2) % 8) < 4
-            corner = at_end(q2, rim[ii * nlon + jw, c : c + 2, :], rim[ii * nlon + je, c : c + 2, :])
+            near = ii * nlon + j
+            both = rim[near, pl.ds(k, 12, stride=8), :] * scale
+            single = rim[near, pl.ds(k + 1 + 4 * k, 6, stride=16), :] * scale
+            pay[d, lat_base + lo : lat_base + lo + 12, :] = both
+            pay[d, lat_base + lo + 12 : lat_base + lo + 18, :] = single
+            corner = at_end(q2, rim[ii * nlon + jw, 96 + k : 98 + k, :], rim[ii * nlon + je, 96 + k : 98 + k, :])
             pay[d, lat_base + c : lat_base + c + 2, :] = corner * scale
         send(d, 1).start()
         return 0
@@ -159,13 +177,15 @@
     return pl.pallas_call(
         functools.partial(pack_kernel, nlat, nlon, per),
         out_shape=f32(n, rows, BX),
-        in_specs=[VMEM, SMEM],
+        in_specs=[VMEM, pl.BlockSpec(memory_space=pl.ANY)],
         out_specs=pl.BlockSpec(memory_space=pl.ANY),
         scratch_shapes=[
             pltpu.VMEM((n, rows, BX), jnp.float32),
             pltpu.VMEM((n, per, BX), jnp.float32),
-            pltpu.VMEM((n, 40, BX), jnp.float32),
+            pltpu.VMEM((n, 104, BX), jnp.float32),
+            pltpu.SMEM(owner.shape, jnp.int32),
             pltpu.SemaphoreType.DMA((2, n)),
+            pltpu.SemaphoreType.DMA,
         ],
         compiler_params=params(24),
         name="pack",
@@ -347,10 +367,12 @@
     return jnp.where(at0, s, e), jnp.where(at0, roll(side, -63), o), wide
 
 
-def ice_kernel(n, per, count, ids, recv, begin, fixed, below, above, back, moved, unused,
-               spot, hw, he, speed, state, forced, out8, still):
+def ice_kernel(n, per, count, ids_in, recv, begin, fixed, below, above, back, moved, unused,
+               spot, hw, he, speed, state, forced, out8, still, ids, ready):
     tiles = (count + 4 + 7) // 8
     height = tiles * 8
+    fetched = pltpu.make_async_copy(ids_in, ids, ready)
+    fetched.start()
     blank = jnp.zeros((8, BX), jnp.float32)
     for k in (0, 8):
         spot[k : k + 8, :] = blank
@@ -359,29 +381,6 @@
     for k in (0, height - 8):
         hw[k : k + 8, :] = blank
         he[k : k + 8, :] = blank
-
-    def place(o, acc):
-        for j in range(per):
-            b = (ids[o, j] + 2) * STEP
-            spot[pl.ds(b, 12), :] = recv[o, 12 * j : 12 * j + 12, :]
-            row = recv[o, 12 * per + j : 12 * per + j + 1, :]
-            hw[pl.ds(ids[o, per + j] + 2, 1), :] = row
-            he[pl.ds(ids[o, 2 * per + j] + 2, 1), :] = row
-        return acc + recv[o, 13 * per : 13 * per + 40, :]
-
-    rim = lax.fori_loop(0, n, place, jnp.zeros((40, BX), jnp.float32))
-    up, down = (count + 2) * STEP, STEP
-    spot[up : up + 12, :] = rim[0:12]
-    spot[down : down + 12, :] = rim[18:30]
-    for ch in range(6):
-        k = up + STEP + 2 * ch
-        spot[k : k + 1, :] = rim[12 + ch : 13 + ch]
-        k = 2 * ch + 1
-        spot[k : k + 1, :] = rim[30 + ch : 31 + ch]
-    for ref in (hw, he):
-        ref[count + 2 : count + 4, :] = rim[36:38]
-        ref[1:2, :] = rim[38:39]
-        ref[0:1, :] = rim[39:40]
 
     q, mid, mid2 = (lanes(8) % 8) < 4, middle(8), middle(2)
     for r in range(tiles):
@@ -412,6 +411,31 @@
             for k, x in enumerate((hard, m2, CW * conc * act, act, conc)):
                 still[k, z, at, :] = x
 
+    fetched.wait()
+
+    def place(o, acc):
+        for j in range(per):
+            b = (ids[o, j] + 2) * STEP
+            spot[pl.ds(b, 12), :] = recv[o, 12 * j : 12 * j + 12, :]
+            row = recv[o, 12 * per + j : 12 * per + j + 1, :]
+            hw[pl.ds(ids[o, per + j] + 2, 1), :] = row
+            he[pl.ds(ids[o, 2 * per + j] + 2, 1), :] = row
+        return acc + recv[o, 13 * per : 13 * per + 40, :]
+
+    rim = lax.fori_loop(0, n, place, jnp.zeros((40, BX), jnp.float32))
+    up, down = (count + 2) * STEP, STEP
+    spot[up : up + 12, :] = rim[0:12]
+    spot[down : down + 12, :] = rim[18:30]
+    for ch in range(6):
+        k = up + STEP + 2 * ch
+        spot[k : k + 1, :] = rim[12 + ch : 13 + ch]
+        k = 2 * ch + 1
+        spot[k : k + 1, :] = rim[30 + ch : 31 + ch]
+    for ref in (hw, he):
+        ref[count + 2 : count + 4, :] = rim[36:38]
+        ref[1:2, :] = rim[38:39]
+        ref[0:1, :] = rim[39:40]
+
     for r in range(tiles):
         at = slice(8 * r, 8 * r + 8)
         ends = jnp.where(q, hw[at, :], he[at, :])
@@ -494,14 +518,14 @@
             speed[0, z, to, :] = part * (m2 * u + fx + forced[0, z, at, :] + drag * cx + mc * v)
             speed[1, z, to, :] = part * (m2 * v + fy + forced[1, z, at, :] + drag * cy - mc * u)
 
-    def subcycle(_, carry):
+    def subcycle():
         for r in range(tiles):
             stresses(r)
         for r in range(tiles):
             speeds(r)
-        return carry
-
-    lax.fori_loop(0, NSUB, subcycle, 0)
+
+    for _ in range(NSUB):
+        subcycle()
 
     for r in range(tiles):
         to = slice(FRONT + 8 * r, FRONT + 8 * r + 8)
@@ -533,9 +557,10 @@
     return pl.pallas_call(
         functools.partial(ice_kernel, n, per, count),
         out_shape=[f32(n, 4 * per, BX), f32(2, count, 2 * BX), f32(n, 2 * per, BX)],
-        in_specs=[SMEM] + [VMEM] * 5,
+        in_specs=[pl.BlockSpec(memory_space=pl.ANY)] + [VMEM] * 5,
         out_specs=[VMEM] * 3,
-        scratch_shapes=[pltpu.VMEM(s, jnp.float32) for s in scratch],
+        scratch_shapes=[pltpu.VMEM(s, jnp.float32) for s in scratch]
+        + [pltpu.SMEM(ids.shape, jnp.int32), pltpu.SemaphoreType.DMA],
         compiler_params=params(16),
         name="ice_step",
     )(ids, recv, begin, fixed, below, above)

time: 49.6 us -> 49.3 us (level)
  no operation moved by 1% of the time
where the time goes in v10:
time: 49.3 us; the launch traced here: 49 us
  starting transfers between devices  17.3 us (35%)
  blocking collectives  13.1 us (27%)
  waiting for transfers between devices  11.1 us (23%)
  Pallas kernels  4.96 us (10%)
  local copies, waits for them, and re-layouts  2.47 us (5%)
    all_to_all x1, blocking collectives, everyone(): lax.all_to_all(x, ('lat', 'lon'), split_axis=0, concat_axis=0, tiled=True)  13.1 us
    all_to_all x1, starting transfers between devices, everyone(): lax.all_to_all(x, ('lat', 'lon'), split_axis=0, concat_axis=0, tiled=True)  8.23 us
    all_to_all x1, waiting for transfers between devices, everyone(): lax.all_to_all(x, ('lat', 'lon'), split_axis=0, concat_axis=0, tiled=True)  7.77 us
    ppermute x1, starting transfers between devices, per_device(): swap = lax.ppermute(owned, 'comp', [(0, 1), (1, 0)])  5.32 us
    ppermute x1, starting transfers between devices, per_device(): got = lax.ppermute(back, 'comp', [(0, 1), (1, 0)])  3.23 us
    another operation x6, local copies, waits for them, and re-layouts  2.43 us
    ppermute x1, waiting for transfers between devices, per_device(): other = lax.ppermute(split, 'comp', [(0, 1), (1, 0)])  2.31 us
    pallas_call x1, Pallas kernels, table(): pl.pallas_call(functools.partial(table_kernel, nlat, nlon, per), out_shap...  1.52 us
  transfers between devices with their start and end apart: 4, of which 3 were waited for; matrix products, arithmetic and copies ran while one was open for 0% of the time, Pallas kernels for 3%

profile of v10, /device:TPU:0, one launch (start us, length us, event | category | flops | bytes accessed | tf_op | source)
XLA Modules:
  0.0 49.0 jit_solution(2707087265315261107)
XLA Ops:
  0.0 0.5 %collective-permute-start.4 = (f32[7,16,8,256]{3,2,1,0:T(8,128)}, f32[7,16,8,256]{3,2,1,0:T(8,128)S(1)}, u32[]{:S(2)}, u32[]{:S(2)}) collective-permute-start(f32[7,16,8,256]{3,2,1,0:T(8,128)} %bitcast.12), channel_id=1, source_target_pairs={{0,16},{16,0},{1,17},{17,1},{2,18},{18,2},{3,19},{19,3},{4,20},{20... | collective-permute-start | bytes 2752520 | tf_op jit(solution)/shard_map/ppermute | solution.py:644
  0.5 2.3 %collective-permute-done.4 = f32[7,16,8,256]{3,2,1,0:T(8,128)S(1)} collective-permute-done((f32[7,16,8,256]{3,2,1,0:T(8,128)}, f32[7,16,8,256]{3,2,1,0:T(8,128)S(1)}, u32[]{:S(2)}, u32[]{:S(2)}) %collective-permute-start.4) | collective-permute-done | bytes 917536 | tf_op jit(solution)/shard_map/ppermute | solution.py:644
  2.8 21.2 %conditional.3 = (f32[16,144,128]{2,1,0:T(8,128)}, s32[16,24]{1,0:T(8,128)S(1)}, f32[34,128]{1,0:T(8,128)}, f32[34,128]{1,0:T(8,128)}, f32[5,3,136,128]{3,2,1,0:...) conditional(s32[]{:T(128)} %convert_element_type.2, (s32[1,128]{1,0:T(1,128)}, ...), branch_computations={%region_0.0_spmd, %region_1.0_spmd} | conditional | bytes 8400720 | solution.py:671
  2.8 1.5 %table.1 = s32[16,24]{1,0:T(8,128)} custom-call(s32[1,128]{1,0:T(1,128)} %get-tuple-element.48.owner), custom_call_target="tpu_custom_call" | custom-call | tf_op jit(solution)/shard_map/cond/branch_0_fun/table/pallas_call | solution.py:252
  4.3 8.2 %all-to-all-start.3 = ((s32[16,1,24]{2,1,0:T(1,128)}), s32[16,1,24]{2,1,0:T(1,128)S(1)}, u32[]{:S(2)}, u32[]{:S(2)}) async-start(s32[16,1,24]{2,1,0:T(1,128)} %bitcast.1), calls=%async_computation.3 | async-start | bytes 16384 | tf_op jit(solution)/shard_map/cond/branch_0_fun/all_to_all | solution.py:647
  12.6 7.8 %all-to-all-done.3 = s32[16,1,24]{2,1,0:T(1,128)S(1)} async-done(((s32[16,1,24]{2,1,0:T(1,128)}), s32[16,1,24]{2,1,0:T(1,128)S(1)}, u32[]{:S(2)}, u32[]{:S(2)}) %all-to-all-start.3) | async-done | bytes 1568 | tf_op jit(solution)/shard_map/cond/branch_0_fun/all_to_all | solution.py:647
  20.4 1.2 %slot_cover.1 = f32[16,16,128]{2,1,0:T(8,128)S(1)} custom-call(s32[16,24]{1,0:T(8,128)S(1)} %bitcast.18, f32[128,256]{1,0:T(8,128)S(1)} %slice_bitcast_fusion.conc, s32[1,128]{1,0:T(1,128)} %get-tuple-element.50.covered, s32[128,256]{1,0:T(8,128)} %get-tuple-element.51.land), custom_call_target="tpu_custom_call" | custom-call | tf_op jit(solution)/shard_map/cond/branch_0_fun/slot_cover/pallas_call | solution.py:588
  21.6 1.1 %broadcast.15 = f32[16,144,128]{2,1,0:T(8,128)} broadcast(f32[]{:T(128)} %constant.4.clone), dimensions={} | broadcast | bytes 1179652 | tf_op jit(solution)/shard_map/broadcast.7
  22.7 0.1 broadcast.17
  22.8 0.1 broadcast.18
  22.8 0.6 %broadcast.16 = f32[34,128]{1,0:T(8,128)} broadcast(f32[]{:T(128)} %constant.4.clone), dimensions={} | broadcast | bytes 17412 | tf_op jit(solution)/shard_map/broadcast.6
  23.4 0.6 %broadcast.16.clone = f32[34,128]{1,0:T(8,128)} broadcast(f32[]{:T(128)} %constant.4.clone), dimensions={} | broadcast | bytes 17412 | tf_op jit(solution)/shard_map/broadcast.6
  24.0 5.3 %collective-permute-start.5 = (s32[16,24]{1,0:T(8,128)S(1)}, s32[16,24]{1,0:T(8,128)S(1)}, u32[]{:S(2)}, u32[]{:S(2)}) collective-permute-start(s32[16,24]{1,0:T(8,128)S(1)} %get-tuple-element.88), channel_id=1, source_target_pairs={{0,16},{16,0},{1,17},{17,1},{2,18},{18,2},{3,19},{19,3},{4,20},{20... | collective-permute-start | bytes 4616 | tf_op jit(solution)/shard_map/ppermute | solution.py:674
  29.4 1.3 %fetch.1 = (f32[16,144,128]{2,1,0:T(8,128)S(1)}, f32[34,128]{1,0:T(8,128)S(1)}, f32[34,128]{1,0:T(8,128)S(1)}) custom-call(f32[16,144,128]{2,1,0:T(8,128)} %get-tuple-element.89.refs_0_, f32[34,128]{1,0:T(8,128)} %get-tuple-element.90.refs_1_, f32[34,128]{1,0:T(8,128)} %get-tuple-element.91.refs_2_), custom_call_target="tpu_custom_call" | custom-call | tf_op jit(solution)/shard_map/fetch/pallas_call | solution.py:347
  30.7 0.0 collective-permute-done.5
  30.7 13.1 %conditional.4 = (f32[16,16,128]{2,1,0:T(8,128)S(1)}, f32[16,32,128]{2,1,0:T(8,128)S(1)}, f32[2,16,8,256]{3,2,1,0:T(8,128)S(1)}) conditional(s32[]{:T(128)} %convert_element_type.2, f32[16,16,128]{2,1,0:T(8,128)S(1)} %get-tuple-element.87, (s32[16,24]{1,0:T(8,128)S(1)}, f32[16,144,128]{2,1,0:T(8,128)S(1)}, f32[5,3,136,128]{3,2,1,0:T(8,128)S(1)}, ...), branch_computations={%region_2.0_spmd, %region_3.0_spmd} | conditional | bytes 786464 | solution.py:683
  30.7 13.1 %all_to_all.20 = f32[16,16,128]{2,1,0:T(8,128)S(1)} all-to-all(f32[16,16,128]{2,1,0:T(8,128)S(1)} %param.2), channel_id=1, replica_groups=mesh['comp'=2,'lat'=4,'lon'=4] {'lat','lon'}, dimensions={0} | all-to-all | bytes 262144 | tf_op jit(solution)/shard_map/cond/branch_0_fun/all_to_all | solution.py:647
  43.8 0.0 copy-start
  43.8 3.2 %collective-permute-start.6 = (f32[16,32,128]{2,1,0:T(8,128)S(1)}, f32[16,32,128]{2,1,0:T(8,128)S(1)}, u32[]{:S(2)}, u32[]{:S(2)}) collective-permute-start(f32[16,32,128]{2,1,0:T(8,128)S(1)} %get-tuple-element.120), channel_id=1, source_target_pairs={{0,16},{16,0},{1,17},{17,1},{2,18},{18,2},{3,19},{19,3},{4,20},{20... | collective-permute-start | bytes 786440 | tf_op jit(solution)/shard_map/ppermute | solution.py:687
  47.1 0.0 copy-done
  47.1 0.1 open_stress.1.opened
  47.2 1.1 %collective-permute-done.6.got = f32[16,32,128]{2,1,0:T(8,128)S(1)} collective-permute-done((f32[16,32,128]{2,1,0:T(8,128)S(1)}, f32[16,32,128]{2,1,0:T(8,128)S(1)}, u32[]{:S(2)}, u32[]{:S(2)}) %collective-permute-start.6) | collective-permute-done | bytes 262176 | tf_op jit(solution)/shard_map/ppermute | solution.py:687
  48.2 0.8 %final.1 = f32[2,16,8,256]{3,2,1,0:T(8,128)} custom-call(f32[16,32,128]{2,1,0:T(8,128)S(1)} %collective-permute-done.6.got, f32[16,16,128]{2,1,0:T(8,128)S(1)} %get-tuple-element.98.cover, f32[16,8,8,128]{3,2,1,0:T(8,128)S(1)} %open_stress.1.opened, f32[2,16,8,256]{3,2,1,0:T(8,128)S(1)} %get-tuple-element.99.moved), custom_call_target="tpu_custom_call" | custom-call | tf_op jit(solution)/shard_map/final/pallas_call | solution.py:625
  (4 shorter events, 0.1 us)
Async XLA Ops:
  0.0 2.8 %collective-permute-start.4 = (f32[7,16,8,256]{3,2,1,0:T(8,128)}, f32[7,16,8,256]{3,2,1,0:T(8,128)S(1)}, u32[]{:S(2)}, u32[]{:S(2)}) collective-permute-start(f32[7,16,8,256]{3,2,1,0:T(8,128)} %bitcast.12), channel_id=1, source_target_pairs={{0,16},{16,0},{1,17},{17,1},{2,18},{18,2},{3,19},{19,3},{4,20},{20... | collective-permute-start | bytes 2752520 | tf_op jit(solution)/shard_map/ppermute | solution.py:644
  4.3 16.0 %all-to-all-start.3 = ((s32[16,1,24]{2,1,0:T(1,128)}), s32[16,1,24]{2,1,0:T(1,128)S(1)}, u32[]{:S(2)}, u32[]{:S(2)}) async-start(s32[16,1,24]{2,1,0:T(1,128)} %bitcast.1), calls=%async_computation.3 | async-start | bytes 16384 | tf_op jit(solution)/shard_map/cond/branch_0_fun/all_to_all | solution.py:647
  24.0 6.6 %collective-permute-start.5 = (s32[16,24]{1,0:T(8,128)S(1)}, s32[16,24]{1,0:T(8,128)S(1)}, u32[]{:S(2)}, u32[]{:S(2)}) collective-permute-start(s32[16,24]{1,0:T(8,128)S(1)} %get-tuple-element.88), channel_id=1, source_target_pairs={{0,16},{16,0},{1,17},{17,1},{2,18},{18,2},{3,19},{19,3},{4,20},{20... | collective-permute-start | bytes 4616 | tf_op jit(solution)/shard_map/ppermute | solution.py:674
  43.8 3.3 %copy-start = (f32[1,7,128,256]{3,2,1,0:T(8,128)S(1)}, f32[1,7,128,256]{3,2,1,0:T(8,128)}, u32[]{:S(2)}) copy-start(f32[1,7,128,256]{3,2,1,0:T(8,128)} %param.10) | copy-start | bytes 2752516
  43.8 4.4 %collective-permute-start.6 = (f32[16,32,128]{2,1,0:T(8,128)S(1)}, f32[16,32,128]{2,1,0:T(8,128)S(1)}, u32[]{:S(2)}, u32[]{:S(2)}) collective-permute-start(f32[16,32,128]{2,1,0:T(8,128)S(1)} %get-tuple-element.120), channel_id=1, source_target_pairs={{0,16},{16,0},{1,17},{17,1},{2,18},{18,2},{3,19},{19,3},{4,20},{20... | collective-permute-start | bytes 786440 | tf_op jit(solution)/shard_map/ppermute | solution.py:687

commit v11 on v10

--- a/solution.py
+++ b/solution.py
@@ -336,7 +336,12 @@
 
 def fetch_kernel(*refs):
     k = len(refs) // 2
-    copies = [pltpu.make_async_copy(refs[i], refs[k + i], refs[-1].at[i]) for i in range(k)]
+    big, parts = refs[0].shape[0], 4
+    pieces = [(0, pl.ds(c * big // parts, big // parts)) for c in range(parts)] if big % parts == 0 else [(0, pl.ds(0, big))]
+    pieces += [(i, pl.ds(0, refs[i].shape[0])) for i in range(1, k)]
+    copies = [
+        pltpu.make_async_copy(refs[i].at[at], refs[k + i].at[at], refs[-1].at[c]) for c, (i, at) in enumerate(pieces)
+    ]
     for copy in copies:
         copy.start()
     for copy in copies:
@@ -349,7 +354,7 @@
         out_shape=[f32(*x.shape) for x in arrays],
         in_specs=[pl.BlockSpec(memory_space=pl.ANY)] * len(arrays),
         out_specs=[VMEM] * len(arrays),
-        scratch_shapes=[pltpu.SemaphoreType.DMA((len(arrays),))],
+        scratch_shapes=[pltpu.SemaphoreType.DMA((len(arrays) + 3,))],
         compiler_params=params(4),
         name="fetch",
     )(*arrays)
@@ -422,7 +427,12 @@
             he[pl.ds(ids[o, 2 * per + j] + 2, 1), :] = row
         return acc + recv[o, 13 * per : 13 * per + 40, :]
 
-    rim = lax.fori_loop(0, n, place, jnp.zeros((40, BX), jnp.float32))
+    rim = jnp.zeros((40, BX), jnp.float32)
+    if n <= 32:
+        for o in range(n):
+            rim = place(o, rim)
+    else:
+        rim = lax.fori_loop(0, n, place, rim)
     up, down = (count + 2) * STEP, STEP
     spot[up : up + 12, :] = rim[0:12]
     spot[down : down + 12, :] = rim[18:30]
@@ -542,7 +552,7 @@
             back[o, 4 * j : 4 * j + 4, :] = out8[pl.ds(b, 4), :]
         return 0
 
-    lax.fori_loop(0, n, answer, 0)
+    steps(0, n, answer)
 
 
 def ice_step(ids, recv, begin, fixed, below, above):

time: 49.3 us -> 49 us (level)
  no operation moved by 1% of the time
where the time goes in v11:
time: 49 us; the launch traced here: 48.7 us
  starting transfers between devices  17.1 us (35%)
  blocking collectives  13 us (27%)
  waiting for transfers between devices  11.1 us (23%)
  Pallas kernels  4.94 us (10%)
  local copies, waits for them, and re-layouts  2.47 us (5%)
    all_to_all x1, blocking collectives, everyone(): lax.all_to_all(x, ('lat', 'lon'), split_axis=0, concat_axis=0, tiled=True)  13 us
    all_to_all x1, starting transfers between devices, everyone(): lax.all_to_all(x, ('lat', 'lon'), split_axis=0, concat_axis=0, tiled=True)  8.23 us
    all_to_all x1, waiting for transfers between devices, everyone(): lax.all_to_all(x, ('lat', 'lon'), split_axis=0, concat_axis=0, tiled=True)  7.77 us
    ppermute x1, starting transfers between devices, per_device(): swap = lax.ppermute(owned, 'comp', [(0, 1), (1, 0)])  5.32 us
    ppermute x1, starting transfers between devices, per_device(): got = lax.ppermute(back, 'comp', [(0, 1), (1, 0)])  3.03 us
    another operation x6, local copies, waits for them, and re-layouts  2.43 us
    ppermute x1, waiting for transfers between devices, per_device(): other = lax.ppermute(split, 'comp', [(0, 1), (1, 0)])  2.31 us
    pallas_call x1, Pallas kernels, table(): pl.pallas_call(functools.partial(table_kernel, nlat, nlon, per), out_shap...  1.52 us
  transfers between devices with their start and end apart: 4, of which 3 were waited for; matrix products, arithmetic and copies ran while one was open for 0% of the time, Pallas kernels for 3%

profile of v11, /device:TPU:0, one launch (start us, length us, event | category | flops | bytes accessed | tf_op | source)
XLA Modules:
  0.0 48.7 jit_solution(8349894206263424389)
XLA Ops:
  0.0 0.5 %collective-permute-start.4 = (f32[7,16,8,256]{3,2,1,0:T(8,128)}, f32[7,16,8,256]{3,2,1,0:T(8,128)S(1)}, u32[]{:S(2)}, u32[]{:S(2)}) collective-permute-start(f32[7,16,8,256]{3,2,1,0:T(8,128)} %bitcast.12), channel_id=1, source_target_pairs={{0,16},{16,0},{1,17},{17,1},{2,18},{18,2},{3,19},{19,3},{4,20},{20... | collective-permute-start | bytes 2752520 | tf_op jit(solution)/shard_map/ppermute | solution.py:654
  0.5 2.3 %collective-permute-done.4 = f32[7,16,8,256]{3,2,1,0:T(8,128)S(1)} collective-permute-done((f32[7,16,8,256]{3,2,1,0:T(8,128)}, f32[7,16,8,256]{3,2,1,0:T(8,128)S(1)}, u32[]{:S(2)}, u32[]{:S(2)}) %collective-permute-start.4) | collective-permute-done | bytes 917536 | tf_op jit(solution)/shard_map/ppermute | solution.py:654
  2.8 21.2 %conditional.3 = (f32[16,144,128]{2,1,0:T(8,128)}, s32[16,24]{1,0:T(8,128)S(1)}, f32[34,128]{1,0:T(8,128)}, f32[34,128]{1,0:T(8,128)}, f32[5,3,136,128]{3,2,1,0:...) conditional(s32[]{:T(128)} %convert_element_type.2, (s32[1,128]{1,0:T(1,128)}, ...), branch_computations={%region_0.0_spmd, %region_1.0_spmd} | conditional | bytes 8400720 | solution.py:681
  2.8 1.5 %table.1 = s32[16,24]{1,0:T(8,128)} custom-call(s32[1,128]{1,0:T(1,128)} %get-tuple-element.48.owner), custom_call_target="tpu_custom_call" | custom-call | tf_op jit(solution)/shard_map/cond/branch_0_fun/table/pallas_call | solution.py:252
  4.3 8.2 %all-to-all-start.3 = ((s32[16,1,24]{2,1,0:T(1,128)}), s32[16,1,24]{2,1,0:T(1,128)S(1)}, u32[]{:S(2)}, u32[]{:S(2)}) async-start(s32[16,1,24]{2,1,0:T(1,128)} %bitcast.1), calls=%async_computation.3 | async-start | bytes 16384 | tf_op jit(solution)/shard_map/cond/branch_0_fun/all_to_all | solution.py:657
  12.6 7.8 %all-to-all-done.3 = s32[16,1,24]{2,1,0:T(1,128)S(1)} async-done(((s32[16,1,24]{2,1,0:T(1,128)}), s32[16,1,24]{2,1,0:T(1,128)S(1)}, u32[]{:S(2)}, u32[]{:S(2)}) %all-to-all-start.3) | async-done | bytes 1568 | tf_op jit(solution)/shard_map/cond/branch_0_fun/all_to_all | solution.py:657
  20.4 1.2 %slot_cover.1 = f32[16,16,128]{2,1,0:T(8,128)S(1)} custom-call(s32[16,24]{1,0:T(8,128)S(1)} %bitcast.18, f32[128,256]{1,0:T(8,128)S(1)} %slice_bitcast_fusion.conc, s32[1,128]{1,0:T(1,128)} %get-tuple-element.50.covered, s32[128,256]{1,0:T(8,128)} %get-tuple-element.51.land), custom_call_target="tpu_custom_call" | custom-call | tf_op jit(solution)/shard_map/cond/branch_0_fun/slot_cover/pallas_call | solution.py:598
  21.6 1.1 %broadcast.15 = f32[16,144,128]{2,1,0:T(8,128)} broadcast(f32[]{:T(128)} %constant.4.clone), dimensions={} | broadcast | bytes 1179652 | tf_op jit(solution)/shard_map/broadcast.7
  22.7 0.1 broadcast.17
  22.8 0.1 broadcast.18
  22.8 0.6 %broadcast.16 = f32[34,128]{1,0:T(8,128)} broadcast(f32[]{:T(128)} %constant.4.clone), dimensions={} | broadcast | bytes 17412 | tf_op jit(solution)/shard_map/broadcast.6
  23.4 0.6 %broadcast.16.clone = f32[34,128]{1,0:T(8,128)} broadcast(f32[]{:T(128)} %constant.4.clone), dimensions={} | broadcast | bytes 17412 | tf_op jit(solution)/shard_map/broadcast.6
  24.0 5.3 %collective-permute-start.5 = (s32[16,24]{1,0:T(8,128)S(1)}, s32[16,24]{1,0:T(8,128)S(1)}, u32[]{:S(2)}, u32[]{:S(2)}) collective-permute-start(s32[16,24]{1,0:T(8,128)S(1)} %get-tuple-element.88), channel_id=1, source_target_pairs={{0,16},{16,0},{1,17},{17,1},{2,18},{18,2},{3,19},{19,3},{4,20},{20... | collective-permute-start | bytes 4616 | tf_op jit(solution)/shard_map/ppermute | solution.py:684
  29.4 1.3 %fetch.1 = (f32[16,144,128]{2,1,0:T(8,128)S(1)}, f32[34,128]{1,0:T(8,128)S(1)}, f32[34,128]{1,0:T(8,128)S(1)}) custom-call(f32[16,144,128]{2,1,0:T(8,128)} %get-tuple-element.89.refs_0_, f32[34,128]{1,0:T(8,128)} %get-tuple-element.90.refs_1_, f32[34,128]{1,0:T(8,128)} %get-tuple-element.91.refs_2_), custom_call_target="tpu_custom_call" | custom-call | tf_op jit(solution)/shard_map/fetch/pallas_call | solution.py:352
  30.6 0.0 collective-permute-done.5
  30.7 13.0 %conditional.4 = (f32[16,16,128]{2,1,0:T(8,128)S(1)}, f32[16,32,128]{2,1,0:T(8,128)S(1)}, f32[2,16,8,256]{3,2,1,0:T(8,128)S(1)}) conditional(s32[]{:T(128)} %convert_element_type.2, f32[16,16,128]{2,1,0:T(8,128)S(1)} %get-tuple-element.87, (s32[16,24]{1,0:T(8,128)S(1)}, f32[16,144,128]{2,1,0:T(8,128)S(1)}, f32[5,3,136,128]{3,2,1,0:T(8,128)S(1)}, ...), branch_computations={%region_2.0_spmd, %region_3.0_spmd} | conditional | bytes 786464 | solution.py:693
  30.7 13.0 %all_to_all.20 = f32[16,16,128]{2,1,0:T(8,128)S(1)} all-to-all(f32[16,16,128]{2,1,0:T(8,128)S(1)} %param.2), channel_id=1, replica_groups=mesh['comp'=2,'lat'=4,'lon'=4] {'lat','lon'}, dimensions={0} | all-to-all | bytes 262144 | tf_op jit(solution)/shard_map/cond/branch_0_fun/all_to_all | solution.py:657
  43.7 0.0 copy-start
  43.7 3.0 %collective-permute-start.6 = (f32[16,32,128]{2,1,0:T(8,128)S(1)}, f32[16,32,128]{2,1,0:T(8,128)S(1)}, u32[]{:S(2)}, u32[]{:S(2)}) collective-permute-start(f32[16,32,128]{2,1,0:T(8,128)S(1)} %get-tuple-element.120), channel_id=1, source_target_pairs={{0,16},{16,0},{1,17},{17,1},{2,18},{18,2},{3,19},{19,3},{4,20},{20... | collective-permute-start | bytes 786440 | tf_op jit(solution)/shard_map/ppermute | solution.py:697
  46.7 0.0 copy-done
  46.7 0.1 open_stress.1.opened
  46.9 1.1 %collective-permute-done.6.got = f32[16,32,128]{2,1,0:T(8,128)S(1)} collective-permute-done((f32[16,32,128]{2,1,0:T(8,128)S(1)}, f32[16,32,128]{2,1,0:T(8,128)S(1)}, u32[]{:S(2)}, u32[]{:S(2)}) %collective-permute-start.6) | collective-permute-done | bytes 262176 | tf_op jit(solution)/shard_map/ppermute | solution.py:697
  47.9 0.8 %final.1 = f32[2,16,8,256]{3,2,1,0:T(8,128)} custom-call(f32[16,32,128]{2,1,0:T(8,128)S(1)} %collective-permute-done.6.got, f32[16,16,128]{2,1,0:T(8,128)S(1)} %get-tuple-element.98.cover, f32[16,8,8,128]{3,2,1,0:T(8,128)S(1)} %open_stress.1.opened, f32[2,16,8,256]{3,2,1,0:T(8,128)S(1)} %get-tuple-element.99.moved), custom_call_target="tpu_custom_call" | custom-call | tf_op jit(solution)/shard_map/final/pallas_call | solution.py:635
  (4 shorter events, 0.1 us)
Async XLA Ops:
  0.0 2.8 %collective-permute-start.4 = (f32[7,16,8,256]{3,2,1,0:T(8,128)}, f32[7,16,8,256]{3,2,1,0:T(8,128)S(1)}, u32[]{:S(2)}, u32[]{:S(2)}) collective-permute-start(f32[7,16,8,256]{3,2,1,0:T(8,128)} %bitcast.12), channel_id=1, source_target_pairs={{0,16},{16,0},{1,17},{17,1},{2,18},{18,2},{3,19},{19,3},{4,20},{20... | collective-permute-start | bytes 2752520 | tf_op jit(solution)/shard_map/ppermute | solution.py:654
  4.3 16.0 %all-to-all-start.3 = ((s32[16,1,24]{2,1,0:T(1,128)}), s32[16,1,24]{2,1,0:T(1,128)S(1)}, u32[]{:S(2)}, u32[]{:S(2)}) async-start(s32[16,1,24]{2,1,0:T(1,128)} %bitcast.1), calls=%async_computation.3 | async-start | bytes 16384 | tf_op jit(solution)/shard_map/cond/branch_0_fun/all_to_all | solution.py:657
  24.0 6.6 %collective-permute-start.5 = (s32[16,24]{1,0:T(8,128)S(1)}, s32[16,24]{1,0:T(8,128)S(1)}, u32[]{:S(2)}, u32[]{:S(2)}) collective-permute-start(s32[16,24]{1,0:T(8,128)S(1)} %get-tuple-element.88), channel_id=1, source_target_pairs={{0,16},{16,0},{1,17},{17,1},{2,18},{18,2},{3,19},{19,3},{4,20},{20... | collective-permute-start | bytes 4616 | tf_op jit(solution)/shard_map/ppermute | solution.py:684
  43.7 3.1 %copy-start = (f32[1,7,128,256]{3,2,1,0:T(8,128)S(1)}, f32[1,7,128,256]{3,2,1,0:T(8,128)}, u32[]{:S(2)}) copy-start(f32[1,7,128,256]{3,2,1,0:T(8,128)} %param.10) | copy-start | bytes 2752516
  43.7 4.2 %collective-permute-start.6 = (f32[16,32,128]{2,1,0:T(8,128)S(1)}, f32[16,32,128]{2,1,0:T(8,128)S(1)}, u32[]{:S(2)}, u32[]{:S(2)}) collective-permute-start(f32[16,32,128]{2,1,0:T(8,128)S(1)} %get-tuple-element.120), channel_id=1, source_target_pairs={{0,16},{16,0},{1,17},{17,1},{2,18},{18,2},{3,19},{19,3},{4,20},{20... | collective-permute-start | bytes 786440 | tf_op jit(solution)/shard_map/ppermute | solution.py:697

commit v12 on v11

--- a/solution.py
+++ b/solution.py
@@ -59,7 +59,7 @@
         lax.fori_loop(lo, hi, body, 0)
 
 
-def pack_kernel(nlat, nlon, per, raw, owner_in, out, pay, edge, rim, owner, sems, ready):
+def pack_kernel(nlat, nlon, per, raw, spread, out, pay, edge, rim, sems):
     n = nlat * nlon
     count = n * per
     cut = 12 * per if (12 * per) % 8 == 0 else 0
@@ -68,8 +68,6 @@
         at = pl.ds(0, cut) if k == 0 else pl.ds(cut, 13 * per + 40 - cut)
         return pltpu.make_async_copy(pay.at[d, at], out.at[d, at], sems.at[k, d])
 
-    fetched = pltpu.make_async_copy(owner_in, owner, ready)
-    fetched.start()
     lane = lanes(per)
     group = lane // 8
     slot = lax.broadcasted_iota(jnp.int32, (per, BX), 0)
@@ -99,10 +97,7 @@
     def rims(t, _):
         planes = [pay[t, pl.ds(p, per, stride=12), :] for p in range(12)]
         ends = edge[t]
-        ids = jnp.zeros((per, BX), jnp.int32)
-        for j in range(per):
-            ids = jnp.where(slot == j, owner[0, t * per + j] - t * count, ids)
-
+        ids = spread[t]
         edges = (0, 1, count - 1, count - 2)
         if per == 8:
             where = [jnp.sum(jnp.where(ids == b, slot + 1, 0), axis=0, keepdims=True) for b in edges]
@@ -120,7 +115,6 @@
         return 0
 
     steps(0, n, tile)
-    fetched.wait()
     steps(0, n, rims)
 
     def dest(d, _):
@@ -171,25 +165,48 @@
     ends[...] = total
 
 
-def pack(raw, owner, nlat, nlon):
+def pack(raw, spread, nlat, nlon):
     _, n, per, _ = raw.shape
     rows = 13 * per + 40
     return pl.pallas_call(
         functools.partial(pack_kernel, nlat, nlon, per),
         out_shape=f32(n, rows, BX),
-        in_specs=[VMEM, pl.BlockSpec(memory_space=pl.ANY)],
+        in_specs=[VMEM, VMEM],
         out_specs=pl.BlockSpec(memory_space=pl.ANY),
         scratch_shapes=[
             pltpu.VMEM((n, rows, BX), jnp.float32),
             pltpu.VMEM((n, per, BX), jnp.float32),
             pltpu.VMEM((n, 104, BX), jnp.float32),
-            pltpu.SMEM(owner.shape, jnp.int32),
             pltpu.SemaphoreType.DMA((2, n)),
-            pltpu.SemaphoreType.DMA,
         ],
         compiler_params=params(24),
         name="pack",
-    )(raw, owner)
+    )(raw, spread)
+
+
+def spread_kernel(n, per, owner, out):
+    slot = lax.broadcasted_iota(jnp.int32, (per, BX), 0)
+
+    def tile(t, _):
+        ids = jnp.zeros((per, BX), jnp.int32)
+        for j in range(per):
+            ids = jnp.where(slot == j, owner[0, t * per + j] - t * (n * per), ids)
+        out[t] = ids
+        return 0
+
+    steps(0, n, tile)
+
+
+def spread_ids(owner, n):
+    per = owner.shape[1] // n
+    return pl.pallas_call(
+        functools.partial(spread_kernel, n, per),
+        out_shape=jax.ShapeDtypeStruct((n, per, BX), jnp.int32),
+        in_specs=[SMEM],
+        out_specs=VMEM,
+        compiler_params=params(4),
+        name="spread",
+    )(owner)
 
 
 def open_kernel(n, per, raw, opened):
@@ -658,8 +675,8 @@
 
     height = (count + 4 + 7) // 8 * 8
 
-    def ice_side(other, fields, covered, land, owner):
-        recv = everyone(pack(other, owner, nlat, nlon))
+    def ice_side(other, fields, covered, land, owner, spread):
+        recv = everyone(pack(other, spread, nlat, nlon))
         active, ends = ice_ends(fields, covered, land)
         ring = [(i, (i + 1) % nlon) for i in range(nlon)]
         west = lax.ppermute(ends, "lon", ring)
@@ -671,7 +688,7 @@
         begin, fixed, mine = prep(fields, active, sides, (n, 2 * per, BX))
         return recv, jnp.zeros((n, 3 * per), jnp.int32), below, above, begin, fixed, mine
 
-    def ocean_side(other, fields, covered, land, owner):
+    def ocean_side(other, fields, covered, land, owner, spread):
         row = jnp.zeros((34, BX), jnp.float32)
         blank = jnp.zeros((5, 3, height, BX), jnp.float32)
         owned = everyone(table(owner, nlat, nlon))
@@ -679,7 +696,7 @@
         return jnp.zeros((n, 13 * per + 40, BX), jnp.float32), owned, row, row, blank, blank[:4], mine
 
     recv, owned, below, above, begin, fixed, mine = lax.cond(
-        side == 1, ice_side, ocean_side, other, fields, ice_covered.reshape(1, count), land_mask, owner
+        side == 1, ice_side, ocean_side, other, fields, ice_covered.reshape(1, count), land_mask, owner, spread_ids(owner, n)
     )
     swap = lax.ppermute(owned, "comp", [(0, 1), (1, 0)])
     recv, below, above = fetch(recv, below, above)

time: 49 us -> 48.2 us (0.984)
  starting transfers between devices: 17.1 us -> 16.3 us
  waiting for transfers between devices: 11.1 us -> 10.3 us
  Pallas kernels: 4.94 us -> 5.68 us
    ppermute x1, waiting for transfers between devices: 2.31 us -> 1.57 us  [per_device(): other = lax.ppermute(split, 'comp', [(0, 1), (1, 0)])]
    pallas_call x0 -> x1, Pallas kernels: none -> 0.73 us  [spread_ids(): pl.pallas_call(functools.partial(spread_kernel, n, per), out_shape=jax.Sh...]
    ppermute x1, starting transfers between devices: 5.32 us -> 4.59 us  [per_device(): swap = lax.ppermute(owned, 'comp', [(0, 1), (1, 0)])]
  transfers between devices with their start and end apart: 4 -> 4, of which waited for: 3 -> 3; matrix products, arithmetic and copies ran while one was open for 0% -> 0% of each run, Pallas kernels for 3% -> 4%
where the time goes in v12:
time: 48.2 us; the launch traced here: 47.9 us
  starting transfers between devices  16.3 us (34%)
  blocking collectives  13 us (27%)
  waiting for transfers between devices  10.3 us (21%)
  Pallas kernels  5.68 us (12%)
  local copies, waits for them, and re-layouts  2.47 us (5%)
    all_to_all x1, blocking collectives, everyone(): lax.all_to_all(x, ('lat', 'lon'), split_axis=0, concat_axis=0, tiled=True)  13 us
    all_to_all x1, starting transfers between devices, everyone(): lax.all_to_all(x, ('lat', 'lon'), split_axis=0, concat_axis=0, tiled=True)  8.23 us
    all_to_all x1, waiting for transfers between devices, everyone(): lax.all_to_all(x, ('lat', 'lon'), split_axis=0, concat_axis=0, tiled=True)  7.7 us
    ppermute x1, starting transfers between devices, per_device(): swap = lax.ppermute(owned, 'comp', [(0, 1), (1, 0)])  4.59 us
    ppermute x1, starting transfers between devices, per_device(): got = lax.ppermute(back, 'comp', [(0, 1), (1, 0)])  3.03 us
    another operation x6, local copies, waits for them, and re-layouts  2.43 us
    ppermute x1, waiting for transfers between devices, per_device(): other = lax.ppermute(split, 'comp', [(0, 1), (1, 0)])  1.57 us
    pallas_call x1, Pallas kernels, table(): pl.pallas_call(functools.partial(table_kernel, nlat, nlon, per), out_shap...  1.52 us
  transfers between devices with their start and end apart: 4, of which 3 were waited for; matrix products, arithmetic and copies ran while one was open for 0% of the time, Pallas kernels for 4%

profile of v12, /device:TPU:0, one launch (start us, length us, event | category | flops | bytes accessed | tf_op | source)
XLA Modules:
  0.0 47.9 jit_solution(11989814534654401323)
XLA Ops:
  0.0 0.5 %collective-permute-start.4 = (f32[7,16,8,256]{3,2,1,0:T(8,128)}, f32[7,16,8,256]{3,2,1,0:T(8,128)S(1)}, u32[]{:S(2)}, u32[]{:S(2)}) collective-permute-start(f32[7,16,8,256]{3,2,1,0:T(8,128)} %bitcast.12), channel_id=1, source_target_pairs={{0,16},{16,0},{1,17},{17,1},{2,18},{18,2},{3,19},{19,3},{4,20},{20... | collective-permute-start | bytes 2752520 | tf_op jit(solution)/shard_map/ppermute | solution.py:671
  0.5 0.7 %spread.1 = s32[16,8,128]{2,1,0:T(8,128)S(1)} custom-call(s32[1,128]{1,0:T(1,128)} %bitcast.22), custom_call_target="tpu_custom_call" | custom-call | tf_op jit(solution)/shard_map/spread/pallas_call | solution.py:202
  1.2 1.6 %collective-permute-done.4 = f32[7,16,8,256]{3,2,1,0:T(8,128)S(1)} collective-permute-done((f32[7,16,8,256]{3,2,1,0:T(8,128)}, f32[7,16,8,256]{3,2,1,0:T(8,128)S(1)}, u32[]{:S(2)}, u32[]{:S(2)}) %collective-permute-start.4) | collective-permute-done | bytes 917536 | tf_op jit(solution)/shard_map/ppermute | solution.py:671
  2.8 21.2 %conditional.3 = (f32[16,144,128]{2,1,0:T(8,128)}, s32[16,24]{1,0:T(8,128)S(1)}, f32[34,128]{1,0:T(8,128)}, f32[34,128]{1,0:T(8,128)}, f32[5,3,136,128]{3,2,1,0:...) conditional(s32[]{:T(128)} %convert_element_type.2, (s32[1,128]{1,0:T(1,128)}, ...), branch_computations={%region_0.0_spmd, %region_1.0_spmd} | conditional | bytes 8400720 | solution.py:698
  2.8 1.5 %table.1 = s32[16,24]{1,0:T(8,128)} custom-call(s32[1,128]{1,0:T(1,128)} %get-tuple-element.48.owner), custom_call_target="tpu_custom_call" | custom-call | tf_op jit(solution)/shard_map/cond/branch_0_fun/table/pallas_call | solution.py:269
  4.3 8.2 %all-to-all-start.3 = ((s32[16,1,24]{2,1,0:T(1,128)}), s32[16,1,24]{2,1,0:T(1,128)S(1)}, u32[]{:S(2)}, u32[]{:S(2)}) async-start(s32[16,1,24]{2,1,0:T(1,128)} %bitcast.1), calls=%async_computation.3 | async-start | bytes 16384 | tf_op jit(solution)/shard_map/cond/branch_0_fun/all_to_all | solution.py:674
  12.6 7.7 %all-to-all-done.3 = s32[16,1,24]{2,1,0:T(1,128)S(1)} async-done(((s32[16,1,24]{2,1,0:T(1,128)}), s32[16,1,24]{2,1,0:T(1,128)S(1)}, u32[]{:S(2)}, u32[]{:S(2)}) %all-to-all-start.3) | async-done | bytes 1568 | tf_op jit(solution)/shard_map/cond/branch_0_fun/all_to_all | solution.py:674
  20.3 1.2 %slot_cover.1 = f32[16,16,128]{2,1,0:T(8,128)S(1)} custom-call(s32[16,24]{1,0:T(8,128)S(1)} %bitcast.18, f32[128,256]{1,0:T(8,128)S(1)} %slice_bitcast_fusion.conc, s32[1,128]{1,0:T(1,128)} %get-tuple-element.50.covered, s32[128,256]{1,0:T(8,128)} %get-tuple-element.51.land), custom_call_target="tpu_custom_call" | custom-call | tf_op jit(solution)/shard_map/cond/branch_0_fun/slot_cover/pallas_call | solution.py:615
  21.5 1.1 %broadcast.15 = f32[16,144,128]{2,1,0:T(8,128)} broadcast(f32[]{:T(128)} %constant.4.clone), dimensions={} | broadcast | bytes 1179652 | tf_op jit(solution)/shard_map/broadcast.7
  22.6 0.1 broadcast.17
  22.7 0.1 broadcast.18
  22.8 0.6 %broadcast.16 = f32[34,128]{1,0:T(8,128)} broadcast(f32[]{:T(128)} %constant.4.clone), dimensions={} | broadcast | bytes 17412 | tf_op jit(solution)/shard_map/broadcast.6
  23.4 0.6 %broadcast.16.clone = f32[34,128]{1,0:T(8,128)} broadcast(f32[]{:T(128)} %constant.4.clone), dimensions={} | broadcast | bytes 17412 | tf_op jit(solution)/shard_map/broadcast.6
  24.0 4.6 %collective-permute-start.5 = (s32[16,24]{1,0:T(8,128)S(1)}, s32[16,24]{1,0:T(8,128)S(1)}, u32[]{:S(2)}, u32[]{:S(2)}) collective-permute-start(s32[16,24]{1,0:T(8,128)S(1)} %get-tuple-element.88), channel_id=1, source_target_pairs={{0,16},{16,0},{1,17},{17,1},{2,18},{18,2},{3,19},{19,3},{4,20},{20... | collective-permute-start | bytes 4616 | tf_op jit(solution)/shard_map/ppermute | solution.py:701
  28.6 1.3 %fetch.1 = (f32[16,144,128]{2,1,0:T(8,128)S(1)}, f32[34,128]{1,0:T(8,128)S(1)}, f32[34,128]{1,0:T(8,128)S(1)}) custom-call(f32[16,144,128]{2,1,0:T(8,128)} %get-tuple-element.89.refs_0_, f32[34,128]{1,0:T(8,128)} %get-tuple-element.90.refs_1_, f32[34,128]{1,0:T(8,128)} %get-tuple-element.91.refs_2_), custom_call_target="tpu_custom_call" | custom-call | tf_op jit(solution)/shard_map/fetch/pallas_call | solution.py:369
  29.8 0.0 collective-permute-done.5
  29.9 13.0 %conditional.4 = (f32[16,16,128]{2,1,0:T(8,128)S(1)}, f32[16,32,128]{2,1,0:T(8,128)S(1)}, f32[2,16,8,256]{3,2,1,0:T(8,128)S(1)}) conditional(s32[]{:T(128)} %convert_element_type.2, f32[16,16,128]{2,1,0:T(8,128)S(1)} %get-tuple-element.87, (s32[16,24]{1,0:T(8,128)S(1)}, f32[16,144,128]{2,1,0:T(8,128)S(1)}, f32[5,3,136,128]{3,2,1,0:T(8,128)S(1)}, ...), branch_computations={%region_2.0_spmd, %region_3.0_spmd} | conditional | bytes 786464 | solution.py:710
  29.9 13.0 %all_to_all.20 = f32[16,16,128]{2,1,0:T(8,128)S(1)} all-to-all(f32[16,16,128]{2,1,0:T(8,128)S(1)} %param.2), channel_id=1, replica_groups=mesh['comp'=2,'lat'=4,'lon'=4] {'lat','lon'}, dimensions={0} | all-to-all | bytes 262144 | tf_op jit(solution)/shard_map/cond/branch_0_fun/all_to_all | solution.py:674
  42.9 0.0 copy-start
  42.9 3.0 %collective-permute-start.6 = (f32[16,32,128]{2,1,0:T(8,128)S(1)}, f32[16,32,128]{2,1,0:T(8,128)S(1)}, u32[]{:S(2)}, u32[]{:S(2)}) collective-permute-start(f32[16,32,128]{2,1,0:T(8,128)S(1)} %get-tuple-element.120), channel_id=1, source_target_pairs={{0,16},{16,0},{1,17},{17,1},{2,18},{18,2},{3,19},{19,3},{4,20},{20... | collective-permute-start | bytes 786440 | tf_op jit(solution)/shard_map/ppermute | solution.py:714
  46.0 0.0 copy-done
  46.0 0.1 open_stress.1.opened
  46.1 1.1 %collective-permute-done.6.got = f32[16,32,128]{2,1,0:T(8,128)S(1)} collective-permute-done((f32[16,32,128]{2,1,0:T(8,128)S(1)}, f32[16,32,128]{2,1,0:T(8,128)S(1)}, u32[]{:S(2)}, u32[]{:S(2)}) %collective-permute-start.6) | collective-permute-done | bytes 262176 | tf_op jit(solution)/shard_map/ppermute | solution.py:714
  47.1 0.8 %final.1 = f32[2,16,8,256]{3,2,1,0:T(8,128)} custom-call(f32[16,32,128]{2,1,0:T(8,128)S(1)} %collective-permute-done.6.got, f32[16,16,128]{2,1,0:T(8,128)S(1)} %get-tuple-element.98.cover, f32[16,8,8,128]{3,2,1,0:T(8,128)S(1)} %open_stress.1.opened, f32[2,16,8,256]{3,2,1,0:T(8,128)S(1)} %get-tuple-element.99.moved), custom_call_target="tpu_custom_call" | custom-call | tf_op jit(solution)/shard_map/final/pallas_call | solution.py:652
  (4 shorter events, 0.1 us)
Async XLA Ops:
  0.0 2.8 %collective-permute-start.4 = (f32[7,16,8,256]{3,2,1,0:T(8,128)}, f32[7,16,8,256]{3,2,1,0:T(8,128)S(1)}, u32[]{:S(2)}, u32[]{:S(2)}) collective-permute-start(f32[7,16,8,256]{3,2,1,0:T(8,128)} %bitcast.12), channel_id=1, source_target_pairs={{0,16},{16,0},{1,17},{17,1},{2,18},{18,2},{3,19},{19,3},{4,20},{20... | collective-permute-start | bytes 2752520 | tf_op jit(solution)/shard_map/ppermute | solution.py:671
  4.3 16.0 %all-to-all-start.3 = ((s32[16,1,24]{2,1,0:T(1,128)}), s32[16,1,24]{2,1,0:T(1,128)S(1)}, u32[]{:S(2)}, u32[]{:S(2)}) async-start(s32[16,1,24]{2,1,0:T(1,128)} %bitcast.1), calls=%async_computation.3 | async-start | bytes 16384 | tf_op jit(solution)/shard_map/cond/branch_0_fun/all_to_all | solution.py:674
  24.0 5.9 %collective-permute-start.5 = (s32[16,24]{1,0:T(8,128)S(1)}, s32[16,24]{1,0:T(8,128)S(1)}, u32[]{:S(2)}, u32[]{:S(2)}) collective-permute-start(s32[16,24]{1,0:T(8,128)S(1)} %get-tuple-element.88), channel_id=1, source_target_pairs={{0,16},{16,0},{1,17},{17,1},{2,18},{18,2},{3,19},{19,3},{4,20},{20... | collective-permute-start | bytes 4616 | tf_op jit(solution)/shard_map/ppermute | solution.py:701
  42.9 3.1 %copy-start = (f32[1,7,128,256]{3,2,1,0:T(8,128)S(1)}, f32[1,7,128,256]{3,2,1,0:T(8,128)}, u32[]{:S(2)}) copy-start(f32[1,7,128,256]{3,2,1,0:T(8,128)} %param.10) | copy-start | bytes 2752516
  42.9 4.2 %collective-permute-start.6 = (f32[16,32,128]{2,1,0:T(8,128)S(1)}, f32[16,32,128]{2,1,0:T(8,128)S(1)}, u32[]{:S(2)}, u32[]{:S(2)}) collective-permute-start(f32[16,32,128]{2,1,0:T(8,128)S(1)} %get-tuple-element.120), channel_id=1, source_target_pairs={{0,16},{16,0},{1,17},{17,1},{2,18},{18,2},{3,19},{19,3},{4,20},{20... | collective-permute-start | bytes 786440 | tf_op jit(solution)/shard_map/ppermute | solution.py:714

commit v13 on v12

--- a/solution.py
+++ b/solution.py
@@ -35,6 +35,10 @@
     return lax.broadcasted_iota(jnp.int32, (rows, BX), 1)
 
 
+def root(x):
+    return x * lax.rsqrt(x)
+
+
 def roll(x, by):
     return pltpu.roll(x, by % BX, 1)
 
@@ -80,7 +84,7 @@
         planes = [None] * 12
         for y in range(2):
             wx, wy, rho = half(0, y), half(1, y), half(6, y)
-            scale = rho * CD_ICE * jnp.sqrt(wx * wx + wy * wy + 1.0)
+            scale = rho * CD_ICE * root(wx * wx + wy * wy + 1.0)
             planes[y] = scale * wx
             planes[2 + y] = scale * wy
             for ch in range(2, 6):
@@ -216,7 +220,7 @@
             for y in range(2):
                 wx, wy, cx, cy, rho = [raw[ch, t, :, y * BX : (y + 1) * BX] for ch in (0, 1, 2, 3, 6)]
                 rx, ry = wx - cx, wy - cy
-                speed = jnp.sqrt(rx * rx + ry * ry + 1.0)
+                speed = root(rx * rx + ry * ry + 1.0)
                 rate = rho * (0.1 + 0.05 * speed) * speed
                 opened[t, 2 * y] = rate * rx
                 opened[t, 2 * y + 1] = rate * ry
@@ -634,7 +638,7 @@
                 u, v = [got[t, pl.ds(2 * k + y, per, stride=4), :] for k in range(2)]
                 part = cover[t, pl.ds(y, per, stride=2), :]
                 dx, dy = u - opened[t, 4 + 2 * y], v - opened[t, 5 + 2 * y]
-                factor = (CW * part) * jnp.sqrt(dx * dx + dy * dy + DRAG_FLOOR)
+                factor = (CW * part) * root(dx * dx + dy * dy + DRAG_FLOOR)
                 rest = 1.0 - part
                 out[0, t, :, cells] = factor * dx + rest * opened[t, 2 * y]
                 out[1, t, :, cells] = factor * dy + rest * opened[t, 2 * y + 1]

time: 48.2 us -> 48.2 us (level)
  no operation moved by 1% of the time
where the time goes in v13:
time: 48.2 us; the launch traced here: 47.9 us
  starting transfers between devices  16.3 us (34%)
  blocking collectives  13 us (27%)
  waiting for transfers between devices  10.3 us (21%)
  Pallas kernels  5.63 us (12%)
  local copies, waits for them, and re-layouts  2.47 us (5%)
    all_to_all x1, blocking collectives, everyone(): lax.all_to_all(x, ('lat', 'lon'), split_axis=0, concat_axis=0, tiled=True)  13 us
    all_to_all x1, starting transfers between devices, everyone(): lax.all_to_all(x, ('lat', 'lon'), split_axis=0, concat_axis=0, tiled=True)  8.23 us
    all_to_all x1, waiting for transfers between devices, everyone(): lax.all_to_all(x, ('lat', 'lon'), split_axis=0, concat_axis=0, tiled=True)  7.69 us
    ppermute x1, starting transfers between devices, per_device(): swap = lax.ppermute(owned, 'comp', [(0, 1), (1, 0)])  4.59 us
    ppermute x1, starting transfers between devices, per_device(): got = lax.ppermute(back, 'comp', [(0, 1), (1, 0)])  3.03 us
    another operation x6, local copies, waits for them, and re-layouts  2.43 us
    ppermute x1, waiting for transfers between devices, per_device(): other = lax.ppermute(split, 'comp', [(0, 1), (1, 0)])  1.57 us
    pallas_call x1, Pallas kernels, table(): pl.pallas_call(functools.partial(table_kernel, nlat, nlon, per), out_shap...  1.52 us
  transfers between devices with their start and end apart: 4, of which 3 were waited for; matrix products, arithmetic and copies ran while one was open for 0% of the time, Pallas kernels for 4%

profile of v13, /device:TPU:0, one launch (start us, length us, event | category | flops | bytes accessed | tf_op | source)
XLA Modules:
  0.0 47.9 jit_solution(17231434539474935375)
XLA Ops:
  0.0 0.5 %collective-permute-start.4 = (f32[7,16,8,256]{3,2,1,0:T(8,128)}, f32[7,16,8,256]{3,2,1,0:T(8,128)S(1)}, u32[]{:S(2)}, u32[]{:S(2)}) collective-permute-start(f32[7,16,8,256]{3,2,1,0:T(8,128)} %bitcast.12), channel_id=1, source_target_pairs={{0,16},{16,0},{1,17},{17,1},{2,18},{18,2},{3,19},{19,3},{4,20},{20... | collective-permute-start | bytes 2752520 | tf_op jit(solution)/shard_map/ppermute | solution.py:675
  0.5 0.7 %spread.1 = s32[16,8,128]{2,1,0:T(8,128)S(1)} custom-call(s32[1,128]{1,0:T(1,128)} %bitcast.22), custom_call_target="tpu_custom_call" | custom-call | tf_op jit(solution)/shard_map/spread/pallas_call | solution.py:206
  1.2 1.6 %collective-permute-done.4 = f32[7,16,8,256]{3,2,1,0:T(8,128)S(1)} collective-permute-done((f32[7,16,8,256]{3,2,1,0:T(8,128)}, f32[7,16,8,256]{3,2,1,0:T(8,128)S(1)}, u32[]{:S(2)}, u32[]{:S(2)}) %collective-permute-start.4) | collective-permute-done | bytes 917536 | tf_op jit(solution)/shard_map/ppermute | solution.py:675
  2.8 21.2 %conditional.3 = (f32[16,144,128]{2,1,0:T(8,128)}, s32[16,24]{1,0:T(8,128)S(1)}, f32[34,128]{1,0:T(8,128)}, f32[34,128]{1,0:T(8,128)}, f32[5,3,136,128]{3,2,1,0:...) conditional(s32[]{:T(128)} %convert_element_type.2, (s32[1,128]{1,0:T(1,128)}, ...), branch_computations={%region_0.0_spmd, %region_1.0_spmd} | conditional | bytes 8400720 | solution.py:702
  2.8 1.5 %table.1 = s32[16,24]{1,0:T(8,128)} custom-call(s32[1,128]{1,0:T(1,128)} %get-tuple-element.48.owner), custom_call_target="tpu_custom_call" | custom-call | tf_op jit(solution)/shard_map/cond/branch_0_fun/table/pallas_call | solution.py:273
  4.3 8.2 %all-to-all-start.3 = ((s32[16,1,24]{2,1,0:T(1,128)}), s32[16,1,24]{2,1,0:T(1,128)S(1)}, u32[]{:S(2)}, u32[]{:S(2)}) async-start(s32[16,1,24]{2,1,0:T(1,128)} %bitcast.1), calls=%async_computation.3 | async-start | bytes 16384 | tf_op jit(solution)/shard_map/cond/branch_0_fun/all_to_all | solution.py:678
  12.6 7.7 %all-to-all-done.3 = s32[16,1,24]{2,1,0:T(1,128)S(1)} async-done(((s32[16,1,24]{2,1,0:T(1,128)}), s32[16,1,24]{2,1,0:T(1,128)S(1)}, u32[]{:S(2)}, u32[]{:S(2)}) %all-to-all-start.3) | async-done | bytes 1568 | tf_op jit(solution)/shard_map/cond/branch_0_fun/all_to_all | solution.py:678
  20.3 1.2 %slot_cover.1 = f32[16,16,128]{2,1,0:T(8,128)S(1)} custom-call(s32[16,24]{1,0:T(8,128)S(1)} %bitcast.18, f32[128,256]{1,0:T(8,128)S(1)} %slice_bitcast_fusion.conc, s32[1,128]{1,0:T(1,128)} %get-tuple-element.50.covered, s32[128,256]{1,0:T(8,128)} %get-tuple-element.51.land), custom_call_target="tpu_custom_call" | custom-call | tf_op jit(solution)/shard_map/cond/branch_0_fun/slot_cover/pallas_call | solution.py:619
  21.5 1.1 %broadcast.15 = f32[16,144,128]{2,1,0:T(8,128)} broadcast(f32[]{:T(128)} %constant.4.clone), dimensions={} | broadcast | bytes 1179652 | tf_op jit(solution)/shard_map/broadcast.7
  22.6 0.1 broadcast.17
  22.7 0.1 broadcast.18
  22.8 0.6 %broadcast.16 = f32[34,128]{1,0:T(8,128)} broadcast(f32[]{:T(128)} %constant.4.clone), dimensions={} | broadcast | bytes 17412 | tf_op jit(solution)/shard_map/broadcast.6
  23.4 0.6 %broadcast.16.clone = f32[34,128]{1,0:T(8,128)} broadcast(f32[]{:T(128)} %constant.4.clone), dimensions={} | broadcast | bytes 17412 | tf_op jit(solution)/shard_map/broadcast.6
  24.0 4.6 %collective-permute-start.5 = (s32[16,24]{1,0:T(8,128)S(1)}, s32[16,24]{1,0:T(8,128)S(1)}, u32[]{:S(2)}, u32[]{:S(2)}) collective-permute-start(s32[16,24]{1,0:T(8,128)S(1)} %get-tuple-element.88), channel_id=1, source_target_pairs={{0,16},{16,0},{1,17},{17,1},{2,18},{18,2},{3,19},{19,3},{4,20},{20... | collective-permute-start | bytes 4616 | tf_op jit(solution)/shard_map/ppermute | solution.py:705
  28.6 1.3 %fetch.1 = (f32[16,144,128]{2,1,0:T(8,128)S(1)}, f32[34,128]{1,0:T(8,128)S(1)}, f32[34,128]{1,0:T(8,128)S(1)}) custom-call(f32[16,144,128]{2,1,0:T(8,128)} %get-tuple-element.89.refs_0_, f32[34,128]{1,0:T(8,128)} %get-tuple-element.90.refs_1_, f32[34,128]{1,0:T(8,128)} %get-tuple-element.91.refs_2_), custom_call_target="tpu_custom_call" | custom-call | tf_op jit(solution)/shard_map/fetch/pallas_call | solution.py:373
  29.8 0.0 collective-permute-done.5
  29.9 13.0 %conditional.4 = (f32[16,16,128]{2,1,0:T(8,128)S(1)}, f32[16,32,128]{2,1,0:T(8,128)S(1)}, f32[2,16,8,256]{3,2,1,0:T(8,128)S(1)}) conditional(s32[]{:T(128)} %convert_element_type.2, f32[16,16,128]{2,1,0:T(8,128)S(1)} %get-tuple-element.87, (s32[16,24]{1,0:T(8,128)S(1)}, f32[16,144,128]{2,1,0:T(8,128)S(1)}, f32[5,3,136,128]{3,2,1,0:T(8,128)S(1)}, ...), branch_computations={%region_2.0_spmd, %region_3.0_spmd} | conditional | bytes 786464 | solution.py:714
  29.9 13.0 %all_to_all.20 = f32[16,16,128]{2,1,0:T(8,128)S(1)} all-to-all(f32[16,16,128]{2,1,0:T(8,128)S(1)} %param.2), channel_id=1, replica_groups=mesh['comp'=2,'lat'=4,'lon'=4] {'lat','lon'}, dimensions={0} | all-to-all | bytes 262144 | tf_op jit(solution)/shard_map/cond/branch_0_fun/all_to_all | solution.py:678
  42.9 0.0 copy-start
  42.9 3.0 %collective-permute-start.6 = (f32[16,32,128]{2,1,0:T(8,128)S(1)}, f32[16,32,128]{2,1,0:T(8,128)S(1)}, u32[]{:S(2)}, u32[]{:S(2)}) collective-permute-start(f32[16,32,128]{2,1,0:T(8,128)S(1)} %get-tuple-element.120), channel_id=1, source_target_pairs={{0,16},{16,0},{1,17},{17,1},{2,18},{18,2},{3,19},{19,3},{4,20},{20... | collective-permute-start | bytes 786440 | tf_op jit(solution)/shard_map/ppermute | solution.py:718
  46.0 0.0 copy-done
  46.0 0.1 open_stress.1.opened
  46.0 1.1 %collective-permute-done.6.got = f32[16,32,128]{2,1,0:T(8,128)S(1)} collective-permute-done((f32[16,32,128]{2,1,0:T(8,128)S(1)}, f32[16,32,128]{2,1,0:T(8,128)S(1)}, u32[]{:S(2)}, u32[]{:S(2)}) %collective-permute-start.6) | collective-permute-done | bytes 262176 | tf_op jit(solution)/shard_map/ppermute | solution.py:718
  47.1 0.8 %final.1 = f32[2,16,8,256]{3,2,1,0:T(8,128)} custom-call(f32[16,32,128]{2,1,0:T(8,128)S(1)} %collective-permute-done.6.got, f32[16,16,128]{2,1,0:T(8,128)S(1)} %get-tuple-element.98.cover, f32[16,8,8,128]{3,2,1,0:T(8,128)S(1)} %open_stress.1.opened, f32[2,16,8,256]{3,2,1,0:T(8,128)S(1)} %get-tuple-element.99.moved), custom_call_target="tpu_custom_call" | custom-call | tf_op jit(solution)/shard_map/final/pallas_call | solution.py:656
  (4 shorter events, 0.1 us)
Async XLA Ops:
  0.0 2.8 %collective-permute-start.4 = (f32[7,16,8,256]{3,2,1,0:T(8,128)}, f32[7,16,8,256]{3,2,1,0:T(8,128)S(1)}, u32[]{:S(2)}, u32[]{:S(2)}) collective-permute-start(f32[7,16,8,256]{3,2,1,0:T(8,128)} %bitcast.12), channel_id=1, source_target_pairs={{0,16},{16,0},{1,17},{17,1},{2,18},{18,2},{3,19},{19,3},{4,20},{20... | collective-permute-start | bytes 2752520 | tf_op jit(solution)/shard_map/ppermute | solution.py:675
  4.3 16.0 %all-to-all-start.3 = ((s32[16,1,24]{2,1,0:T(1,128)}), s32[16,1,24]{2,1,0:T(1,128)S(1)}, u32[]{:S(2)}, u32[]{:S(2)}) async-start(s32[16,1,24]{2,1,0:T(1,128)} %bitcast.1), calls=%async_computation.3 | async-start | bytes 16384 | tf_op jit(solution)/shard_map/cond/branch_0_fun/all_to_all | solution.py:678
  24.0 5.9 %collective-permute-start.5 = (s32[16,24]{1,0:T(8,128)S(1)}, s32[16,24]{1,0:T(8,128)S(1)}, u32[]{:S(2)}, u32[]{:S(2)}) collective-permute-start(s32[16,24]{1,0:T(8,128)S(1)} %get-tuple-element.88), channel_id=1, source_target_pairs={{0,16},{16,0},{1,17},{17,1},{2,18},{18,2},{3,19},{19,3},{4,20},{20... | collective-permute-start | bytes 4616 | tf_op jit(solution)/shard_map/ppermute | solution.py:705
  42.9 3.1 %copy-start = (f32[1,7,128,256]{3,2,1,0:T(8,128)S(1)}, f32[1,7,128,256]{3,2,1,0:T(8,128)}, u32[]{:S(2)}) copy-start(f32[1,7,128,256]{3,2,1,0:T(8,128)} %param.10) | copy-start | bytes 2752516
  42.9 4.2 %collective-permute-start.6 = (f32[16,32,128]{2,1,0:T(8,128)S(1)}, f32[16,32,128]{2,1,0:T(8,128)S(1)}, u32[]{:S(2)}, u32[]{:S(2)}) collective-permute-start(f32[16,32,128]{2,1,0:T(8,128)S(1)} %get-tuple-element.120), channel_id=1, source_target_pairs={{0,16},{16,0},{1,17},{17,1},{2,18},{18,2},{3,19},{19,3},{4,20},{20... | collective-permute-start | bytes 786440 | tf_op jit(solution)/shard_map/ppermute | solution.py:718
